TPU v7x, 32 devices: a whole 2x2x4 slice. The times are simulated.
32 devices in a mesh: dp: 8 (over z, x), tensor: 4 (over y, core).
Axes of the slice: x: 2, y: 2, z: 4, core: 2. Of those that a mesh axis runs over, the one named last changes fastest.
Arguments:
- patches: bfloat16 [64, 196, 768], P(('dp', 'tensor')), may hold values from -6 to 6
- labels: int32 [64], P(('dp', 'tensor')), may hold values from 0 to 999
- image_count: int32 [8], replicated, may hold values from 1 to 8, as said below
- attn_weight: float32 [3, 768, 4, 768], P(None, 'dp', None, 'tensor'), may hold values from -0.21875 to 0.21875
- attn_rows: float32 [3, 4, 768], P(None, None, 'dp'), may hold values from 7.947286e-08 to 7.947286e-05
- attn_cols: float32 [3, 4, 768], P(None, None, 'tensor'), may hold values from 7.947286e-08 to 7.947286e-05
- mlp_weight: float32 [3, 2, 768, 3072], P(None, None, 'dp', 'tensor'), may hold values from -0.21875 to 0.21875
- mlp_rows: float32 [3, 2, 768], P(None, None, 'dp'), may hold values from 7.947286e-08 to 7.947286e-05
- mlp_cols: float32 [3, 2, 3072], P(None, None, 'tensor'), may hold values from 7.947286e-08 to 7.947286e-05
- patch_weight: float32 [768, 768], P(('dp', 'tensor')), may hold values from -0.21875 to 0.21875
- patch_rows: float32 [768], P(('dp', 'tensor')), may hold values from 2.6490954e-09 to 2.6490952e-06
- patch_cols: float32 [768], replicated, may hold values from 2.6490954e-09 to 2.6490952e-06
- embed_table: float32 [768, 198], P(('dp', 'tensor')), may hold values from -3 to 3
- embed_rows: float32 [768], P(('dp', 'tensor')), may hold values from 2.6490954e-09 to 2.6490952e-06
- embed_cols: float32 [198], replicated, may hold values from 2.6490954e-09 to 2.6490952e-06
- head_weight: float32 [768, 1000], P(('dp', 'tensor')), may hold values from -0.4375 to 0.4375
- head_rows: float32 [768], P(('dp', 'tensor')), may hold values from 1.5625e-06 to 0.0015625
- head_cols: float32 [1000], replicated, may hold values from 1.5625e-06 to 0.0015625
- split_vec: float32 [3, 2, 768], P(None, None, 'tensor'), may hold values from -2 to 2
- split_sq: float32 [3, 2, 768], P(None, None, 'tensor'), may hold values from 6.1035156e-05 to 0.00024414062
- hidden_bias: float32 [3, 3072], P(None, 'tensor'), may hold values from -2 to 2
- hidden_sq: float32 [3, 3072], P(None, 'tensor'), may hold values from 6.1035156e-05 to 0.00024414062
- shared_vec: float32 [20, 768], replicated, may hold values from 0.25 to 1.75
- shared_sq: float32 [20, 768], replicated, may hold values from 6.1035156e-05 to 0.00024414062
- head_bias: float32 [1000], replicated, may hold values from -3 to 3
- head_bias_sq: float32 [1000], replicated, may hold values from 1e-06 to 4e-06
Outputs:
- mean_loss: float32 [], replicated
- attn_new: float32 [3, 768, 4, 768], P(None, 'dp', None, 'tensor')
- attn_rows_new: float32 [3, 4, 768], P(None, None, 'dp')
- attn_cols_new: float32 [3, 4, 768], P(None, None, 'tensor')
- mlp_new: float32 [3, 2, 768, 3072], P(None, None, 'dp', 'tensor')
- mlp_rows_new: float32 [3, 2, 768], P(None, None, 'dp')
- mlp_cols_new: float32 [3, 2, 3072], P(None, None, 'tensor')
- patch_new: float32 [768, 768], P(('dp', 'tensor'))
- patch_rows_new: float32 [768], P(('dp', 'tensor'))
- patch_cols_new: float32 [768], replicated
- embed_new: float32 [768, 198], P(('dp', 'tensor'))
- embed_rows_new: float32 [768], P(('dp', 'tensor'))
- embed_cols_new: float32 [198], replicated
- head_new: float32 [768, 1000], P(('dp', 'tensor'))
- head_rows_new: float32 [768], P(('dp', 'tensor'))
- head_cols_new: float32 [1000], replicated
- split_new: float32 [3, 2, 768], P(None, None, 'tensor')
- split_sq_new: float32 [3, 2, 768], P(None, None, 'tensor')
- hidden_new: float32 [3, 3072], P(None, 'tensor')
- hidden_sq_new: float32 [3, 3072], P(None, 'tensor')
- shared_new: float32 [20, 768], replicated
- shared_sq_new: float32 [20, 768], replicated
- head_bias_new: float32 [1000], replicated
- head_bias_sq_new: float32 [1000], replicated
Inputs may be any that keep to these rules, and one draw needn't show every extreme that they name: Image slot s of dp index i holds a given image when s < image_count[i]; some index holds 8 images and some holds one.
All inputs are finite; a program needn't handle non-finite values.
Results may differ from a plain program's by a relative error of at most 0.014.
Values may be sent and summed in bfloat16 or wider, within the bound.
A program may use at most 256 MiB of HBM per device.

v0:
```python
from functools import partial
import math

import jax
import jax.numpy as jnp
from jax import lax
from jax.sharding import PartitionSpec as P

D = 768
HEAD_DIM = 64
FF = 3072
PATCH = 768
CLASSES = 1000
TOK_IMG = 197
LAYERS = 3
SEQ = 200
EXTRA = 198


decay_rate = 0.5
tiny_sq = 1e-30
floor_scale = 0.001
step_ratio = 1.0
clip_level = 0.1
smoothing = 0.1
norm_eps = 1e-06


def layer_norm(values, gain_vec, shift_vec):
    centred = values - jnp.mean(values, axis=-1, keepdims=True)
    spread = jnp.mean(centred * centred, axis=-1, keepdims=True)
    return centred * lax.rsqrt(spread + norm_eps) * gain_vec + shift_vec


def gather_rows(values):
    return lax.all_gather(values, "tensor", axis=0, tiled=True)


def gather_grads(values):
    return lax.all_gather(values, "tensor", axis=0, tiled=True)


def reduce_rows(left_rows, right_matrix, row_count):

    def row_term(start, count):
        return lax.dot_general(
            left_rows, right_matrix, (((1,), (1,)), ((), ())), preferred_element_type=jnp.float32
        )

    return lax.psum_scatter(
        row_term(jnp.int32(0), row_count * lax.axis_size("tensor")).astype(jnp.bfloat16),
        "tensor",
        scatter_dimension=0,
        tiled=True,
    ).astype(jnp.float32)


def reduce_grads(left_rows, right_matrix, row_count):

    def row_term(start, count):
        return lax.dot_general(
            left_rows, right_matrix, (((1,), (1,)), ((), ())), preferred_element_type=jnp.float32
        )

    return lax.psum_scatter(
        row_term(jnp.int32(0), row_count * lax.axis_size("tensor")).astype(jnp.bfloat16),
        "tensor",
        scatter_dimension=0,
        tiled=True,
    ).astype(jnp.float32)


def outer_sum(left_rows, right_rows):
    return lax.dot_general(
        left_rows, right_rows, (((0,), (0,)), ((), ())), preferred_element_type=jnp.float32
    )


def flatten_all(arrays):
    return jnp.concatenate([jnp.ravel(member) for member in arrays])


def split_all(flat, shapes):
    outputs = []
    offset = 0
    for form_shape in shapes:
        length = math.prod(form_shape)
        outputs.append(flat[offset : offset + length].reshape(form_shape))
        offset = offset + length
    return outputs


def tensor_total(flat):
    return lax.psum(flat, "tensor")


def shard_total(flat):
    return lax.psum(flat, "dp")


def global_total(flat):
    return lax.psum(flat, ("dp", "tensor"))


def summed_over(total_fn, arrays):
    return split_all(total_fn(flatten_all(arrays)), [member.shape for member in arrays])


def finish_step(weight, update, update_sq, weight_sq, entries):
    clip_factor = jnp.maximum(1.0, jnp.sqrt(update_sq / entries) / clip_level)
    step_size = step_ratio * jnp.maximum(floor_scale, jnp.sqrt(weight_sq / entries))
    return weight - step_size * update / clip_factor


def shards(
    patches,
    labels,
    image_count,
    attn_weight,
    attn_rows,
    attn_cols,
    mlp_weight,
    mlp_rows,
    mlp_cols,
    patch_weight,
    patch_rows,
    patch_cols,
    embed_table,
    embed_rows,
    embed_cols,
    head_weight,
    head_rows,
    head_cols,
    split_vec,
    split_sq,
    hidden_bias,
    hidden_sq,
    shared_vec,
    shared_sq,
    head_bias,
    head_bias_sq,
):
    tensor_width = lax.axis_size("tensor")
    tensor_rank = lax.axis_index("tensor")
    shard_rank = lax.axis_index("dp")
    images = patches.shape[0]
    row_count = images * SEQ
    group_images = images * tensor_width
    group_rows = row_count * tensor_width
    head_width = attn_weight.shape[3]
    local_heads = head_width // HEAD_DIM
    score_scale = HEAD_DIM ** (-0.5)
    head_shape = (group_images, SEQ, local_heads, HEAD_DIM)
    key_valid = jnp.arange(SEQ) < TOK_IMG
    slot_index = tensor_rank * images + jnp.arange(images)
    image_total = jnp.sum(image_count).astype(jnp.float32)
    image_weight = (
        jnp.where(slot_index < image_count[shard_rank], 1.0, 0.0).astype(jnp.float32) / image_total
    )
    weight_sq = summed_over(
        global_total,
        [
            jnp.sum(attn_weight * attn_weight, axis=(1, 3)),
            jnp.sum(mlp_weight * mlp_weight, axis=(2, 3)),
            jnp.sum(patch_weight * patch_weight),
            jnp.sum(embed_table * embed_table),
            jnp.sum(head_weight * head_weight),
        ],
    )
    vector_sq = summed_over(
        tensor_total,
        [jnp.sum(split_vec * split_vec, axis=-1), jnp.sum(hidden_bias * hidden_bias, axis=-1)],
    )
    patch_full, table_full, head_full = (
        lax.all_gather(patch_weight.astype(jnp.bfloat16), ("dp", "tensor"), axis=0, tiled=True),
        lax.all_gather(embed_table.astype(jnp.bfloat16), ("dp", "tensor"), axis=0, tiled=True),
        lax.all_gather(head_weight.astype(jnp.bfloat16), ("dp", "tensor"), axis=0, tiled=True),
    )
    table_rows = table_full.astype(jnp.float32).T
    pixel_rows = patches.reshape(images * (TOK_IMG - 1), PATCH)
    embedded = jnp.dot(pixel_rows, patch_full, preferred_element_type=jnp.float32).reshape(
        images, TOK_IMG - 1, D
    )
    embedded = embedded + table_rows[1:TOK_IMG] + table_rows[TOK_IMG]
    residual = jnp.concatenate(
        [
            jnp.broadcast_to(table_rows[0], (images, 1, D)),
            embedded,
            jnp.zeros((images, SEQ - TOK_IMG, D), jnp.float32),
        ],
        axis=1,
    ).reshape(row_count, D)

    def attend(query_heads, key_heads):
        scores = (
            jnp.einsum(
                "bqhd,bkhd->bhqk", query_heads, key_heads, preferred_element_type=jnp.float32
            )
            * score_scale
        )
        return jnp.where(key_valid, scores, -1e30)

    saved = []
    for layer_idx in range(LAYERS):
        attn_layer, mlp_layer = (
            lax.all_gather(attn_weight[layer_idx].astype(jnp.bfloat16), "dp", axis=0, tiled=True),
            lax.all_gather(mlp_weight[layer_idx].astype(jnp.bfloat16), "dp", axis=1, tiled=True),
        )
        gains = shared_vec[6 * layer_idx : 6 * layer_idx + 6]
        attn_input = residual
        normed = gather_rows(layer_norm(residual, gains[0], gains[1]).astype(jnp.bfloat16))
        projected = jnp.dot(
            normed, attn_layer[:, :3].reshape(D, 3 * head_width), preferred_element_type=jnp.float32
        ).reshape(group_rows, 3, head_width)
        query_rows = (projected[:, 0] + split_vec[layer_idx, 0]).astype(jnp.bfloat16)
        key_rows = projected[:, 1].astype(jnp.bfloat16)
        value_rows = (projected[:, 2] + split_vec[layer_idx, 1]).astype(jnp.bfloat16)
        scores = attend(query_rows.reshape(head_shape), key_rows.reshape(head_shape))
        log_total = jax.nn.logsumexp(scores, axis=-1, keepdims=True)
        probs = jnp.exp(scores - log_total)
        mixed = (
            jnp.einsum(
                "bhqk,bkhd->bqhd",
                probs.astype(jnp.bfloat16),
                value_rows.reshape(head_shape),
                preferred_element_type=jnp.float32,
            )
            .astype(jnp.bfloat16)
            .reshape(group_rows, head_width)
        )
        attn_out = reduce_rows(mixed, attn_layer[:, 3], row_count)
        residual = residual + attn_out + gains[2]
        mlp_input = residual
        mlp_normed = gather_rows(layer_norm(residual, gains[3], gains[4]).astype(jnp.bfloat16))
        hidden_pre = (
            jnp.dot(mlp_normed, mlp_layer[0], preferred_element_type=jnp.float32)
            + hidden_bias[layer_idx]
        )
        hidden_act = jax.nn.gelu(hidden_pre, approximate=False).astype(jnp.bfloat16)
        residual = residual + reduce_rows(hidden_act, mlp_layer[1], row_count) + gains[5]
        layer_copy = None
        saved.append(
            (
                layer_copy,
                attn_input,
                normed,
                query_rows,
                key_rows,
                value_rows,
                log_total,
                mixed,
                mlp_input,
                mlp_normed,
                hidden_pre,
                hidden_act,
            )
        )
    cls_rows = residual.reshape(images, SEQ, D)[:, 0]
    feature, final_back = jax.vjp(
        layer_norm, cls_rows, shared_vec[6 * LAYERS], shared_vec[6 * LAYERS + 1]
    )
    feature_low = feature.astype(jnp.bfloat16)
    logits = jnp.dot(feature_low, head_full, preferred_element_type=jnp.float32) + head_bias
    log_norm = jax.nn.logsumexp(logits, axis=-1, keepdims=True)
    onehot = jnp.where(labels[:, None] == jnp.arange(CLASSES)[None, :], 1.0, 0.0).astype(
        jnp.float32
    )
    target = (1.0 - smoothing) * onehot + smoothing / CLASSES
    loss_part = jnp.sum((log_norm[:, 0] - jnp.sum(target * logits, axis=-1)) * image_weight)
    grad_logits = (jnp.exp(logits - log_norm) - target) * image_weight[:, None]
    grad_head_bias = jnp.sum(grad_logits, axis=0)
    logits_low = grad_logits.astype(jnp.bfloat16)
    grad_head = outer_sum(feature_low, logits_low)
    grad_feature = lax.dot_general(
        logits_low, head_full, (((1,), (1,)), ((), ())), preferred_element_type=jnp.float32
    )
    grad_cls, grad_final_gain, grad_final_shift = final_back(grad_feature)
    grad_rows = jnp.concatenate(
        [grad_cls[:, None], jnp.zeros((images, SEQ - 1, D), jnp.float32)], axis=1
    ).reshape(row_count, D)
    shared_list = [None] * LAYERS
    split_list = [None] * LAYERS
    hidden_list = [None] * LAYERS
    attn_list = [None] * LAYERS
    mlp_list = [None] * LAYERS
    for layer_idx in reversed(range(LAYERS)):
        (
            layer_copy,
            attn_input,
            normed,
            query_rows,
            key_rows,
            value_rows,
            log_total,
            mixed,
            mlp_input,
            mlp_normed,
            hidden_pre,
            hidden_act,
        ) = saved[layer_idx]
        attn_layer, mlp_layer = (
            lax.all_gather(attn_weight[layer_idx].astype(jnp.bfloat16), "dp", axis=0, tiled=True),
            lax.all_gather(mlp_weight[layer_idx].astype(jnp.bfloat16), "dp", axis=1, tiled=True),
        )
        gains = shared_vec[6 * layer_idx : 6 * layer_idx + 6]
        grad_down_bias = jnp.sum(grad_rows, axis=0)
        grad_out = gather_grads(grad_rows.astype(jnp.bfloat16))
        grad_act = jnp.dot(grad_out, mlp_layer[1], preferred_element_type=jnp.float32)
        grad_down = outer_sum(grad_out, hidden_act)
        _, gelu_back = jax.vjp(partial(jax.nn.gelu, approximate=False), hidden_pre)
        grad_pre = gelu_back(grad_act)[0]
        grad_hidden_bias = jnp.sum(grad_pre, axis=0)
        pre_low = grad_pre.astype(jnp.bfloat16)
        grad_up = outer_sum(mlp_normed, pre_low)
        grad_mlp_in = reduce_grads(pre_low, mlp_layer[0], row_count)
        _, second_back = jax.vjp(layer_norm, mlp_input, gains[3], gains[4])
        grad_mid, grad_gain_two, grad_shift_two = second_back(grad_mlp_in)
        grad_rows = grad_rows + grad_mid
        grad_out_bias = jnp.sum(grad_rows, axis=0)
        grad_attn_out = gather_grads(grad_rows.astype(jnp.bfloat16))
        grad_mixed = (
            jnp.dot(grad_attn_out, attn_layer[:, 3], preferred_element_type=jnp.float32)
            .astype(jnp.bfloat16)
            .reshape(head_shape)
        )
        grad_out_proj = outer_sum(grad_attn_out, mixed)
        query_heads = query_rows.reshape(head_shape)
        key_heads = key_rows.reshape(head_shape)
        value_heads = value_rows.reshape(head_shape)
        probs = jnp.exp(attend(query_heads, key_heads) - log_total)
        grad_probs = jnp.einsum(
            "bqhd,bkhd->bhqk", grad_mixed, value_heads, preferred_element_type=jnp.float32
        )
        grad_value = jnp.einsum(
            "bhqk,bqhd->bkhd",
            probs.astype(jnp.bfloat16),
            grad_mixed,
            preferred_element_type=jnp.float32,
        )
        inner_sum = jnp.sum(probs * grad_probs, axis=-1, keepdims=True)
        grad_scores = (probs * (grad_probs - inner_sum) * score_scale).astype(jnp.bfloat16)
        grad_query = jnp.einsum(
            "bhqk,bkhd->bqhd", grad_scores, key_heads, preferred_element_type=jnp.float32
        )
        grad_key = jnp.einsum(
            "bhqk,bqhd->bkhd", grad_scores, query_heads, preferred_element_type=jnp.float32
        )
        grad_qkv = jnp.stack(
            [
                grad_query.reshape(group_rows, head_width),
                grad_key.reshape(group_rows, head_width),
                grad_value.reshape(group_rows, head_width),
            ],
            axis=1,
        )
        split_list[layer_idx] = jnp.stack(
            [jnp.sum(grad_qkv[:, 0], axis=0), jnp.sum(grad_qkv[:, 2], axis=0)]
        )
        qkv_low = grad_qkv.astype(jnp.bfloat16).reshape(group_rows, 3 * head_width)
        grad_proj = outer_sum(normed, qkv_low).reshape(D, 3, head_width)
        grad_attn_in = reduce_grads(
            qkv_low, attn_layer[:, :3].reshape(D, 3 * head_width), row_count
        )
        _, first_back = jax.vjp(layer_norm, attn_input, gains[0], gains[1])
        grad_low, grad_gain_one, grad_shift_one = first_back(grad_attn_in)
        grad_rows = grad_rows + grad_low
        attn_full = jnp.concatenate([grad_proj, grad_out_proj[:, None]], axis=1)
        mlp_full = jnp.stack([grad_up, grad_down])
        attn_list[layer_idx], mlp_list[layer_idx] = (
            lax.psum_scatter(attn_full, "dp", scatter_dimension=0, tiled=True),
            lax.psum_scatter(mlp_full, "dp", scatter_dimension=1, tiled=True),
        )
        hidden_list[layer_idx] = grad_hidden_bias
        shared_list[layer_idx] = jnp.stack(
            [
                grad_gain_one,
                grad_shift_one,
                grad_out_bias,
                grad_gain_two,
                grad_shift_two,
                grad_down_bias,
            ]
        )
    grad_image = grad_rows.reshape(images, SEQ, D)
    grad_first = jnp.sum(grad_image[:, 0], axis=0)
    grad_position = jnp.sum(grad_image[:, 1:TOK_IMG], axis=0)
    grad_patch_bias = jnp.sum(grad_position, axis=0)
    embed_low = grad_image[:, 1:TOK_IMG].astype(jnp.bfloat16).reshape(images * (TOK_IMG - 1), D)
    grad_patch = outer_sum(pixel_rows, embed_low)
    grad_table = jnp.concatenate([grad_first[None], grad_position, grad_patch_bias[None]], axis=0).T
    patch_grad, table_grad, head_grad = (
        lax.psum_scatter(grad_patch, ("dp", "tensor"), scatter_dimension=0, tiled=True),
        lax.psum_scatter(grad_table, ("dp", "tensor"), scatter_dimension=0, tiled=True),
        lax.psum_scatter(grad_head, ("dp", "tensor"), scatter_dimension=0, tiled=True),
    )
    attn_grad = jnp.stack(attn_list)
    mlp_grad = jnp.stack(mlp_list)
    split_grad = jnp.stack(split_list)
    hidden_grad = jnp.stack(hidden_list)
    shared_grad = jnp.concatenate(
        shared_list + [jnp.stack([grad_final_gain, grad_final_shift])], axis=0
    )
    attn_sq = attn_grad * attn_grad
    mlp_sq = mlp_grad * mlp_grad
    patch_sq = patch_grad * patch_grad
    table_sq = table_grad * table_grad
    head_sq = head_grad * head_grad
    attn_row_full, mlp_row_full = summed_over(
        tensor_total, [jnp.sum(attn_sq, axis=3).transpose(0, 2, 1), jnp.sum(mlp_sq, axis=3)]
    )
    attn_row_new = decay_rate * attn_rows + (1.0 - decay_rate) * (attn_row_full / D + tiny_sq)
    mlp_row_new = decay_rate * mlp_rows + (1.0 - decay_rate) * (mlp_row_full / FF + tiny_sq)
    patch_row_new = decay_rate * patch_rows + (1.0 - decay_rate) * (
        jnp.sum(patch_sq, axis=1) / D + tiny_sq
    )
    table_row_new = decay_rate * embed_rows + (1.0 - decay_rate) * (
        jnp.sum(table_sq, axis=1) / EXTRA + tiny_sq
    )
    head_row_new = decay_rate * head_rows + (1.0 - decay_rate) * (
        jnp.sum(head_sq, axis=1) / CLASSES + tiny_sq
    )
    attn_col_full, mlp_col_full, split_full, hidden_full = summed_over(
        shard_total, [jnp.sum(attn_sq, axis=1), jnp.sum(mlp_sq, axis=2), split_grad, hidden_grad]
    )
    patch_col_full, table_col_full, head_col_full, shared_full, head_bias_full, loss_total = (
        summed_over(
            global_total,
            [
                jnp.sum(patch_sq, axis=0),
                jnp.sum(table_sq, axis=0),
                jnp.sum(head_sq, axis=0),
                shared_grad,
                grad_head_bias,
                loss_part,
            ],
        )
    )
    attn_row_sum, mlp_row_sum = summed_over(
        shard_total, [jnp.sum(attn_row_new, axis=-1), jnp.sum(mlp_row_new, axis=-1)]
    )
    attn_row_mean = attn_row_sum / D
    mlp_row_mean = mlp_row_sum / D
    (whole_row_sum,) = summed_over(
        global_total,
        [jnp.stack([jnp.sum(patch_row_new), jnp.sum(table_row_new), jnp.sum(head_row_new)])],
    )
    whole_row_mean = whole_row_sum / jnp.array([PATCH, D, D], jnp.float32)
    attn_col_new = decay_rate * attn_cols + (1.0 - decay_rate) * (attn_col_full / D + tiny_sq)
    mlp_col_new = decay_rate * mlp_cols + (1.0 - decay_rate) * (mlp_col_full / D + tiny_sq)
    patch_col_new = decay_rate * patch_cols + (1.0 - decay_rate) * (
        patch_col_full / PATCH + tiny_sq
    )
    table_col_new = decay_rate * embed_cols + (1.0 - decay_rate) * (table_col_full / D + tiny_sq)
    head_col_new = decay_rate * head_cols + (1.0 - decay_rate) * (head_col_full / D + tiny_sq)
    attn_update = attn_grad * lax.rsqrt(
        attn_row_new.transpose(0, 2, 1)[:, :, :, None]
        * attn_col_new[:, None]
        / attn_row_mean[:, None, :, None]
    )
    mlp_update = mlp_grad * lax.rsqrt(
        mlp_row_new[:, :, :, None] * mlp_col_new[:, :, None, :] / mlp_row_mean[:, :, None, None]
    )
    patch_update = patch_grad * lax.rsqrt(
        patch_row_new[:, None] * patch_col_new[None, :] / whole_row_mean[0]
    )
    table_update = table_grad * lax.rsqrt(
        table_row_new[:, None] * table_col_new[None, :] / whole_row_mean[1]
    )
    head_update = head_grad * lax.rsqrt(
        head_row_new[:, None] * head_col_new[None, :] / whole_row_mean[2]
    )
    split_sq_new = decay_rate * split_sq + (1.0 - decay_rate) * (split_full * split_full + tiny_sq)
    split_update = split_full * lax.rsqrt(split_sq_new)
    hidden_sq_new = decay_rate * hidden_sq + (1.0 - decay_rate) * (
        hidden_full * hidden_full + tiny_sq
    )
    hidden_update = hidden_full * lax.rsqrt(hidden_sq_new)
    shared_sq_new = decay_rate * shared_sq + (1.0 - decay_rate) * (
        shared_full * shared_full + tiny_sq
    )
    shared_update = shared_full * lax.rsqrt(shared_sq_new)
    head_bias_sq_new = decay_rate * head_bias_sq + (1.0 - decay_rate) * (
        head_bias_full * head_bias_full + tiny_sq
    )
    head_bias_update = head_bias_full * lax.rsqrt(head_bias_sq_new)
    attn_u2, mlp_u2, patch_u2, table_u2, head_u2 = summed_over(
        global_total,
        [
            jnp.sum(attn_update * attn_update, axis=(1, 3)),
            jnp.sum(mlp_update * mlp_update, axis=(2, 3)),
            jnp.sum(patch_update * patch_update),
            jnp.sum(table_update * table_update),
            jnp.sum(head_update * head_update),
        ],
    )
    split_u2, hidden_u2 = summed_over(
        tensor_total,
        [
            jnp.sum(split_update * split_update, axis=-1),
            jnp.sum(hidden_update * hidden_update, axis=-1),
        ],
    )
    attn_new = finish_step(
        attn_weight, attn_update, attn_u2[:, None, :, None], weight_sq[0][:, None, :, None], D * D
    )
    mlp_new = finish_step(
        mlp_weight, mlp_update, mlp_u2[:, :, None, None], weight_sq[1][:, :, None, None], D * FF
    )
    patch_new = finish_step(patch_weight, patch_update, patch_u2, weight_sq[2], PATCH * D)
    embed_new = finish_step(embed_table, table_update, table_u2, weight_sq[3], D * EXTRA)
    head_new = finish_step(head_weight, head_update, head_u2, weight_sq[4], D * CLASSES)
    split_new = finish_step(
        split_vec, split_update, split_u2[:, :, None], vector_sq[0][:, :, None], D
    )
    hidden_new = finish_step(
        hidden_bias, hidden_update, hidden_u2[:, None], vector_sq[1][:, None], FF
    )
    shared_new = finish_step(
        shared_vec,
        shared_update,
        jnp.sum(shared_update * shared_update, axis=-1, keepdims=True),
        jnp.sum(shared_vec * shared_vec, axis=-1, keepdims=True),
        D,
    )
    head_bias_new = finish_step(
        head_bias,
        head_bias_update,
        jnp.sum(head_bias_update * head_bias_update),
        jnp.sum(head_bias * head_bias),
        CLASSES,
    )
    return (
        loss_total,
        attn_new,
        attn_row_new,
        attn_col_new,
        mlp_new,
        mlp_row_new,
        mlp_col_new,
        patch_new,
        patch_row_new,
        patch_col_new,
        embed_new,
        table_row_new,
        table_col_new,
        head_new,
        head_row_new,
        head_col_new,
        split_new,
        split_sq_new,
        hidden_new,
        hidden_sq_new,
        shared_new,
        shared_sq_new,
        head_bias_new,
        head_bias_sq_new,
    )


def solution(mesh):
    in_specs = (
        P(("dp", "tensor"), None, None),
        P(("dp", "tensor")),
        P(),
        P(None, "dp", None, "tensor"),
        P(None, None, "dp"),
        P(None, None, "tensor"),
        P(None, None, "dp", "tensor"),
        P(None, None, "dp"),
        P(None, None, "tensor"),
        P(("dp", "tensor"), None),
        P(("dp", "tensor")),
        P(),
        P(("dp", "tensor"), None),
        P(("dp", "tensor")),
        P(),
        P(("dp", "tensor"), None),
        P(("dp", "tensor")),
        P(),
        P(None, None, "tensor"),
        P(None, None, "tensor"),
        P(None, "tensor"),
        P(None, "tensor"),
        P(),
        P(),
        P(),
        P(),
    )
    out_specs = (
        P(),
        P(None, "dp", None, "tensor"),
        P(None, None, "dp"),
        P(None, None, "tensor"),
        P(None, None, "dp", "tensor"),
        P(None, None, "dp"),
        P(None, None, "tensor"),
        P(("dp", "tensor"), None),
        P(("dp", "tensor")),
        P(),
        P(("dp", "tensor"), None),
        P(("dp", "tensor")),
        P(),
        P(("dp", "tensor"), None),
        P(("dp", "tensor")),
        P(),
        P(None, None, "tensor"),
        P(None, None, "tensor"),
        P(None, "tensor"),
        P(None, "tensor"),
        P(),
        P(),
        P(),
        P(),
    )
    return jax.shard_map(shards, mesh=mesh, in_specs=in_specs, out_specs=out_specs, check_vma=False)
```

profile of v0, /device:TPU:0, one launch (start us, length us, event | category | flops | bytes accessed | tf_op | source)
XLA Modules:
  0.0 2499.2 jit_solution(16805962588689009073)
XLA Ops:
  13.2 44.5 %all_gather.69 = bf16[768,198]{1,0:T(8,128)(2,1)S(1)} all-gather(bf16[24,198]{1,0:T(8,128)(2,1)S(1)} %get-tuple-element.269), channel_id=1, replica_groups=mesh['dp'=8,'tensor'=4] {'dp','tensor'}, dimensions={0}, use_global_device_ids=true | all-gather | bytes 313632 | tf_op jit(solution)/shard_map/all_gather | solution.py:176
  72.8 41.6 %all-gather.55.cloned.1.call-done = bf16[1,768,4,192]{3,2,0,1:T(4,128)(2,1)} async-done(((bf16[1,96,4,192]{3,2,0,1:T(4,128)(2,1)}), bf16[1,768,4,192]{3,2,0,1:T(4,128)(2,1)}) %all-gather.55.cloned.1.call-update) | async-done | bytes 1179664 | tf_op jit(solution)/shard_map/all_gather | solution.py:206
  117.1 22.4 all-gather.29.cloned.1.call-done
  169.3 29.4 %reduce-scatter.32.cloned.1.call-done = bf16[400,768]{1,0:T(8,128)(2,1)} async-done(((bf16[1600,768]{1,0:T(8,128)(2,1)}), bf16[400,768]{1,0:T(8,128)(2,1)}) %reduce-scatter.32.cloned.1.call-update) | async-done | bytes 614416 | tf_op jit(solution)/shard_map/reduce_scatter | solution.py:50
  201.7 50.8 %all-gather.57.cloned.1.call-done = bf16[1,2,768,768]{3,2,1,0:T(8,128)(2,1)} async-done(((bf16[1,2,96,768]{3,2,1,0:T(8,128)(2,1)}), bf16[1,2,768,768]{3,2,1,0:T(8,128)(2,1)}) %all-gather.57.cloned.1.call-update) | async-done | bytes 2359312 | tf_op jit(solution)/shard_map/all_gather | solution.py:207
  252.5 24.6 all-gather.31.cloned.1.call-done
  277.1 15.7 multiply_convert_fusion.5
  298.6 32.8 %reduce-scatter.34.cloned.1.call-done = bf16[400,768]{1,0:T(8,128)(2,1)} async-done(((bf16[1600,768]{1,0:T(8,128)(2,1)}), bf16[400,768]{1,0:T(8,128)(2,1)}) %reduce-scatter.34.cloned.1.call-update) | async-done | bytes 614416 | tf_op jit(solution)/shard_map/reduce_scatter | solution.py:50
  334.9 42.9 %all-gather.59.cloned.1.call-done = bf16[1,768,4,192]{3,2,0,1:T(4,128)(2,1)} async-done(((bf16[1,96,4,192]{3,2,0,1:T(4,128)(2,1)}), bf16[1,768,4,192]{3,2,0,1:T(4,128)(2,1)}) %all-gather.59.cloned.1.call-update) | async-done | bytes 1179664 | tf_op jit(solution)/shard_map/all_gather | solution.py:206
  380.5 21.9 all-gather.33.cloned.1.call-done
  428.7 32.8 %reduce-scatter.36.cloned.1.call-done = bf16[400,768]{1,0:T(8,128)(2,1)} async-done(((bf16[1600,768]{1,0:T(8,128)(2,1)}), bf16[400,768]{1,0:T(8,128)(2,1)}) %reduce-scatter.36.cloned.1.call-update) | async-done | bytes 614416 | tf_op jit(solution)/shard_map/reduce_scatter | solution.py:50
  464.6 51.0 %all-gather.61.cloned.1.call-done = bf16[1,2,768,768]{3,2,1,0:T(8,128)(2,1)} async-done(((bf16[1,2,96,768]{3,2,1,0:T(8,128)(2,1)}), bf16[1,2,768,768]{3,2,1,0:T(8,128)(2,1)}) %all-gather.61.cloned.1.call-update) | async-done | bytes 2359312 | tf_op jit(solution)/shard_map/all_gather | solution.py:207
  515.6 24.6 all-gather.35.cloned.1.call-done
  540.2 15.7 multiply_convert_fusion.4
  561.5 33.0 %reduce-scatter.38.cloned.1.call-done = bf16[400,768]{1,0:T(8,128)(2,1)} async-done(((bf16[1600,768]{1,0:T(8,128)(2,1)}), bf16[400,768]{1,0:T(8,128)(2,1)}) %reduce-scatter.38.cloned.1.call-update) | async-done | bytes 614416 | tf_op jit(solution)/shard_map/reduce_scatter | solution.py:50
  597.7 43.1 %all-gather.63.cloned.1.call-done = bf16[1,768,4,192]{3,2,0,1:T(4,128)(2,1)} async-done(((bf16[1,96,4,192]{3,2,0,1:T(4,128)(2,1)}), bf16[1,768,4,192]{3,2,0,1:T(4,128)(2,1)}) %all-gather.63.cloned.1.call-update) | async-done | bytes 1179664 | tf_op jit(solution)/shard_map/all_gather | solution.py:206
  644.4 20.8 all-gather.37.cloned.1.call-done
  694.4 33.0 %reduce-scatter.40.cloned.1.call-done = bf16[400,768]{1,0:T(8,128)(2,1)} async-done(((bf16[1600,768]{1,0:T(8,128)(2,1)}), bf16[400,768]{1,0:T(8,128)(2,1)}) %reduce-scatter.40.cloned.1.call-update) | async-done | bytes 614416 | tf_op jit(solution)/shard_map/reduce_scatter | solution.py:50
  731.1 50.0 %all-gather.65.cloned.1.call-done = bf16[1,2,768,768]{3,2,1,0:T(8,128)(2,1)} async-done(((bf16[1,2,96,768]{3,2,1,0:T(8,128)(2,1)}), bf16[1,2,768,768]{3,2,1,0:T(8,128)(2,1)}) %all-gather.65.cloned.1.call-update) | async-done | bytes 2359312 | tf_op jit(solution)/shard_map/all_gather | solution.py:207
  781.2 24.6 all-gather.39.cloned.1.call-done
  805.8 15.7 multiply_convert_fusion.3
  830.6 29.6 %reduce-scatter.42.cloned.1.call-done = bf16[400,768]{1,0:T(8,128)(2,1)} async-done(((bf16[1600,768]{1,0:T(8,128)(2,1)}), bf16[400,768]{1,0:T(8,128)(2,1)}) %reduce-scatter.42.cloned.1.call-update) | async-done | bytes 614416 | tf_op jit(solution)/shard_map/reduce_scatter | solution.py:50
  862.7 55.7 %all-gather.41.cloned.1.call-done = bf16[768,1000]{1,0:T(8,128)(2,1)} async-done(((bf16[24,1000]{1,0:T(8,128)(2,1)}), bf16[768,1000]{1,0:T(8,128)(2,1)}) %all-gather.41.cloned.1.call-update) | async-done | bytes 1536016 | tf_op jit(solution)/shard_map/all_gather | solution.py:177
  926.1 23.2 all-gather.43.cloned.1.call-done
  963.6 33.5 %reduce-scatter.44.cloned.1.call-done = bf16[400,768]{1,0:T(8,128)(2,1)} async-done(((bf16[1600,768]{1,0:T(8,128)(2,1)}), bf16[400,768]{1,0:T(8,128)(2,1)}) %reduce-scatter.44.cloned.1.call-update) | async-done | bytes 614416 | tf_op jit(solution)/shard_map/reduce_scatter | solution.py:65
  1005.2 24.7 all-gather.45.cloned.1.call-done
  1045.0 11.2 fusion.93
  1082.3 33.6 %reduce-scatter.46.cloned.1.call-done = bf16[400,768]{1,0:T(8,128)(2,1)} async-done(((bf16[1600,768]{1,0:T(8,128)(2,1)}), bf16[400,768]{1,0:T(8,128)(2,1)}) %reduce-scatter.46.cloned.1.call-update) | async-done | bytes 614416 | tf_op jit(solution)/shard_map/reduce_scatter | solution.py:65
  1121.9 24.7 all-gather.47.cloned.1.call-done
  1160.3 33.5 %reduce-scatter.48.cloned.1.call-done = bf16[400,768]{1,0:T(8,128)(2,1)} async-done(((bf16[1600,768]{1,0:T(8,128)(2,1)}), bf16[400,768]{1,0:T(8,128)(2,1)}) %reduce-scatter.48.cloned.1.call-update) | async-done | bytes 614416 | tf_op jit(solution)/shard_map/reduce_scatter | solution.py:65
  1200.4 24.3 all-gather.49.cloned.1.call-done
  1236.1 11.2 fusion.87
  1270.4 33.6 %reduce-scatter.50.cloned.1.call-done = bf16[400,768]{1,0:T(8,128)(2,1)} async-done(((bf16[1600,768]{1,0:T(8,128)(2,1)}), bf16[400,768]{1,0:T(8,128)(2,1)}) %reduce-scatter.50.cloned.1.call-update) | async-done | bytes 614416 | tf_op jit(solution)/shard_map/reduce_scatter | solution.py:65
  1309.9 24.7 all-gather.51.cloned.1.call-done
  1347.7 33.4 %reduce-scatter.52.cloned.1.call-done = bf16[400,768]{1,0:T(8,128)(2,1)} async-done(((bf16[1600,768]{1,0:T(8,128)(2,1)}), bf16[400,768]{1,0:T(8,128)(2,1)}) %reduce-scatter.52.cloned.1.call-update) | async-done | bytes 614416 | tf_op jit(solution)/shard_map/reduce_scatter | solution.py:65
  1454.8 11.2 fusion.81
  1523.1 68.5 %reduce-scatter.72.cloned.1.call-done = f32[96,768]{1,0:T(8,128)} async-done(((f32[768,768]{1,0:T(8,128)}), f32[96,768]{1,0:T(8,128)}) %reduce-scatter.72.cloned.1.call-update) | async-done | bytes 294928
  1596.4 67.5 %reduce-scatter.70.cloned.1.call-done = f32[96,768]{1,0:T(8,128)} async-done(((f32[768,768]{1,0:T(8,128)}), f32[96,768]{1,0:T(8,128)}) %reduce-scatter.70.cloned.1.call-update) | async-done | bytes 294928
  1667.7 94.8 %reduce-scatter.62.cloned.1.call-done = f32[2,96,768]{2,1,0:T(8,128)} async-done(((f32[2,768,768]{2,1,0:T(8,128)}), f32[2,96,768]{2,1,0:T(8,128)}) %reduce-scatter.62.cloned.1.call-update) | async-done | bytes 589840 | tf_op jit(solution)/shard_map/reduce_scatter | solution.py:371
  1762.5 98.8 %reduce-scatter.60.cloned.1.call-done = f32[2,96,768]{2,1,0:T(8,128)} async-done(((f32[2,768,768]{2,1,0:T(8,128)}), f32[2,96,768]{2,1,0:T(8,128)}) %reduce-scatter.60.cloned.1.call-update) | async-done | bytes 589840 | tf_op jit(solution)/shard_map/reduce_scatter | solution.py:371
  1861.3 98.8 %reduce-scatter.58.cloned.1.call-done = f32[2,96,768]{2,1,0:T(8,128)} async-done(((f32[2,768,768]{2,1,0:T(8,128)}), f32[2,96,768]{2,1,0:T(8,128)}) %reduce-scatter.58.cloned.1.call-update) | async-done | bytes 589840 | tf_op jit(solution)/shard_map/reduce_scatter | solution.py:371
  1962.0 71.0 %reduce-scatter.68.cloned.1.call-done = f32[96,768]{1,0:T(8,128)} async-done(((f32[768,768]{1,0:T(8,128)}), f32[96,768]{1,0:T(8,128)}) %reduce-scatter.68.cloned.1.call-update) | async-done | bytes 294928
  2043.5 35.7 %all-reduce.2 = (f32[18]{0:T(128)S(1)}, f32[10368]{0:T(1024)S(1)}) all-reduce(f32[18]{0:T(128)S(1)} %pad_maximum_fusion.12, f32[10368]{0:T(1024)S(1)} %pad_maximum_fusion.8), channel_id=1, replica_groups=mesh['dp'=8,'tensor'=4] {'dp'}, use_global_device_ids=true, to_apply=%region_114.115 | all-reduce | flops 10386 | bytes 83088 | tf_op jit(solution)/shard_map/psum | solution.py:98
  2103.0 77.8 %reduce-scatter.66.cloned.1.call-done = f32[24,198]{1,0:T(8,128)} async-done(((f32[768,198]{1,0:T(8,128)}), f32[24,198]{1,0:T(8,128)}) %reduce-scatter.66.cloned.1.call-update) | async-done | bytes 19024
  2182.4 102.4 %reduce-scatter.64.cloned.1.call-done = f32[24,768]{1,0:T(8,128)} async-done(((f32[768,768]{1,0:T(8,128)}), f32[24,768]{1,0:T(8,128)}) %reduce-scatter.64.cloned.1.call-update) | async-done | bytes 73744
  2290.1 40.0 %psum.68 = f32[3]{0:T(128)S(1)} all-reduce(f32[3]{0:T(128)S(1)} %pad_maximum_fusion.13), channel_id=1, replica_groups=mesh['dp'=8,'tensor'=4] {'dp','tensor'}, use_global_device_ids=true, to_apply=%region_123.124 | all-reduce | flops 3 | bytes 24 | tf_op jit(solution)/shard_map/psum | solution.py:102
  2330.7 79.6 %all-reduce.6.cloned.1.call-done = f32[18327]{0:T(1024)} async-done(((f32[18327]{0:T(1024)}), f32[18327]{0:T(1024)}) %all-reduce.6.cloned.1.call-update) | async-done | bytes 73324 | tf_op jit(solution)/shard_map/psum | solution.py:102
  2422.0 42.2 %all-reduce.1 = (f32[21]{0:T(128)S(1)}, f32[21]{0:T(128)S(1)}) all-reduce(f32[21]{0:T(128)S(1)} %concatenate.57, f32[21]{0:T(128)S(1)} %copy-done.206), channel_id=1, replica_groups=mesh['dp'=8,'tensor'=4] {'dp','tensor'}, use_global_device_ids=true, to_apply=%region_127.128 | all-reduce | flops 42 | bytes 336 | tf_op jit(solution)/shard_map/psum | solution.py:102
  (906 shorter events, 519.6 us)
Async XLA Ops:
  7.2 61.3 %all-gather.27.cloned.1.call-start = ((), (), s32[]{:S(2)}) async-start(), calls=%async_computation.21 | async-start | bytes 1216512 | tf_op jit(solution)/shard_map/all_gather | solution.py:175
  9.4 104.9 %all-gather.55.cloned.1.call-start = ((), (), s32[]{:S(2)}) async-start(), calls=%async_computation.52 | async-start | bytes 1769472 | tf_op jit(solution)/shard_map/all_gather | solution.py:206
  11.7 127.8 %all-gather.29.cloned.1.call-start = ((), (), s32[]{:S(2)}) async-start(), calls=%async_computation.22 | async-start | bytes 3072000 | tf_op jit(solution)/shard_map/all_gather | solution.py:36
  72.3 126.3 %reduce-scatter.32.cloned.1.call-start = ((), (), s32[]{:S(2)}) async-start(), calls=%async_computation.23 | async-start | bytes 3072000 | tf_op jit(solution)/shard_map/reduce_scatter | solution.py:50
  165.0 87.5 %all-gather.57.cloned.1.call-start = ((), (), s32[]{:S(2)}) async-start(), calls=%async_computation.53 | async-start | bytes 2654208 | tf_op jit(solution)/shard_map/all_gather | solution.py:207
  169.0 108.1 %all-gather.31.cloned.1.call-start = ((), (), s32[]{:S(2)}) async-start(), calls=%async_computation.24 | async-start | bytes 3072000 | tf_op jit(solution)/shard_map/all_gather | solution.py:36
  201.6 129.8 %reduce-scatter.34.cloned.1.call-start = ((), (), s32[]{:S(2)}) async-start(), calls=%async_computation.25 | async-start | bytes 3072000 | tf_op jit(solution)/shard_map/reduce_scatter | solution.py:50
  297.8 80.0 %all-gather.59.cloned.1.call-start = ((), (), s32[]{:S(2)}) async-start(), calls=%async_computation.54 | async-start | bytes 1769472 | tf_op jit(solution)/shard_map/all_gather | solution.py:206
  298.6 103.8 %all-gather.33.cloned.1.call-start = ((), (), s32[]{:S(2)}) async-start(), calls=%async_computation.26 | async-start | bytes 3072000 | tf_op jit(solution)/shard_map/all_gather | solution.py:36
  334.2 127.3 %reduce-scatter.36.cloned.1.call-start = ((), (), s32[]{:S(2)}) async-start(), calls=%async_computation.27 | async-start | bytes 3072000 | tf_op jit(solution)/shard_map/reduce_scatter | solution.py:50
  428.0 87.6 %all-gather.61.cloned.1.call-start = ((), (), s32[]{:S(2)}) async-start(), calls=%async_computation.55 | async-start | bytes 2654208 | tf_op jit(solution)/shard_map/all_gather | solution.py:207
  428.7 111.5 %all-gather.35.cloned.1.call-start = ((), (), s32[]{:S(2)}) async-start(), calls=%async_computation.28 | async-start | bytes 3072000 | tf_op jit(solution)/shard_map/all_gather | solution.py:36
  464.3 130.2 %reduce-scatter.38.cloned.1.call-start = ((), (), s32[]{:S(2)}) async-start(), calls=%async_computation.29 | async-start | bytes 3072000 | tf_op jit(solution)/shard_map/reduce_scatter | solution.py:50
  560.9 79.9 %all-gather.63.cloned.1.call-start = ((), (), s32[]{:S(2)}) async-start(), calls=%async_computation.56 | async-start | bytes 1769472 | tf_op jit(solution)/shard_map/all_gather | solution.py:206
  561.5 103.7 %all-gather.37.cloned.1.call-start = ((), (), s32[]{:S(2)}) async-start(), calls=%async_computation.30 | async-start | bytes 3072000 | tf_op jit(solution)/shard_map/all_gather | solution.py:36
  597.3 130.0 %reduce-scatter.40.cloned.1.call-start = ((), (), s32[]{:S(2)}) async-start(), calls=%async_computation.31 | async-start | bytes 3072000 | tf_op jit(solution)/shard_map/reduce_scatter | solution.py:50
  693.7 87.5 %all-gather.65.cloned.1.call-start = ((), (), s32[]{:S(2)}) async-start(), calls=%async_computation.57 | async-start | bytes 2654208 | tf_op jit(solution)/shard_map/all_gather | solution.py:207
  694.3 111.5 %all-gather.39.cloned.1.call-start = ((), (), s32[]{:S(2)}) async-start(), calls=%async_computation.32 | async-start | bytes 3072000 | tf_op jit(solution)/shard_map/all_gather | solution.py:36
  730.8 129.4 %reduce-scatter.42.cloned.1.call-start = ((), (), s32[]{:S(2)}) async-start(), calls=%async_computation.33 | async-start | bytes 3072000 | tf_op jit(solution)/shard_map/reduce_scatter | solution.py:50
  826.6 91.9 %all-gather.41.cloned.1.call-start = ((), (), s32[]{:S(2)}) async-start(), calls=%async_computation.34 | async-start | bytes 1622016 | tf_op jit(solution)/shard_map/all_gather | solution.py:177
  828.7 120.6 %all-gather.43.cloned.1.call-start = ((), (), s32[]{:S(2)}) async-start(), calls=%async_computation.35 | async-start | bytes 3072000 | tf_op jit(solution)/shard_map/all_gather | solution.py:40
  925.6 71.5 %reduce-scatter.44.cloned.1.call-start = ((), (), s32[]{:S(2)}) async-start(), calls=%async_computation.36 | async-start | bytes 3072000 | tf_op jit(solution)/shard_map/reduce_scatter | solution.py:65
  963.5 66.5 %all-gather.45.cloned.1.call-start = ((), (), s32[]{:S(2)}) async-start(), calls=%async_computation.37 | async-start | bytes 3072000 | tf_op jit(solution)/shard_map/all_gather | solution.py:40
  1005.2 110.7 %reduce-scatter.46.cloned.1.call-start = ((), (), s32[]{:S(2)}) async-start(), calls=%async_computation.38 | async-start | bytes 3072000 | tf_op jit(solution)/shard_map/reduce_scatter | solution.py:65
  1082.3 64.3 %all-gather.47.cloned.1.call-start = ((), (), s32[]{:S(2)}) async-start(), calls=%async_computation.39 | async-start | bytes 3072000 | tf_op jit(solution)/shard_map/all_gather | solution.py:40
  1121.8 72.0 %reduce-scatter.48.cloned.1.call-start = ((), (), s32[]{:S(2)}) async-start(), calls=%async_computation.40 | async-start | bytes 3072000 | tf_op jit(solution)/shard_map/reduce_scatter | solution.py:65
  1160.2 64.5 %all-gather.49.cloned.1.call-start = ((), (), s32[]{:S(2)}) async-start(), calls=%async_computation.41 | async-start | bytes 3072000 | tf_op jit(solution)/shard_map/all_gather | solution.py:40
  1199.9 104.0 %reduce-scatter.50.cloned.1.call-start = ((), (), s32[]{:S(2)}) async-start(), calls=%async_computation.42 | async-start | bytes 3072000 | tf_op jit(solution)/shard_map/reduce_scatter | solution.py:65
  1270.4 64.2 %all-gather.51.cloned.1.call-start = ((), (), s32[]{:S(2)}) async-start(), calls=%async_computation.43 | async-start | bytes 3072000 | tf_op jit(solution)/shard_map/all_gather | solution.py:40
  1309.9 71.2 %reduce-scatter.52.cloned.1.call-start = ((), (), s32[]{:S(2)}) async-start(), calls=%async_computation.44 | async-start | bytes 3072000 | tf_op jit(solution)/shard_map/reduce_scatter | solution.py:65
  1347.4 92.4 %all-gather.53.cloned.1.call-start = ((), (), s32[]{:S(2)}) async-start(), calls=%async_computation.45 | async-start | bytes 3072000 | tf_op jit(solution)/shard_map/all_gather | solution.py:40
  1387.3 132.4 %reduce-scatter.56.cloned.1.call-start = ((), (), s32[]{:S(2)}) async-start(), calls=%async_computation.47 | async-start | bytes 3244032 | tf_op jit(solution)/shard_map/reduce_scatter | solution.py:394
  1389.7 201.8 %reduce-scatter.72.cloned.1.call-start = ((), (), s32[]{:S(2)}) async-start(), calls=%async_computation.62 | async-start | bytes 2654208
  1399.4 264.5 %reduce-scatter.70.cloned.1.call-start = ((), (), s32[]{:S(2)}) async-start(), calls=%async_computation.61 | async-start | bytes 2654208
  1409.1 353.4 %reduce-scatter.62.cloned.1.call-start = ((), (), s32[]{:S(2)}) async-start(), calls=%async_computation.51 | async-start | bytes 5308416 | tf_op jit(solution)/shard_map/reduce_scatter | solution.py:371
  1419.6 441.8 %reduce-scatter.60.cloned.1.call-start = ((), (), s32[]{:S(2)}) async-start(), calls=%async_computation.50 | async-start | bytes 5308416 | tf_op jit(solution)/shard_map/reduce_scatter | solution.py:371
  1429.5 530.7 %reduce-scatter.58.cloned.1.call-start = ((), (), s32[]{:S(2)}) async-start(), calls=%async_computation.49 | async-start | bytes 5308416 | tf_op jit(solution)/shard_map/reduce_scatter | solution.py:371
  1439.5 593.4 %reduce-scatter.68.cloned.1.call-start = ((), (), s32[]{:S(2)}) async-start(), calls=%async_computation.60 | async-start | bytes 2654208
  1493.4 585.9 %reduce-scatter.54.cloned.1.call-start = ((), (), s32[]{:S(2)}) async-start(), calls=%async_computation.46 | async-start | bytes 3072000 | tf_op jit(solution)/shard_map/reduce_scatter | solution.py:65
  1498.5 682.3 %reduce-scatter.66.cloned.1.call-start = ((), (), s32[]{:S(2)}) async-start(), calls=%async_computation.59 | async-start | bytes 811008
  1592.7 449.6 %copy-start.198 = (f32[3,2,96]{2,1,0:T(2,128)S(1)}, f32[3,2,96]{2,1,0:T(2,128)}, u32[]{:S(2)}) copy-start(f32[3,2,96]{2,1,0:T(2,128)} %param.34) | copy-start | bytes 6916
  1592.7 449.8 %copy-start.184 = (f32[3,4,96]{2,1,0:T(4,128)S(1)}, f32[3,4,96]{2,1,0:T(4,128)}, u32[]{:S(2)}) copy-start(f32[3,4,96]{2,1,0:T(4,128)} %param.31) | copy-start | bytes 13828
  1595.1 484.2 %copy-start.3 = (f32[2,200,768]{2,1,0:T(8,128)S(1)}, f32[2,200,768]{2,1,0:T(8,128)}, u32[]{:S(2)}) copy-start(f32[2,200,768]{2,1,0:T(8,128)} %copy-done.2) | copy-start | bytes 3686404
  1595.1 484.2 %copy-start.105 = (f32[768]{0:T(1024)S(1)}, f32[768]{0:T(1024)}, u32[]{:S(2)}) copy-start(f32[768]{0:T(1024)} %copy-done.104) | copy-start | bytes 9220
  1595.1 484.2 %copy-start.133 = (f32[400]{0:T(512)S(1)}, f32[400]{0:T(512)}, u32[]{:S(2)}) copy-start(f32[400]{0:T(512)} %copy-done.132) | copy-start | bytes 4804
  1595.1 484.2 %copy-start.135 = (f32[400]{0:T(512)S(1)}, f32[400]{0:T(512)}, u32[]{:S(2)}) copy-start(f32[400]{0:T(512)} %copy-done.134) | copy-start | bytes 4804
  2086.9 197.9 %reduce-scatter.64.cloned.1.call-start = ((), (), s32[]{:S(2)}) async-start(), calls=%async_computation.58 | async-start | bytes 2433024
  2099.7 310.6 %all-reduce.6.cloned.1.call-start = ((), (), s32[]{:S(2)}) async-start(), calls=%async_computation.48 | async-start | bytes 147456 | tf_op jit(solution)/shard_map/psum | solution.py:102
  (211 other events, 10426.1 us)
Sparse Core Ops, SparseCore 0:
  11.5 56.9 all-gather.26
  71.2 43.0 all-gather.54
  116.5 22.9 all-gather.28
  165.2 33.4 reduce-scatter.31
  200.7 51.7 all-gather.56
  253.9 23.1 all-gather.30
  297.9 33.4 reduce-scatter.33
  333.6 44.1 all-gather.58
  379.4 22.9 all-gather.32
  428.1 33.4 reduce-scatter.35
  463.8 51.7 all-gather.60
  517.0 23.1 all-gather.34
  561.0 33.4 reduce-scatter.37
  596.6 44.1 all-gather.62
  642.2 22.9 all-gather.36
  693.8 33.4 reduce-scatter.39
  729.4 51.7 all-gather.64
  782.6 23.1 all-gather.38
  826.7 33.4 reduce-scatter.41
  863.5 54.9 all-gather.40
  925.7 23.5 all-gather.42
  963.6 33.3 reduce-scatter.43
  1005.3 24.6 all-gather.44
  1082.4 33.4 reduce-scatter.45
  1122.0 24.5 all-gather.46
  1160.3 33.4 reduce-scatter.47
  1200.0 24.5 all-gather.48
  1270.5 33.4 reduce-scatter.49
  1310.0 24.5 all-gather.50
  1347.5 33.4 reduce-scatter.51
  1387.4 24.5 all-gather.52
  1417.4 102.2 reduce-scatter.55
  1523.0 68.5 reduce-scatter.71
  1595.1 68.8 reduce-scatter.69
  1667.6 94.8 reduce-scatter.61
  1766.0 95.2 reduce-scatter.59
  1864.8 95.2 reduce-scatter.57
  1963.7 69.2 reduce-scatter.67
  2035.4 32.6 reduce-scatter.53
  2087.0 93.7 reduce-scatter.65
  2186.1 98.6 reduce-scatter.63
  2290.9 119.3 all-reduce.5
where the time goes:
time: 2510 us; the launch traced here: 2500 us
  waiting for transfers between devices  1740 us (69%)
  matrix products  293 us (12%)
  blocking collectives  174 us (7%)
  local copies, waits for them, and re-layouts  153 us (6%)
  other arithmetic  116 us (5%)
    unnamed x47, waiting for transfers between devices  390 us
    reduce_scatter x3, waiting for transfers between devices, shards(): lax.psum_scatter(mlp_full, 'dp', scatter_dimension=1, tiled=True)  292 us
    reduce_scatter x6, waiting for transfers between devices, reduce_rows(): lax.psum_scatter(row_term(jnp.int32(0), row_count * lax.axis_size('tensor...  191 us
    reduce_scatter x6, waiting for transfers between devices, reduce_grads(): lax.psum_scatter(row_term(jnp.int32(0), row_count * lax.axis_size('tensor...  168 us
    all_gather x3, waiting for transfers between devices, shards(): lax.all_gather(mlp_weight[layer_idx].astype(jnp.bfloat16), 'dp', axis=1,...  152 us
    all_gather x6, waiting for transfers between devices, gather_rows(): return lax.all_gather(values, 'tensor', axis=0, tiled=True)  139 us
    all_gather x3, waiting for transfers between devices, shards(): lax.all_gather(attn_weight[layer_idx].astype(jnp.bfloat16), 'dp', axis=0,...  128 us
    all_gather x6, waiting for transfers between devices, gather_grads(): return lax.all_gather(values, 'tensor', axis=0, tiled=True)  122 us
  transfers between devices with their start and end apart: 42, of which 40 were waited for; matrix products, arithmetic and copies ran while one was open for 8% of the time, Pallas kernels for 0%

commit v1 on v0

v1 whole, which is shorter than its diff:
```python
from functools import partial
import math

import jax
import jax.numpy as jnp
from jax import lax
from jax.sharding import PartitionSpec as P

D = 768
HEAD_DIM = 64
FF = 3072
PATCH = 768
CLASSES = 1000
TOK_IMG = 197
LAYERS = 3
SEQ = 200
EXTRA = 198


decay_rate = 0.5
tiny_sq = 1e-30
floor_scale = 0.001
step_ratio = 1.0
clip_level = 0.1
smoothing = 0.1
norm_eps = 1e-06


def layer_norm(values, gain_vec, shift_vec):
    centred = values - jnp.mean(values, axis=-1, keepdims=True)
    spread = jnp.mean(centred * centred, axis=-1, keepdims=True)
    return centred * lax.rsqrt(spread + norm_eps) * gain_vec + shift_vec


def outer_sum(left_rows, right_rows):
    return lax.dot_general(
        left_rows, right_rows, (((0,), (0,)), ((), ())), preferred_element_type=jnp.float32
    )


def times_transposed(left_rows, right_matrix):
    return lax.dot_general(
        left_rows, right_matrix, (((1,), (1,)), ((), ())), preferred_element_type=jnp.float32
    )


def flatten_all(arrays):
    return jnp.concatenate([jnp.ravel(member) for member in arrays])


def split_all(flat, shapes):
    outputs = []
    offset = 0
    for form_shape in shapes:
        length = math.prod(form_shape)
        outputs.append(flat[offset : offset + length].reshape(form_shape))
        offset = offset + length
    return outputs


def summed_over(axes, arrays):
    return split_all(
        lax.psum(flatten_all(arrays), axes), [member.shape for member in arrays]
    )


def gather_blocks(blocks):
    width = lax.axis_size("tensor")
    full = lax.all_gather(blocks, ("dp", "tensor"), axis=0, tiled=False)
    return full.reshape((-1, width) + blocks.shape)


def scatter_blocks(blocks):
    flat = blocks.reshape((-1,) + blocks.shape[2:])
    return lax.psum_scatter(flat, ("dp", "tensor"), scatter_dimension=0, tiled=False)


def finish_step(weight, update, update_sq, weight_sq, entries):
    clip_factor = jnp.maximum(1.0, jnp.sqrt(update_sq / entries) / clip_level)
    step_size = step_ratio * jnp.maximum(floor_scale, jnp.sqrt(weight_sq / entries))
    return weight - step_size * update / clip_factor


def shards(
    patches, labels, image_count,
    attn_weight, attn_rows, attn_cols,
    mlp_weight, mlp_rows, mlp_cols,
    patch_weight, patch_rows, patch_cols,
    embed_table, embed_rows, embed_cols,
    head_weight, head_rows, head_cols,
    split_vec, split_sq, hidden_bias, hidden_sq,
    shared_vec, shared_sq, head_bias, head_bias_sq,
):
    both = ("dp", "tensor")
    tensor_width = lax.axis_size("tensor")
    dp_width = lax.axis_size("dp")
    tensor_rank = lax.axis_index("tensor")
    shard_rank = lax.axis_index("dp")
    images = patches.shape[0]
    row_count = images * SEQ
    own_rows = attn_weight.shape[1]
    attn_width = attn_weight.shape[3]
    mlp_width = mlp_weight.shape[3]
    heads = D // HEAD_DIM
    score_scale = HEAD_DIM ** (-0.5)
    head_shape = (images, SEQ, heads, HEAD_DIM)
    key_valid = jnp.arange(SEQ) < TOK_IMG
    slot_index = tensor_rank * images + jnp.arange(images)
    image_total = jnp.sum(image_count).astype(jnp.float32)
    image_weight = (
        jnp.where(slot_index < image_count[shard_rank], 1.0, 0.0).astype(jnp.float32) / image_total
    )

    low = jnp.bfloat16
    small_full = gather_blocks(
        jnp.concatenate([patch_weight, embed_table], axis=1).astype(low)[None]
    ).reshape(D, D + EXTRA)
    patch_full, table_full = small_full[:, :D], small_full[:, D:]
    layers = []
    for layer_idx in range(LAYERS):
        attn_full = gather_blocks(
            attn_weight[layer_idx].astype(low).reshape(1, own_rows, 4 * attn_width)
        )
        mlp_full = gather_blocks(mlp_weight[layer_idx].astype(low))
        attn_full = (
            attn_full.reshape(dp_width, tensor_width, own_rows, 4, attn_width)
            .transpose(3, 0, 2, 1, 4)
            .reshape(4, D, D)
        )
        mlp_full = mlp_full.transpose(2, 0, 3, 1, 4).reshape(2, D, FF)
        layers.append((attn_full, mlp_full))
    head_full = gather_blocks(head_weight.astype(low)[None]).reshape(D, CLASSES)
    split_full, hidden_full = split_vec, hidden_bias
    vectors = flatten_all([split_vec, hidden_bias])
    vectors = lax.all_gather(vectors, "tensor", axis=0, tiled=False)
    split_full = (
        vectors[:, : split_vec.size]
        .reshape(tensor_width, LAYERS, 2, attn_width)
        .transpose(1, 2, 0, 3)
        .reshape(LAYERS, 2, D)
    )
    hidden_full = (
        vectors[:, split_vec.size :]
        .reshape(tensor_width, LAYERS, mlp_width)
        .transpose(1, 0, 2)
        .reshape(LAYERS, FF)
    )

    table_rows = table_full.astype(jnp.float32).T
    pixel_rows = patches.reshape(images * (TOK_IMG - 1), PATCH)
    embedded = jnp.dot(pixel_rows, patch_full, preferred_element_type=jnp.float32).reshape(
        images, TOK_IMG - 1, D
    )
    embedded = embedded + table_rows[1:TOK_IMG] + table_rows[TOK_IMG]
    residual = jnp.concatenate(
        [
            jnp.broadcast_to(table_rows[0], (images, 1, D)),
            embedded,
            jnp.zeros((images, SEQ - TOK_IMG, D), jnp.float32),
        ],
        axis=1,
    ).reshape(row_count, D)

    def attend(query_heads, key_heads):
        scores = (
            jnp.einsum(
                "bqhd,bkhd->bhqk", query_heads, key_heads, preferred_element_type=jnp.float32
            )
            * score_scale
        )
        return jnp.where(key_valid, scores, -1e30)

    saved = []
    for layer_idx in range(LAYERS):
        attn_full, mlp_full = layers[layer_idx]
        gains = shared_vec[6 * layer_idx : 6 * layer_idx + 6]
        attn_input = residual
        normed = layer_norm(residual, gains[0], gains[1]).astype(low)
        query_rows = (
            jnp.dot(normed, attn_full[0], preferred_element_type=jnp.float32)
            + split_full[layer_idx, 0]
        ).astype(low)
        key_rows = jnp.dot(normed, attn_full[1], preferred_element_type=jnp.float32).astype(low)
        value_rows = (
            jnp.dot(normed, attn_full[2], preferred_element_type=jnp.float32)
            + split_full[layer_idx, 1]
        ).astype(low)
        scores = attend(query_rows.reshape(head_shape), key_rows.reshape(head_shape))
        log_total = jax.nn.logsumexp(scores, axis=-1, keepdims=True)
        probs = jnp.exp(scores - log_total)
        mixed = (
            jnp.einsum(
                "bhqk,bkhd->bqhd",
                probs.astype(low),
                value_rows.reshape(head_shape),
                preferred_element_type=jnp.float32,
            )
            .astype(low)
            .reshape(row_count, D)
        )
        residual = residual + times_transposed(mixed, attn_full[3]) + gains[2]
        mlp_input = residual
        mlp_normed = layer_norm(residual, gains[3], gains[4]).astype(low)
        hidden_pre = (
            jnp.dot(mlp_normed, mlp_full[0], preferred_element_type=jnp.float32)
            + hidden_full[layer_idx]
        )
        hidden_act = jax.nn.gelu(hidden_pre, approximate=False).astype(low)
        residual = residual + times_transposed(hidden_act, mlp_full[1]) + gains[5]
        saved.append(
            (
                attn_input, normed, query_rows, key_rows, value_rows, log_total,
                mixed, mlp_input, mlp_normed, hidden_pre, hidden_act,
            )
        )
    cls_rows = residual.reshape(images, SEQ, D)[:, 0]
    feature, final_back = jax.vjp(
        layer_norm, cls_rows, shared_vec[6 * LAYERS], shared_vec[6 * LAYERS + 1]
    )
    feature_low = feature.astype(low)
    logits = jnp.dot(feature_low, head_full, preferred_element_type=jnp.float32) + head_bias
    log_norm = jax.nn.logsumexp(logits, axis=-1, keepdims=True)
    onehot = jnp.where(labels[:, None] == jnp.arange(CLASSES)[None, :], 1.0, 0.0).astype(
        jnp.float32
    )
    target = (1.0 - smoothing) * onehot + smoothing / CLASSES
    loss_part = jnp.sum((log_norm[:, 0] - jnp.sum(target * logits, axis=-1)) * image_weight)
    grad_logits = (jnp.exp(logits - log_norm) - target) * image_weight[:, None]
    grad_head_bias = jnp.sum(grad_logits, axis=0)
    logits_low = grad_logits.astype(low)
    grad_head = outer_sum(feature_low, logits_low)
    grad_feature = times_transposed(logits_low, head_full)
    grad_cls, grad_final_gain, grad_final_shift = final_back(grad_feature)
    grad_rows = jnp.concatenate(
        [grad_cls[:, None], jnp.zeros((images, SEQ - 1, D), jnp.float32)], axis=1
    ).reshape(row_count, D)
    head_grad = scatter_blocks(
        grad_head.astype(low).reshape(dp_width, tensor_width, 1, -1, CLASSES)
    )[0].astype(jnp.float32)
    shared_list = [None] * LAYERS
    split_list = [None] * LAYERS
    hidden_list = [None] * LAYERS
    attn_list = [None] * LAYERS
    mlp_list = [None] * LAYERS
    for layer_idx in reversed(range(LAYERS)):
        (
            attn_input, normed, query_rows, key_rows, value_rows, log_total,
            mixed, mlp_input, mlp_normed, hidden_pre, hidden_act,
        ) = saved[layer_idx]
        attn_full, mlp_full = layers[layer_idx]
        gains = shared_vec[6 * layer_idx : 6 * layer_idx + 6]
        grad_down_bias = jnp.sum(grad_rows, axis=0)
        grad_out = grad_rows.astype(low)
        grad_act = jnp.dot(grad_out, mlp_full[1], preferred_element_type=jnp.float32)
        grad_down = outer_sum(grad_out, hidden_act)
        _, gelu_back = jax.vjp(partial(jax.nn.gelu, approximate=False), hidden_pre)
        grad_pre = gelu_back(grad_act)[0]
        hidden_list[layer_idx] = jnp.sum(grad_pre, axis=0)
        pre_low = grad_pre.astype(low)
        grad_up = outer_sum(mlp_normed, pre_low)
        mlp_blocks = (
            jnp.stack([grad_up.astype(low), grad_down.astype(low)])
            .reshape(2, dp_width, own_rows, tensor_width, mlp_width)
            .transpose(1, 3, 0, 2, 4)
        )
        mlp_list[layer_idx] = scatter_blocks(mlp_blocks).astype(jnp.float32)
        grad_mlp_in = times_transposed(pre_low, mlp_full[0])
        _, second_back = jax.vjp(layer_norm, mlp_input, gains[3], gains[4])
        grad_mid, grad_gain_two, grad_shift_two = second_back(grad_mlp_in)
        grad_rows = grad_rows + grad_mid
        grad_out_bias = jnp.sum(grad_rows, axis=0)
        grad_attn_out = grad_rows.astype(low)
        grad_mixed = (
            jnp.dot(grad_attn_out, attn_full[3], preferred_element_type=jnp.float32)
            .astype(low)
            .reshape(head_shape)
        )
        grad_out_proj = outer_sum(grad_attn_out, mixed)
        query_heads = query_rows.reshape(head_shape)
        key_heads = key_rows.reshape(head_shape)
        value_heads = value_rows.reshape(head_shape)
        probs = jnp.exp(attend(query_heads, key_heads) - log_total)
        grad_probs = jnp.einsum(
            "bqhd,bkhd->bhqk", grad_mixed, value_heads, preferred_element_type=jnp.float32
        )
        grad_value = jnp.einsum(
            "bhqk,bqhd->bkhd", probs.astype(low), grad_mixed, preferred_element_type=jnp.float32
        ).reshape(row_count, D)
        inner_sum = jnp.sum(probs * grad_probs, axis=-1, keepdims=True)
        grad_scores = (probs * (grad_probs - inner_sum) * score_scale).astype(low)
        grad_query = jnp.einsum(
            "bhqk,bkhd->bqhd", grad_scores, key_heads, preferred_element_type=jnp.float32
        ).reshape(row_count, D)
        grad_key = jnp.einsum(
            "bhqk,bqhd->bkhd", grad_scores, query_heads, preferred_element_type=jnp.float32
        ).reshape(row_count, D)
        split_list[layer_idx] = jnp.stack([jnp.sum(grad_query, axis=0), jnp.sum(grad_value, axis=0)])
        query_low, key_low, value_low = (
            grad_query.astype(low), grad_key.astype(low), grad_value.astype(low)
        )
        attn_blocks = (
            jnp.stack(
                [
                    outer_sum(normed, query_low).astype(low),
                    outer_sum(normed, key_low).astype(low),
                    outer_sum(normed, value_low).astype(low),
                    grad_out_proj.astype(low),
                ]
            )
            .reshape(4, dp_width, own_rows, tensor_width, attn_width)
            .transpose(1, 3, 2, 0, 4)
            .reshape(dp_width, tensor_width, 1, own_rows, 4 * attn_width)
        )
        attn_list[layer_idx] = (
            scatter_blocks(attn_blocks).astype(jnp.float32).reshape(own_rows, 4, attn_width)
        )
        grad_attn_in = (
            times_transposed(query_low, attn_full[0])
            + times_transposed(key_low, attn_full[1])
            + times_transposed(value_low, attn_full[2])
        )
        _, first_back = jax.vjp(layer_norm, attn_input, gains[0], gains[1])
        grad_low, grad_gain_one, grad_shift_one = first_back(grad_attn_in)
        grad_rows = grad_rows + grad_low
        shared_list[layer_idx] = jnp.stack(
            [
                grad_gain_one, grad_shift_one, grad_out_bias,
                grad_gain_two, grad_shift_two, grad_down_bias,
            ]
        )
    grad_image = grad_rows.reshape(images, SEQ, D)
    grad_first = jnp.sum(grad_image[:, 0], axis=0)
    grad_position = jnp.sum(grad_image[:, 1:TOK_IMG], axis=0)
    grad_patch_bias = jnp.sum(grad_position, axis=0)
    embed_low = grad_image[:, 1:TOK_IMG].astype(low).reshape(images * (TOK_IMG - 1), D)
    grad_patch = outer_sum(pixel_rows, embed_low)
    grad_table = jnp.concatenate([grad_first[None], grad_position, grad_patch_bias[None]], axis=0).T
    small_grad = scatter_blocks(
        jnp.concatenate([grad_patch, grad_table], axis=1)
        .astype(low)
        .reshape(dp_width, tensor_width, 1, -1, D + EXTRA)
    )[0].astype(jnp.float32)
    patch_grad, table_grad = small_grad[:, :D], small_grad[:, D:]
    attn_grad = jnp.stack(attn_list)
    mlp_grad = jnp.stack(mlp_list)
    shared_grad = jnp.concatenate(
        shared_list + [jnp.stack([grad_final_gain, grad_final_shift])], axis=0
    )
    attn_sq = attn_grad * attn_grad
    mlp_sq = mlp_grad * mlp_grad
    patch_sq = patch_grad * patch_grad
    table_sq = table_grad * table_grad
    head_sq = head_grad * head_grad

    split_sums, hidden_sums, shared_full, head_bias_full, loss_total = summed_over(
        both, [jnp.stack(split_list), jnp.stack(hidden_list), shared_grad, grad_head_bias, loss_part]
    )
    split_total = lax.dynamic_slice_in_dim(split_sums, tensor_rank * attn_width, attn_width, 2)
    hidden_total = lax.dynamic_slice_in_dim(hidden_sums, tensor_rank * mlp_width, mlp_width, 1)
    attn_row_full, mlp_row_full = summed_over(
        "tensor", [jnp.sum(attn_sq, axis=3).transpose(0, 2, 1), jnp.sum(mlp_sq, axis=3)]
    )
    attn_col_full, mlp_col_full = summed_over("dp", [jnp.sum(attn_sq, axis=1), jnp.sum(mlp_sq, axis=2)])
    attn_row_new = decay_rate * attn_rows + (1.0 - decay_rate) * (attn_row_full / D + tiny_sq)
    mlp_row_new = decay_rate * mlp_rows + (1.0 - decay_rate) * (mlp_row_full / FF + tiny_sq)
    patch_row_new = decay_rate * patch_rows + (1.0 - decay_rate) * (
        jnp.sum(patch_sq, axis=1) / D + tiny_sq
    )
    table_row_new = decay_rate * embed_rows + (1.0 - decay_rate) * (
        jnp.sum(table_sq, axis=1) / EXTRA + tiny_sq
    )
    head_row_new = decay_rate * head_rows + (1.0 - decay_rate) * (
        jnp.sum(head_sq, axis=1) / CLASSES + tiny_sq
    )
    own_share = 1.0 / tensor_width
    (
        patch_col_full, table_col_full, head_col_full, whole_row_sum,
        attn_old_sum, mlp_old_sum, attn_total, mlp_total, weight_sq_parts,
    ) = summed_over(
        both,
        [
            jnp.sum(patch_sq, axis=0),
            jnp.sum(table_sq, axis=0),
            jnp.sum(head_sq, axis=0),
            jnp.stack([jnp.sum(patch_row_new), jnp.sum(table_row_new), jnp.sum(head_row_new)]),
            jnp.sum(attn_rows, axis=-1) * own_share,
            jnp.sum(mlp_rows, axis=-1) * own_share,
            jnp.sum(attn_sq, axis=(1, 3)),
            jnp.sum(mlp_sq, axis=(2, 3)),
            flatten_all(
                [
                    jnp.sum(attn_weight * attn_weight, axis=(1, 3)),
                    jnp.sum(mlp_weight * mlp_weight, axis=(2, 3)),
                    jnp.sum(patch_weight * patch_weight),
                    jnp.sum(embed_table * embed_table),
                    jnp.sum(head_weight * head_weight),
                ]
            ),
        ],
    )
    weight_sq = split_all(weight_sq_parts, [(LAYERS, 4), (LAYERS, 2), (), (), ()])
    attn_row_mean = (
        decay_rate * attn_old_sum + (1.0 - decay_rate) * (attn_total / D + D * tiny_sq)
    ) / D
    mlp_row_mean = (
        decay_rate * mlp_old_sum + (1.0 - decay_rate) * (mlp_total / FF + D * tiny_sq)
    ) / D
    whole_row_mean = whole_row_sum / jnp.array([PATCH, D, D], jnp.float32)
    attn_col_new = decay_rate * attn_cols + (1.0 - decay_rate) * (attn_col_full / D + tiny_sq)
    mlp_col_new = decay_rate * mlp_cols + (1.0 - decay_rate) * (mlp_col_full / D + tiny_sq)
    patch_col_new = decay_rate * patch_cols + (1.0 - decay_rate) * (
        patch_col_full / PATCH + tiny_sq
    )
    table_col_new = decay_rate * embed_cols + (1.0 - decay_rate) * (table_col_full / D + tiny_sq)
    head_col_new = decay_rate * head_cols + (1.0 - decay_rate) * (head_col_full / D + tiny_sq)
    attn_update = attn_grad * lax.rsqrt(
        attn_row_new.transpose(0, 2, 1)[:, :, :, None]
        * attn_col_new[:, None]
        / attn_row_mean[:, None, :, None]
    )
    mlp_update = mlp_grad * lax.rsqrt(
        mlp_row_new[:, :, :, None] * mlp_col_new[:, :, None, :] / mlp_row_mean[:, :, None, None]
    )
    patch_update = patch_grad * lax.rsqrt(
        patch_row_new[:, None] * patch_col_new[None, :] / whole_row_mean[0]
    )
    table_update = table_grad * lax.rsqrt(
        table_row_new[:, None] * table_col_new[None, :] / whole_row_mean[1]
    )
    head_update = head_grad * lax.rsqrt(
        head_row_new[:, None] * head_col_new[None, :] / whole_row_mean[2]
    )
    split_sq_new = decay_rate * split_sq + (1.0 - decay_rate) * (
        split_total * split_total + tiny_sq
    )
    split_update = split_total * lax.rsqrt(split_sq_new)
    hidden_sq_new = decay_rate * hidden_sq + (1.0 - decay_rate) * (
        hidden_total * hidden_total + tiny_sq
    )
    hidden_update = hidden_total * lax.rsqrt(hidden_sq_new)
    shared_sq_new = decay_rate * shared_sq + (1.0 - decay_rate) * (
        shared_full * shared_full + tiny_sq
    )
    shared_update = shared_full * lax.rsqrt(shared_sq_new)
    head_bias_sq_new = decay_rate * head_bias_sq + (1.0 - decay_rate) * (
        head_bias_full * head_bias_full + tiny_sq
    )
    head_bias_update = head_bias_full * lax.rsqrt(head_bias_sq_new)
    dp_share = 1.0 / dp_width
    attn_u2, mlp_u2, patch_u2, table_u2, head_u2, split_u2, hidden_u2, split_w2, hidden_w2 = (
        summed_over(
            both,
            [
                jnp.sum(attn_update * attn_update, axis=(1, 3)),
                jnp.sum(mlp_update * mlp_update, axis=(2, 3)),
                jnp.sum(patch_update * patch_update),
                jnp.sum(table_update * table_update),
                jnp.sum(head_update * head_update),
                jnp.sum(split_update * split_update, axis=-1) * dp_share,
                jnp.sum(hidden_update * hidden_update, axis=-1) * dp_share,
                jnp.sum(split_vec * split_vec, axis=-1) * dp_share,
                jnp.sum(hidden_bias * hidden_bias, axis=-1) * dp_share,
            ],
        )
    )
    vector_sq = [split_w2, hidden_w2]
    attn_new = finish_step(
        attn_weight, attn_update, attn_u2[:, None, :, None], weight_sq[0][:, None, :, None], D * D
    )
    mlp_new = finish_step(
        mlp_weight, mlp_update, mlp_u2[:, :, None, None], weight_sq[1][:, :, None, None], D * FF
    )
    patch_new = finish_step(patch_weight, patch_update, patch_u2, weight_sq[2], PATCH * D)
    embed_new = finish_step(embed_table, table_update, table_u2, weight_sq[3], D * EXTRA)
    head_new = finish_step(head_weight, head_update, head_u2, weight_sq[4], D * CLASSES)
    split_new = finish_step(
        split_vec, split_update, split_u2[:, :, None], vector_sq[0][:, :, None], D
    )
    hidden_new = finish_step(
        hidden_bias, hidden_update, hidden_u2[:, None], vector_sq[1][:, None], FF
    )
    shared_new = finish_step(
        shared_vec,
        shared_update,
        jnp.sum(shared_update * shared_update, axis=-1, keepdims=True),
        jnp.sum(shared_vec * shared_vec, axis=-1, keepdims=True),
        D,
    )
    head_bias_new = finish_step(
        head_bias,
        head_bias_update,
        jnp.sum(head_bias_update * head_bias_update),
        jnp.sum(head_bias * head_bias),
        CLASSES,
    )
    return (
        loss_total,
        attn_new,
        attn_row_new,
        attn_col_new,
        mlp_new,
        mlp_row_new,
        mlp_col_new,
        patch_new,
        patch_row_new,
        patch_col_new,
        embed_new,
        table_row_new,
        table_col_new,
        head_new,
        head_row_new,
        head_col_new,
        split_new,
        split_sq_new,
        hidden_new,
        hidden_sq_new,
        shared_new,
        shared_sq_new,
        head_bias_new,
        head_bias_sq_new,
    )


def solution(mesh):
    in_specs = (
        P(("dp", "tensor"), None, None),
        P(("dp", "tensor")),
        P(),
        P(None, "dp", None, "tensor"),
        P(None, None, "dp"),
        P(None, None, "tensor"),
        P(None, None, "dp", "tensor"),
        P(None, None, "dp"),
        P(None, None, "tensor"),
        P(("dp", "tensor"), None),
        P(("dp", "tensor")),
        P(),
        P(("dp", "tensor"), None),
        P(("dp", "tensor")),
        P(),
        P(("dp", "tensor"), None),
        P(("dp", "tensor")),
        P(),
        P(None, None, "tensor"),
        P(None, None, "tensor"),
        P(None, "tensor"),
        P(None, "tensor"),
        P(),
        P(),
        P(),
        P(),
    )
    out_specs = (
        P(),
        P(None, "dp", None, "tensor"),
        P(None, None, "dp"),
        P(None, None, "tensor"),
        P(None, None, "dp", "tensor"),
        P(None, None, "dp"),
        P(None, None, "tensor"),
        P(("dp", "tensor"), None),
        P(("dp", "tensor")),
        P(),
        P(("dp", "tensor"), None),
        P(("dp", "tensor")),
        P(),
        P(("dp", "tensor"), None),
        P(("dp", "tensor")),
        P(),
        P(None, None, "tensor"),
        P(None, None, "tensor"),
        P(None, "tensor"),
        P(None, "tensor"),
        P(),
        P(),
        P(),
        P(),
    )
    return jax.shard_map(shards, mesh=mesh, in_specs=in_specs, out_specs=out_specs, check_vma=False)
```

time: 2510 us -> 2180 us (0.87)
  waiting for transfers between devices: 1740 us -> 875 us
  local copies, waits for them, and re-layouts: 153 us -> 668 us
  other arithmetic: 116 us -> 165 us
  blocking collectives: 174 us -> 127 us
    all_gather x20 -> x8, waiting for transfers between devices: 605 us -> 187 us  [gather_blocks(): full = lax.all_gather(blocks, ('dp', 'tensor'), axis=0, tiled=False)]
    unnamed x47 -> x17, waiting for transfers between devices: 390 us -> 1.47 us
    another operation x18 -> x42, local copies, waits for them, and re-layouts: 15.3 us -> 232 us  [the longest x24 98.6 us: shards(): jnp.stack([outer_sum(normed, query_low).astype(low), outer_sum(normed, ke...]
    slice x11 -> x26, local copies, waits for them, and re-layouts: 9.22 us -> 162 us  [the longest x5 56.7 us: shards(): residual = residual + times_transposed(mixed, attn_full[3]) + gains[2]]
    reshape x6 -> x35, local copies, waits for them, and re-layouts: 8.49 us -> 96.3 us  [the longest x3 37.8 us: gather_blocks(): return full.reshape((-1, width) + blocks.shape)]
    transpose x0 -> x6, other arithmetic: none -> 80.9 us  [the longest x3 52 us: shards(): attn_blocks = jnp.stack([outer_sum(normed, query_low).astype(low), outer_...]
    psum x1, waiting for transfers between devices: 79.6 us -> 0.01 us  [summed_over(): lax.psum(flatten_all(arrays), axes)]
    convert_element_type x6 -> x30, local copies, waits for them, and re-layouts: 6.16 us -> 46.3 us  [the longest x6 13.5 us: shards(): grad_query.astype(low)]
  transfers between devices with their start and end apart: 42 -> 17, of which waited for: 40 -> 12; matrix products, arithmetic and copies ran while one was open for 8% -> 39% of each run, Pallas kernels for 0% -> 0%
where the time goes in v1:
time: 2180 us; the launch traced here: 2160 us
  waiting for transfers between devices  875 us (40%)
  local copies, waits for them, and re-layouts  668 us (31%)
  matrix products  304 us (14%)
  other arithmetic  165 us (8%)
  blocking collectives  127 us (6%)
  between operations  24 us (1%)
    reduce_scatter x8, waiting for transfers between devices, scatter_blocks(): lax.psum_scatter(flat, ('dp', 'tensor'), scatter_dimension=0, tiled=False)  687 us
    all_gather x8, waiting for transfers between devices, gather_blocks(): full = lax.all_gather(blocks, ('dp', 'tensor'), axis=0, tiled=False)  187 us
    psum x4, blocking collectives, summed_over(): lax.psum(flatten_all(arrays), axes)  121 us
    another operation x24, local copies, waits for them, and re-layouts, shards(): jnp.stack([outer_sum(normed, query_low).astype(low), outer_sum(normed, ke...  98.6 us
    dot_general x20, matrix products, outer_sum(): lax.dot_general(left_rows, right_rows, (((0,), (0,)), ((), ())), preferre...  63.8 us
    another operation x6, local copies, waits for them, and re-layouts, shards(): jnp.stack([grad_up.astype(low), grad_down.astype(low)])  58.9 us
    slice x5, local copies, waits for them, and re-layouts, shards(): residual = residual + times_transposed(mixed, attn_full[3]) + gains[2]  56.7 us
    transpose x3, other arithmetic, shards(): attn_blocks = jnp.stack([outer_sum(normed, query_low).astype(low), outer_...  52 us
  transfers between devices with their start and end apart: 17, of which 12 were waited for; matrix products, arithmetic and copies ran while one was open for 39% of the time, Pallas kernels for 0%

profile of v1, /device:TPU:0, one launch (start us, length us, event | category | flops | bytes accessed | tf_op | source)
XLA Modules:
  0.0 2162.8 jit_solution(13318066918097520207)
XLA Ops:
  34.8 34.4 %all-gather.12.cloned.1.call-done = bf16[32,1,24,966]{3,2,1,0:T(8,128)(2,1)} async-done(((bf16[1,1,24,966]{3,2,1,0:T(8,128)(2,1)}), bf16[32,1,24,966]{3,2,1,0:T(8,128)(2,1)}) %all-gather.12.cloned.1.call-update) | async-done | bytes 1483792 | tf_op jit(solution)/shard_map/all_gather | solution.py:69
  75.7 58.9 %all-gather.18.cloned.1.call-done = bf16[32,1,96,768]{3,2,1,0:T(8,128)(2,1)} async-done(((bf16[1,1,96,768]{3,2,1,0:T(8,128)(2,1)}), bf16[32,1,96,768]{3,2,1,0:T(8,128)(2,1)}) %all-gather.18.cloned.1.call-update) | async-done | bytes 4718608 | tf_op jit(solution)/shard_map/all_gather | solution.py:69
  134.6 13.2 reshape_reshape.30
  147.8 19.9 fusion.218
  200.0 12.9 reshape_reshape.31
  212.9 19.9 fusion.217
  264.6 12.9 reshape_reshape.29
  277.6 20.1 fusion.219
  360.0 12.6 copy.560
  372.6 11.2 fusion.215
  392.8 37.3 %all-gather.24.cloned.1.call-done = bf16[32,2,96,768]{3,2,1,0:T(8,128)(2,1)} async-done(((bf16[1,2,96,768]{3,2,1,0:T(8,128)(2,1)}), bf16[32,2,96,768]{3,2,1,0:T(8,128)(2,1)}) %all-gather.24.cloned.1.call-update) | async-done | bytes 9437200 | tf_op jit(solution)/shard_map/all_gather | solution.py:69
  430.1 12.4 copy.559
  442.6 10.9 fusion.214
  458.9 54.1 %all-gather.16.cloned.1.call-done = bf16[32,2,96,768]{3,2,1,0:T(8,128)(2,1)} async-done(((bf16[1,2,96,768]{3,2,1,0:T(8,128)(2,1)}), bf16[32,2,96,768]{3,2,1,0:T(8,128)(2,1)}) %all-gather.16.cloned.1.call-update) | async-done | bytes 9437200 | tf_op jit(solution)/shard_map/all_gather | solution.py:69
  513.1 12.7 copy.561
  525.8 10.8 fusion.216
  541.5 15.8 multiply_convert_fusion.5
  590.8 15.8 multiply_convert_fusion.4
  646.9 16.0 multiply_convert_fusion.3
  700.8 10.8 fusion.87
  711.6 11.1 bitcast_reduce_fusion.5
  771.8 10.7 fusion.90
  782.5 11.3 bitcast_reduce_fusion.3
  834.2 10.6 fusion.93
  844.8 10.7 bitcast_reduce_fusion.1
  921.2 17.3 maximum_bitcast_fusion.5
  938.5 11.6 reshape_reshape.36
  992.4 17.3 maximum_bitcast_fusion.4
  1009.7 11.7 reshape_reshape.35
  1063.9 17.3 maximum_bitcast_fusion.3
  1081.3 11.6 reshape_reshape.34
  1100.7 9.8 stack.228
  1116.7 9.8 stack.229
  1153.0 9.8 stack.225
  1168.9 9.8 stack.226
  1178.7 9.7 maximum_bitcast_fusion.1
  1205.6 9.8 stack.222
  1221.5 9.8 stack.223
  1231.4 9.6 maximum_bitcast_fusion
  1269.5 45.5 %reduce-scatter.17.cloned.1.call-done = bf16[1,1,96,768]{3,2,0,1:T(8,128)(2,1)} async-done(((bf16[32,1,96,768]{3,2,0,1:T(8,128)(2,1)}), bf16[1,1,96,768]{3,2,0,1:T(8,128)(2,1)}) %reduce-scatter.17.cloned.1.call-update) | async-done | bytes 147472 | tf_op jit(solution)/shard_map/reduce_scatter | solution.py:75
  1316.2 110.9 %reduce-scatter.15.cloned.1.call-done = bf16[1,1,96,768]{3,2,0,1:T(8,128)(2,1)} async-done(((bf16[32,1,96,768]{3,2,0,1:T(8,128)(2,1)}), bf16[1,1,96,768]{3,2,0,1:T(8,128)(2,1)}) %reduce-scatter.15.cloned.1.call-update) | async-done | bytes 147472 | tf_op jit(solution)/shard_map/reduce_scatter | solution.py:75
  1428.2 110.7 %reduce-scatter.13.cloned.1.call-done = bf16[1,1,96,768]{3,2,0,1:T(8,128)(2,1)} async-done(((bf16[32,1,96,768]{3,2,0,1:T(8,128)(2,1)}), bf16[1,1,96,768]{3,2,0,1:T(8,128)(2,1)}) %reduce-scatter.13.cloned.1.call-update) | async-done | bytes 147472 | tf_op jit(solution)/shard_map/reduce_scatter | solution.py:75
  1541.8 138.0 %reduce-scatter.23.cloned.1.call-done = bf16[1,2,96,768]{3,2,1,0:T(8,128)(2,1)} async-done(((bf16[32,2,96,768]{3,2,1,0:T(8,128)(2,1)}), bf16[1,2,96,768]{3,2,1,0:T(8,128)(2,1)}) %reduce-scatter.23.cloned.1.call-update) | async-done | bytes 294928 | tf_op jit(solution)/shard_map/reduce_scatter | solution.py:75
  1679.8 140.9 %reduce-scatter.21.cloned.1.call-done = bf16[1,2,96,768]{3,2,1,0:T(8,128)(2,1)} async-done(((bf16[32,2,96,768]{3,2,1,0:T(8,128)(2,1)}), bf16[1,2,96,768]{3,2,1,0:T(8,128)(2,1)}) %reduce-scatter.21.cloned.1.call-update) | async-done | bytes 294928 | tf_op jit(solution)/shard_map/reduce_scatter | solution.py:75
  1820.7 140.9 %reduce-scatter.19.cloned.1.call-done = bf16[1,2,96,768]{3,2,1,0:T(8,128)(2,1)} async-done(((bf16[32,2,96,768]{3,2,1,0:T(8,128)(2,1)}), bf16[1,2,96,768]{3,2,1,0:T(8,128)(2,1)}) %reduce-scatter.19.cloned.1.call-update) | async-done | bytes 294928 | tf_op jit(solution)/shard_map/reduce_scatter | solution.py:75
  1974.7 40.0 %psum.36 = f32[2026]{0:T(1024)S(1)} all-reduce(f32[2026]{0:T(1024)S(1)} %concatenate.79), channel_id=1, replica_groups=mesh['dp'=8,'tensor'=4] {'dp','tensor'}, use_global_device_ids=true, to_apply=%region_102.103 | all-reduce | flops 2026 | bytes 16208 | tf_op jit(solution)/shard_map/psum | solution.py:63
  2019.5 37.8 %psum.38 = f32[6912]{0:T(1024)} all-reduce(f32[6912]{0:T(1024)} %pad_maximum_fusion.5), channel_id=1, replica_groups=mesh['dp'=8,'tensor'=4] {'dp'}, use_global_device_ids=true, to_apply=%region_108.109 | all-reduce | flops 6912 | bytes 55296 | tf_op jit(solution)/shard_map/psum | solution.py:63
  2088.6 37.0 %psum.39 = f32[39]{0:T(128)} all-reduce(f32[39]{0:T(128)} %concatenate.82), channel_id=1, replica_groups=mesh['dp'=8,'tensor'=4] {'dp','tensor'}, use_global_device_ids=true, to_apply=%region_118.119 | all-reduce | flops 39 | bytes 312 | tf_op jit(solution)/shard_map/psum | solution.py:63
  (1027 shorter events, 704.9 us)
Async XLA Ops:
  7.2 62.0 %all-gather.12.cloned.1.call-start = ((), (), s32[]{:S(2)}) async-start(), calls=%async_computation.8 | async-start | bytes 1622016 | tf_op jit(solution)/shard_map/all_gather | solution.py:69
  11.0 123.6 %all-gather.18.cloned.1.call-start = ((), (), s32[]{:S(2)}) async-start(), calls=%async_computation.11 | async-start | bytes 4866048 | tf_op jit(solution)/shard_map/all_gather | solution.py:69
  14.9 185.1 %all-gather.22.cloned.1.call-start = ((), (), s32[]{:S(2)}) async-start(), calls=%async_computation.13 | async-start | bytes 4866048 | tf_op jit(solution)/shard_map/all_gather | solution.py:69
  15.8 248.8 %all-gather.14.cloned.1.call-start = ((), (), s32[]{:S(2)}) async-start(), calls=%async_computation.9 | async-start | bytes 4866048 | tf_op jit(solution)/shard_map/all_gather | solution.py:69
  16.8 343.2 %all-gather.20.cloned.1.call-start = ((), (), s32[]{:S(2)}) async-start(), calls=%async_computation.12 | async-start | bytes 9732096 | tf_op jit(solution)/shard_map/all_gather | solution.py:69
  18.7 411.5 %all-gather.24.cloned.1.call-start = ((), (), s32[]{:S(2)}) async-start(), calls=%async_computation.14 | async-start | bytes 9732096 | tf_op jit(solution)/shard_map/all_gather | solution.py:69
  19.2 493.8 %all-gather.16.cloned.1.call-start = ((), (), s32[]{:S(2)}) async-start(), calls=%async_computation.10 | async-start | bytes 9732096 | tf_op jit(solution)/shard_map/all_gather | solution.py:69
  20.0 647.0 %all-gather.26.cloned.1.call-start = ((), (), s32[]{:S(2)}) async-start(), calls=%async_computation.24 | async-start | bytes 1622016 | tf_op jit(solution)/shard_map/all_gather | solution.py:69
  21.3 1232.8 %all-reduce.3.cloned.1.call-start = ((), (), s32[]{:S(2)}) async-start(), calls=%async_computation.15 | async-start | bytes 245760 | tf_op jit(solution)/shard_map/psum | solution.py:63
  27.9 47.6 %copy-start.115 = (f32[768]{0:T(1024)}, f32[768]{0:T(1024)S(1)}, u32[]{:S(2)}) copy-start(f32[768]{0:T(1024)S(1)} %slice_reduce_fusion.30) | copy-start | bytes 9220
  28.6 512.8 %copy-start.166 = (f32[768]{0:T(1024)}, f32[768]{0:T(1024)S(1)}, u32[]{:S(2)}) copy-start(f32[768]{0:T(1024)S(1)} %get-tuple-element.72) | copy-start | bytes 9220
  28.6 512.8 %copy-start.212 = (f32[768]{0:T(1024)}, f32[768]{0:T(1024)S(1)}, u32[]{:S(2)}) copy-start(f32[768]{0:T(1024)S(1)} %get-tuple-element.71) | copy-start | bytes 9220
  32.5 508.9 %copy-start.178 = (f32[3072]{0:T(1024)}, f32[3072]{0:T(1024)S(1)}, u32[]{:S(2)}) copy-start(f32[3072]{0:T(1024)S(1)} %add.687) | copy-start | bytes 36868
  73.1 284.1 %copy-start = (f32[2,200,768]{2,1,0:T(8,128)}, f32[2,200,768]{2,1,0:T(8,128)S(1)}, u32[]{:S(2)}) copy-start(f32[2,200,768]{2,1,0:T(8,128)S(1)} %get-tuple-element.136) | copy-start | bytes 3686404
  73.2 74.5 %copy-start.158 = (f32[400]{0:T(512)}, f32[400]{0:T(512)S(1)}, u32[]{:S(2)}) copy-start(f32[400]{0:T(512)S(1)} %div.437) | copy-start | bytes 4804
  75.7 267.1 %copy-start.90 = (bf16[2,200,768]{2,1,0:T(8,128)(2,1)}, bf16[2,200,768]{2,1,0:T(8,128)(2,1)S(1)}, u32[]{:S(2)}) copy-start(bf16[2,200,768]{2,1,0:T(8,128)(2,1)S(1)} %add_convert_fusion.5) | copy-start | bytes 1843204
  359.6 197.7 %copy-start.10 = (f32[400,768]{1,0:T(8,128)}, f32[400,768]{1,0:T(8,128)S(1)}, u32[]{:S(2)}) copy-start(f32[400,768]{1,0:T(8,128)S(1)} %get-tuple-element.205) | copy-start | bytes 3686404
  359.7 181.8 %copy-start.145 = (f32[400]{0:T(512)}, f32[400]{0:T(512)S(1)}, u32[]{:S(2)}) copy-start(f32[400]{0:T(512)S(1)} %broadcast_multiply_fusion.8) | copy-start | bytes 4804
  360.0 181.5 %copy-start.189 = (f32[400]{0:T(512)}, f32[400]{0:T(512)S(1)}, u32[]{:S(2)}) copy-start(f32[400]{0:T(512)S(1)} %fusion.156) | copy-start | bytes 4804
  559.6 28.5 %copy-start.2 = (f32[400,768]{1,0:T(8,128)}, f32[400,768]{1,0:T(8,128)S(1)}, u32[]{:S(2)}) copy-start(f32[400,768]{1,0:T(8,128)S(1)} %get-tuple-element.208) | copy-start | bytes 3686404
  588.0 18.6 copy-start.58
  588.1 18.6 slice-start.12
  590.4 167.5 %copy-start.13 = (f32[400,768]{1,0:T(8,128)}, f32[400,768]{1,0:T(8,128)S(1)}, u32[]{:S(2)}) copy-start(f32[400,768]{1,0:T(8,128)S(1)} %get-tuple-element.212) | copy-start | bytes 3686404
  590.4 167.5 %copy-start.148 = (f32[400]{0:T(512)}, f32[400]{0:T(512)S(1)}, u32[]{:S(2)}) copy-start(f32[400]{0:T(512)S(1)} %broadcast_multiply_fusion.6) | copy-start | bytes 4804
  590.7 167.2 %copy-start.192 = (f32[400]{0:T(512)}, f32[400]{0:T(512)S(1)}, u32[]{:S(2)}) copy-start(f32[400]{0:T(512)S(1)} %fusion.158) | copy-start | bytes 4804
  644.1 18.8 copy-start.60
  646.5 17.5 copy-start.15
  646.5 37.4 %copy-start.150 = (f32[400]{0:T(512)}, f32[400]{0:T(512)S(1)}, u32[]{:S(2)}) copy-start(f32[400]{0:T(512)S(1)} %broadcast_multiply_fusion.4) | copy-start | bytes 4804
  646.8 37.1 %copy-start.194 = (f32[400]{0:T(512)}, f32[400]{0:T(512)S(1)}, u32[]{:S(2)}) copy-start(f32[400]{0:T(512)S(1)} %fusion.160) | copy-start | bytes 4804
  759.4 50.1 %copy-start.24 = (f32[400,768]{1,0:T(8,128)}, f32[400,768]{1,0:T(8,128)S(1)}, u32[]{:S(2)}) copy-start(f32[400,768]{1,0:T(8,128)S(1)} %get-tuple-element.108) | copy-start | bytes 3686404
  822.1 47.3 %copy-start.26 = (f32[400,768]{1,0:T(8,128)}, f32[400,768]{1,0:T(8,128)S(1)}, u32[]{:S(2)}) copy-start(f32[400,768]{1,0:T(8,128)S(1)} %get-tuple-element.112) | copy-start | bytes 3686404
  875.2 389.6 %reduce-scatter.9.cloned.1.call-start = ((), (), s32[]{:S(2)}) async-start(), calls=%async_computation.16 | async-start | bytes 1622016 | tf_op jit(solution)/shard_map/reduce_scatter | solution.py:75
  876.9 390.6 %reduce-scatter.11.cloned.1.call-start = ((), (), s32[]{:S(2)}) async-start(), calls=%async_computation.17 | async-start | bytes 1622016 | tf_op jit(solution)/shard_map/reduce_scatter | solution.py:75
  880.2 434.8 %reduce-scatter.17.cloned.1.call-start = ((), (), s32[]{:S(2)}) async-start(), calls=%async_computation.20 | async-start | bytes 4866048 | tf_op jit(solution)/shard_map/reduce_scatter | solution.py:75
  950.1 476.9 %reduce-scatter.15.cloned.1.call-start = ((), (), s32[]{:S(2)}) async-start(), calls=%async_computation.19 | async-start | bytes 4866048 | tf_op jit(solution)/shard_map/reduce_scatter | solution.py:75
  1021.4 517.5 %reduce-scatter.13.cloned.1.call-start = ((), (), s32[]{:S(2)}) async-start(), calls=%async_computation.18 | async-start | bytes 4866048 | tf_op jit(solution)/shard_map/reduce_scatter | solution.py:75
  1092.9 586.9 %reduce-scatter.23.cloned.1.call-start = ((), (), s32[]{:S(2)}) async-start(), calls=%async_computation.23 | async-start | bytes 9732096 | tf_op jit(solution)/shard_map/reduce_scatter | solution.py:75
  1145.5 675.2 %reduce-scatter.21.cloned.1.call-start = ((), (), s32[]{:S(2)}) async-start(), calls=%async_computation.22 | async-start | bytes 9732096 | tf_op jit(solution)/shard_map/reduce_scatter | solution.py:75
  1197.7 763.9 %reduce-scatter.19.cloned.1.call-start = ((), (), s32[]{:S(2)}) async-start(), calls=%async_computation.21 | async-start | bytes 9732096 | tf_op jit(solution)/shard_map/reduce_scatter | solution.py:75
  1250.6 17.8 copy-start.238
  1250.7 719.2 %copy-start.205 = (f32[3,4,96]{2,1,0:T(4,128)S(1)}, f32[3,4,96]{2,1,0:T(4,128)}, u32[]{:S(2)}) copy-start(f32[3,4,96]{2,1,0:T(4,128)} %param.31) | copy-start | bytes 13828
  1250.7 719.9 %copy-start.233 = (f32[3,2,96]{2,1,0:T(2,128)S(1)}, f32[3,2,96]{2,1,0:T(2,128)}, u32[]{:S(2)}) copy-start(f32[3,2,96]{2,1,0:T(2,128)} %param.34) | copy-start | bytes 6916
  1255.5 60.7 %copy-start.164 = (f32[1000]{0:T(1024)}, f32[1000]{0:T(1024)S(1)}, u32[]{:S(2)}) copy-start(f32[1000]{0:T(1024)S(1)} %get-tuple-element.89) | copy-start | bytes 12004
  1316.2 831.1 %copy-start.49 = (f32[3,96,4,192]{3,2,1,0:T(4,128)S(1)}, f32[3,96,4,192]{3,2,1,0:T(4,128)}, u32[]{:S(2)}) copy-start(f32[3,96,4,192]{3,2,1,0:T(4,128)} %param.30) | copy-start | bytes 2654212
  1970.7 102.3 %copy-start.141 = (f32[3,2,96]{2,1,0:T(2,128)}, f32[3,2,96]{2,1,0:T(2,128)S(1)}, u32[]{:S(2)}) copy-start(f32[3,2,96]{2,1,0:T(2,128)S(1)} %get-tuple-element.185) | copy-start | bytes 6916
  2016.7 137.6 %copy-start.32 = (f32[3,2,96,768]{3,2,1,0:T(8,128)S(1)}, f32[3,2,96,768]{3,2,1,0:T(8,128)}, u32[]{:S(2)}) copy-start(f32[3,2,96,768]{3,2,1,0:T(8,128)} %param.33) | copy-start | bytes 5308420
  2065.1 90.9 %copy-start.131 = (f32[768]{0:T(1024)}, f32[768]{0:T(1024)S(1)}, u32[]{:S(2)}) copy-start(f32[768]{0:T(1024)S(1)} %fusion.147) | copy-start | bytes 9220
  2075.1 81.0 %copy-start.110 = (f32[3,4,192]{2,1,0:T(4,128)}, f32[3,4,192]{2,1,0:T(4,128)S(1)}, u32[]{:S(2)}) copy-start(f32[3,4,192]{2,1,0:T(4,128)S(1)} %add_multiply_fusion.3) | copy-start | bytes 27652
  (237 other events, 1258.1 us)
Sparse Core Ops, SparseCore 0:
  11.5 57.6 all-gather.11
  72.1 62.4 all-gather.17
  138.1 61.8 all-gather.21
  202.7 61.8 all-gather.13
  267.4 79.7 all-gather.19
  349.9 80.1 all-gather.23
  433.1 79.9 all-gather.15
  516.5 53.4 all-gather.25
  875.3 121.7 all-reduce.2
  1002.8 98.1 reduce-scatter.8
  1106.2 96.8 reduce-scatter.10
  1208.5 106.5 reduce-scatter.16
  1320.5 106.4 reduce-scatter.14
  1432.4 106.4 reduce-scatter.12
  1544.6 135.0 reduce-scatter.22
  1685.5 135.1 reduce-scatter.20
  1826.4 135.0 reduce-scatter.18

commit v2 on v1

--- a/solution.py
+++ b/solution.py
@@ -4,6 +4,8 @@
 import jax
 import jax.numpy as jnp
 from jax import lax
+from jax.experimental import pallas as pl
+from jax.experimental.pallas import tpu as pltpu
 from jax.sharding import PartitionSpec as P
 
 D = 768
@@ -64,15 +66,602 @@
     )
 
 
-def gather_blocks(blocks):
-    width = lax.axis_size("tensor")
-    full = lax.all_gather(blocks, ("dp", "tensor"), axis=0, tiled=False)
-    return full.reshape((-1, width) + blocks.shape)
-
-
-def scatter_blocks(blocks):
-    flat = blocks.reshape((-1,) + blocks.shape[2:])
-    return lax.psum_scatter(flat, ("dp", "tensor"), scatter_dimension=0, tiled=False)
+MESH = pl.DeviceIdType.MESH
+DIMS = ("y", "c", "zb", "za", "x")
+OUT_ORDERS = (("zb", "za", "x", "y", "c"), ("zb", "za", "y", "x", "c"))
+IN_ORDERS = (("c", "y", "x", "za", "zb"), ("c", "x", "y", "za", "zb"))
+
+
+def place_of_device():
+    dp, tensor = lax.axis_index("dp"), lax.axis_index("tensor")
+    return {
+        "x": lax.rem(dp, 2),
+        "za": lax.rem(dp // 2, 2),
+        "zb": dp // 4,
+        "y": tensor // 2,
+        "c": lax.rem(tensor, 2),
+    }
+
+
+def partner_of(place, dim):
+    moved = dict(place)
+    moved[dim] = 1 - place[dim]
+    return (
+        moved["zb"] * 4 + moved["za"] * 2 + moved["x"],
+        moved["y"] * 2 + moved["c"],
+    )
+
+
+def meet_partners(place):
+    barrier = pltpu.get_barrier_semaphore()
+    for dim in DIMS:
+        pl.semaphore_signal(
+            barrier, inc=1, device_id=partner_of(place, dim), device_id_type=MESH
+        )
+    pl.semaphore_wait(barrier, len(DIMS))
+
+
+def spread_kernel(groups, *refs):
+    arrays = len({flow[0] for group in groups for flow in group})
+    sources, targets = refs[:arrays], refs[arrays : 2 * arrays]
+    send_sem, recv_sem, own_sem = refs[2 * arrays :]
+    place = place_of_device()
+    flows = [flow for group in groups for flow in group]
+    number = {flow: position for position, flow in enumerate(flows)}
+
+    def own_copy(flow):
+        array, lead, tail, _ = flow
+        slot = lead + tuple(place[dim] for dim in DIMS) + tail
+        return pltpu.make_async_copy(
+            sources[array].at[lead + tail], targets[array].at[slot], own_sem.at[number[flow]]
+        )
+
+    def stage_copy(flow, stage):
+        array, lead, tail, order = flow
+        dims = OUT_ORDERS[order]
+        done = dims[:stage]
+        slot = lead + tuple(slice(None) if dim in done else place[dim] for dim in DIMS) + tail
+        source = sources[array].at[lead + tail] if stage == 0 else targets[array].at[slot]
+        return pltpu.make_async_remote_copy(
+            src_ref=source,
+            dst_ref=targets[array].at[slot],
+            send_sem=send_sem.at[number[flow], stage],
+            recv_sem=recv_sem.at[number[flow], stage],
+            device_id=partner_of(place, dims[stage]),
+            device_id_type=MESH,
+        )
+
+    meet_partners(place)
+    stages = len(DIMS)
+    for tick in range(len(groups) + stages):
+        for stage in reversed(range(stages + 1)):
+            if not 0 <= tick - stage < len(groups):
+                continue
+            for flow in groups[tick - stage]:
+                if stage == 1:
+                    own_copy(flow).wait()
+                if stage > 0:
+                    stage_copy(flow, stage - 1).wait_recv()
+                if stage == 0:
+                    own_copy(flow).start()
+                if stage < stages:
+                    stage_copy(flow, stage).start()
+    for flow in flows:
+        for stage in range(stages):
+            stage_copy(flow, stage).wait_send()
+
+
+def spread(arrays, groups, collective_id):
+    count = sum(len(group) for group in groups)
+    leads = {flow[0]: len(flow[1]) for group in groups for flow in group}
+    shapes = [
+        member.shape[: leads[position]] + (2,) * len(DIMS) + member.shape[leads[position] :]
+        for position, member in enumerate(arrays)
+    ]
+    return pl.pallas_call(
+        partial(spread_kernel, groups),
+        out_shape=[
+            jax.ShapeDtypeStruct(shape, member.dtype) for shape, member in zip(shapes, arrays)
+        ],
+        in_specs=[pl.BlockSpec(memory_space=pltpu.VMEM)] * len(arrays),
+        out_specs=[pl.BlockSpec(memory_space=pl.ANY)] * len(arrays),
+        scratch_shapes=[
+            pltpu.SemaphoreType.DMA((count, len(DIMS))),
+            pltpu.SemaphoreType.DMA((count, len(DIMS))),
+            pltpu.SemaphoreType.DMA((count,)),
+        ],
+        compiler_params=pltpu.CompilerParams(
+            collective_id=collective_id, has_side_effects=True, vmem_limit_bytes=16 << 20
+        ),
+    )(*arrays)
+
+
+def collect_kernel(groups, arrays, *refs):
+    sources, targets = refs[:arrays], refs[arrays : 2 * arrays]
+    held, landed = refs[2 * arrays], refs[2 * arrays + 1 : 2 * arrays + 6]
+    send_sem, recv_sem, own_sem = refs[2 * arrays + 6 :]
+    place = place_of_device()
+    flows = [flow for group in groups for flow in group]
+    number = {flow: position for position, flow in enumerate(flows)}
+    kept = ("y", "zb", "za", "x")
+
+    def core_slot(flow, core):
+        _, lead, tail, _ = flow
+        return lead + tuple(core if dim == "c" else slice(None) for dim in DIMS) + tail
+
+    def own_copy(flow):
+        return pltpu.make_async_copy(
+            sources[flow[0]].at[core_slot(flow, place["c"])],
+            held.at[number[flow]],
+            own_sem.at[number[flow]],
+        )
+
+    def held_slot(done, moved):
+        slot = ()
+        for dim in kept:
+            if dim == moved:
+                slot += (1 - place[dim],)
+            elif dim in done:
+                slot += (place[dim],)
+            else:
+                slot += (slice(None),)
+        return slot
+
+    def stage_copy(flow, stage):
+        dims = IN_ORDERS[flow[3]]
+        index = number[flow]
+        if stage == 0:
+            source = sources[flow[0]].at[core_slot(flow, 1 - place["c"])]
+        else:
+            source = held.at[(index,) + held_slot(dims[:stage], dims[stage])]
+        return pltpu.make_async_remote_copy(
+            src_ref=source,
+            dst_ref=landed[stage].at[index],
+            send_sem=send_sem.at[index, stage],
+            recv_sem=recv_sem.at[index, stage],
+            device_id=partner_of(place, dims[stage]),
+            device_id_type=MESH,
+        )
+
+    def add_landed(flow, stage):
+        array, lead, tail, order = flow
+        dims = IN_ORDERS[order]
+        index = number[flow]
+        free = [dim for dim in kept if dim not in dims[: stage + 1]]
+
+        def add_block(step, carry):
+            rest = step
+            at = {}
+            for dim in reversed(free):
+                at[dim] = lax.rem(rest, 2)
+                rest = rest // 2
+            slot = (index,) + tuple(at[dim] if dim in free else place[dim] for dim in kept)
+            landed_slot = (index,) + tuple(at[dim] for dim in free)
+            total = held[slot].astype(jnp.float32) + landed[stage][landed_slot].astype(jnp.float32)
+            if stage == len(DIMS) - 1:
+                targets[array][lead + tail] = total
+            else:
+                held[slot] = total.astype(jnp.bfloat16)
+            return carry
+
+        if free:
+            lax.fori_loop(0, 2 ** len(free), add_block, 0)
+        else:
+            add_block(0, 0)
+
+    meet_partners(place)
+    stages = len(DIMS)
+    for tick in range(len(groups) + stages):
+        for stage in reversed(range(stages + 1)):
+            if not 0 <= tick - stage < len(groups):
+                continue
+            for flow in groups[tick - stage]:
+                if stage == 0:
+                    own_copy(flow).start()
+                if stage == 1:
+                    own_copy(flow).wait()
+                if stage > 0:
+                    stage_copy(flow, stage - 1).wait_recv()
+                    add_landed(flow, stage - 1)
+                if stage < stages:
+                    stage_copy(flow, stage).start()
+    for flow in flows:
+        for stage in range(stages):
+            stage_copy(flow, stage).wait_send()
+
+
+def collect(arrays, groups, collective_id):
+    leads = {flow[0]: len(flow[1]) for group in groups for flow in group}
+    count = sum(len(group) for group in groups)
+    block = arrays[0].shape[-2:]
+    low = jnp.bfloat16
+    return pl.pallas_call(
+        partial(collect_kernel, groups, len(arrays)),
+        out_shape=[
+            jax.ShapeDtypeStruct(
+                member.shape[: leads[position]] + member.shape[leads[position] + len(DIMS) :],
+                jnp.float32,
+            )
+            for position, member in enumerate(arrays)
+        ],
+        in_specs=[pl.BlockSpec(memory_space=pl.ANY)] * len(arrays),
+        out_specs=[pl.BlockSpec(memory_space=pltpu.VMEM)] * len(arrays),
+        scratch_shapes=[
+            pltpu.VMEM((count, 2, 2, 2, 2) + block, low),
+            pltpu.VMEM((count, 2, 2, 2, 2) + block, low),
+            pltpu.VMEM((count, 2, 2, 2) + block, low),
+            pltpu.VMEM((count, 2, 2) + block, low),
+            pltpu.VMEM((count, 2) + block, low),
+            pltpu.VMEM((count,) + block, low),
+            pltpu.SemaphoreType.DMA((count, len(DIMS))),
+            pltpu.SemaphoreType.DMA((count, len(DIMS))),
+            pltpu.SemaphoreType.DMA((count,)),
+        ],
+        compiler_params=pltpu.CompilerParams(
+            collective_id=collective_id, has_side_effects=True, vmem_limit_bytes=48 << 20
+        ),
+    )(*arrays)
+
+
+PAD_ROWS = 208
+HALF_ROOT = 0.7071067811865476
+DENSITY = 0.3989422804014327
+
+
+def dot_nn(left, right):
+    return lax.dot_general(left, right, (((1,), (0,)), ((), ())), preferred_element_type=jnp.float32)
+
+
+def dot_nt(left, right):
+    return lax.dot_general(left, right, (((1,), (1,)), ((), ())), preferred_element_type=jnp.float32)
+
+
+def dot_tn(left, right):
+    return lax.dot_general(left, right, (((0,), (0,)), ((), ())), preferred_element_type=jnp.float32)
+
+
+def normal_form(values):
+    centred = values - jnp.mean(values, axis=-1, keepdims=True)
+    spread_sq = jnp.mean(centred * centred, axis=-1, keepdims=True)
+    inverse = lax.rsqrt(spread_sq + norm_eps)
+    return centred * inverse, inverse
+
+
+def norm_back(grad, unit, inverse, gain):
+    inner = grad * gain
+    return inverse * (
+        inner
+        - jnp.mean(inner, axis=-1, keepdims=True)
+        - unit * jnp.mean(inner * unit, axis=-1, keepdims=True)
+    )
+
+
+def head_probs(query, key):
+    scores = dot_nt(query, key) * HEAD_DIM ** (-0.5)
+    column = lax.broadcasted_iota(jnp.int32, scores.shape, 1)
+    scores = jnp.where(column < TOK_IMG, scores, -1e30)
+    powers = jnp.exp(scores - jnp.max(scores, axis=-1, keepdims=True))
+    return powers / jnp.sum(powers, axis=-1, keepdims=True)
+
+
+def forward_kernel(
+    images, parts, x_ref, gain_ref, attn_ref, up_ref, down_ref, split_ref, hidden_ref,
+    next_ref, mid_ref, qkv_ref, mixed_ref, act_ref, slope_ref, normed,
+):
+    step = pl.program_id(0)
+    low = jnp.bfloat16
+    width = mixed_ref.shape[-1]
+    heads = width // HEAD_DIM
+
+    @pl.when(step == 0)
+    def _():
+        unit, _ = normal_form(x_ref[...])
+        normed[...] = (unit * gain_ref[0:1] + gain_ref[1:2]).astype(low)
+        mid_ref[...] = x_ref[...] + gain_ref[2:3]
+
+    @pl.when(step < parts)
+    def _():
+        weights = attn_ref[0]
+        qkv = (dot_nn(normed[...], weights[:, : 3 * width]) + split_ref[0]).astype(low)
+        qkv_ref[0] = qkv
+        columns = []
+        for head in range(heads):
+            rows = []
+            for image in range(images):
+                at = slice(image * PAD_ROWS, (image + 1) * PAD_ROWS)
+                query, key, value = (
+                    qkv[at, kind * width + head * HEAD_DIM : kind * width + (head + 1) * HEAD_DIM]
+                    for kind in range(3)
+                )
+                probs = head_probs(query, key).astype(low)
+                rows.append(dot_nn(probs, value).astype(low))
+            columns.append(jnp.concatenate(rows, axis=0))
+        mixed = jnp.concatenate(columns, axis=1)
+        mixed_ref[0] = mixed
+        mid_ref[...] += dot_nt(mixed, weights[:, 3 * width :])
+
+    @pl.when(step == parts)
+    def _():
+        unit, _ = normal_form(mid_ref[...])
+        normed[...] = (unit * gain_ref[3:4] + gain_ref[4:5]).astype(low)
+        next_ref[...] = mid_ref[...] + gain_ref[5:6]
+
+    @pl.when(step >= parts)
+    def _():
+        pre = dot_nn(normed[...], up_ref[0]) + hidden_ref[0]
+        share = 0.5 * (1.0 + lax.erf(pre * HALF_ROOT))
+        act = (pre * share).astype(low)
+        act_ref[0] = act
+        slope_ref[0] = (share + pre * (DENSITY * jnp.exp(-0.5 * pre * pre))).astype(low)
+        next_ref[...] += dot_nt(act, down_ref[0])
+
+
+def forward_layer(layer_idx, images, x, gains, weights, split_rows, hidden_rows):
+    rows = x.shape[0]
+    parts = hidden_rows.shape[0]
+    base = layer_idx * 3 * parts
+    width, hidden = split_rows.shape[-1] // 3, hidden_rows.shape[-1]
+    block = weights.shape[1:]
+    early = lambda step: jnp.minimum(step, parts - 1)
+    late = lambda step: jnp.maximum(step - parts, 0)
+    whole = lambda shape: pl.BlockSpec(shape, lambda step: (0,) * len(shape))
+    low = jnp.bfloat16
+    return pl.pallas_call(
+        partial(forward_kernel, images, parts),
+        grid=(2 * parts,),
+        out_shape=[
+            jax.ShapeDtypeStruct((rows, D), jnp.float32),
+            jax.ShapeDtypeStruct((rows, D), jnp.float32),
+            jax.ShapeDtypeStruct((parts, rows, 3 * width), low),
+            jax.ShapeDtypeStruct((parts, rows, width), low),
+            jax.ShapeDtypeStruct((parts, rows, hidden), low),
+            jax.ShapeDtypeStruct((parts, rows, hidden), low),
+        ],
+        in_specs=[
+            whole((rows, D)),
+            whole(gains.shape),
+            pl.BlockSpec((1,) + block, lambda step: (base + early(step), 0, 0)),
+            pl.BlockSpec((1,) + block, lambda step: (base + parts + late(step), 0, 0)),
+            pl.BlockSpec((1,) + block, lambda step: (base + 2 * parts + late(step), 0, 0)),
+            pl.BlockSpec((1, 1, 3 * width), lambda step: (early(step), 0, 0)),
+            pl.BlockSpec((1, 1, hidden), lambda step: (late(step), 0, 0)),
+        ],
+        out_specs=[
+            whole((rows, D)),
+            whole((rows, D)),
+            pl.BlockSpec((1, rows, 3 * width), lambda step: (early(step), 0, 0)),
+            pl.BlockSpec((1, rows, width), lambda step: (early(step), 0, 0)),
+            pl.BlockSpec((1, rows, hidden), lambda step: (late(step), 0, 0)),
+            pl.BlockSpec((1, rows, hidden), lambda step: (late(step), 0, 0)),
+        ],
+        scratch_shapes=[pltpu.VMEM((rows, D), low)],
+        compiler_params=pltpu.CompilerParams(vmem_limit_bytes=48 << 20),
+    )(x, gains, weights, weights, weights, split_rows, hidden_rows)
+
+
+def backward_kernel(
+    images, parts, grad_ref, x_ref, mid_ref, gain_ref, attn_ref, up_ref, down_ref,
+    qkv_ref, mixed_ref, act_ref, slope_ref,
+    out_ref, attn_grad_ref, mlp_grad_ref, shared_ref, split_ref, hidden_ref,
+    total, low_grad, turned_grad, turned_in,
+):
+    step = pl.program_id(0)
+    low = jnp.bfloat16
+    width = mixed_ref.shape[-1]
+    heads = width // HEAD_DIM
+
+    def row_sum(values):
+        return jnp.sum(values, axis=0, keepdims=True)
+
+    @pl.when(step == 0)
+    def _():
+        grad = grad_ref[...]
+        shared_ref[5:6] = row_sum(grad)
+        low_grad[...] = grad.astype(low)
+        turned_grad[...] = grad.T.astype(low)
+        unit, _ = normal_form(mid_ref[...])
+        turned_in[...] = (unit * gain_ref[3:4] + gain_ref[4:5]).T.astype(low)
+        total[...] = jnp.zeros_like(total)
+
+    @pl.when(step < parts)
+    def _():
+        act_grad = dot_nn(low_grad[...], down_ref[0])
+        mlp_grad_ref[1, 0] = dot_nn(turned_grad[...], act_ref[0]).astype(low)
+        pre_grad = act_grad * slope_ref[0].astype(jnp.float32)
+        hidden_ref[0] = row_sum(pre_grad)
+        pre_low = pre_grad.astype(low)
+        mlp_grad_ref[0, 0] = dot_nn(turned_in[...], pre_low).astype(low)
+        total[...] += dot_nt(pre_low, up_ref[0])
+
+    @pl.when(step == parts)
+    def _():
+        unit, inverse = normal_form(mid_ref[...])
+        back = total[...]
+        shared_ref[3:4] = row_sum(back * unit)
+        shared_ref[4:5] = row_sum(back)
+        grad = grad_ref[...] + norm_back(back, unit, inverse, gain_ref[3:4])
+        out_ref[...] = grad
+        shared_ref[2:3] = row_sum(grad)
+        low_grad[...] = grad.astype(low)
+        turned_grad[...] = grad.T.astype(low)
+        unit, _ = normal_form(x_ref[...])
+        turned_in[...] = (unit * gain_ref[0:1] + gain_ref[1:2]).T.astype(low)
+        total[...] = jnp.zeros_like(total)
+
+    @pl.when(step >= parts)
+    def _():
+        weights = attn_ref[0]
+        qkv = qkv_ref[0]
+        mixed_grad = dot_nn(low_grad[...], weights[:, 3 * width :]).astype(low)
+        pieces = [[None] * heads for _ in range(3)]
+        for head in range(heads):
+            rows = [[], [], []]
+            for image in range(images):
+                at = slice(image * PAD_ROWS, (image + 1) * PAD_ROWS)
+                query, key, value = (
+                    qkv[at, kind * width + head * HEAD_DIM : kind * width + (head + 1) * HEAD_DIM]
+                    for kind in range(3)
+                )
+                out_grad = mixed_grad[at, head * HEAD_DIM : (head + 1) * HEAD_DIM]
+                probs = head_probs(query, key)
+                prob_grad = dot_nt(out_grad, value)
+                inner = jnp.sum(probs * prob_grad, axis=-1, keepdims=True)
+                score_grad = (probs * (prob_grad - inner) * HEAD_DIM ** (-0.5)).astype(low)
+                rows[0].append(dot_nn(score_grad, key))
+                rows[1].append(dot_tn(score_grad, query))
+                rows[2].append(dot_tn(probs.astype(low), out_grad))
+            for kind in range(3):
+                pieces[kind][head] = jnp.concatenate(rows[kind], axis=0)
+        qkv_grad = jnp.concatenate(pieces[0] + pieces[1] + pieces[2], axis=1)
+        split_ref[0] = row_sum(qkv_grad)
+        qkv_low = qkv_grad.astype(low)
+        attn_grad_ref[0, :, : 3 * width] = dot_nn(turned_in[...], qkv_low).astype(low)
+        attn_grad_ref[0, :, 3 * width :] = dot_nn(turned_grad[...], mixed_ref[0]).astype(low)
+        total[...] += dot_nt(qkv_low, weights[:, : 3 * width])
+
+    @pl.when(step == 2 * parts - 1)
+    def _():
+        unit, inverse = normal_form(x_ref[...])
+        back = total[...]
+        shared_ref[0:1] = row_sum(back * unit)
+        shared_ref[1:2] = row_sum(back)
+        out_ref[...] += norm_back(back, unit, inverse, gain_ref[0:1])
+
+
+def backward_layer(layer_idx, images, grad, x, mid, gains, weights, qkv, mixed, act, slope):
+    rows = x.shape[0]
+    parts = act.shape[0]
+    base = layer_idx * 3 * parts
+    width, hidden = mixed.shape[-1], act.shape[-1]
+    block = weights.shape[1:]
+    early = lambda step: jnp.minimum(step, parts - 1)
+    late = lambda step: jnp.maximum(step - parts, 0)
+    whole = lambda shape: pl.BlockSpec(shape, lambda step: (0,) * len(shape))
+    low = jnp.bfloat16
+    return pl.pallas_call(
+        partial(backward_kernel, images, parts),
+        grid=(2 * parts,),
+        out_shape=[
+            jax.ShapeDtypeStruct((rows, D), jnp.float32),
+            jax.ShapeDtypeStruct((parts,) + block, low),
+            jax.ShapeDtypeStruct((2, parts) + block, low),
+            jax.ShapeDtypeStruct((6, D), jnp.float32),
+            jax.ShapeDtypeStruct((parts, 1, 3 * width), jnp.float32),
+            jax.ShapeDtypeStruct((parts, 1, hidden), jnp.float32),
+        ],
+        in_specs=[
+            whole((rows, D)),
+            whole((rows, D)),
+            whole((rows, D)),
+            whole(gains.shape),
+            pl.BlockSpec((1,) + block, lambda step: (base + late(step), 0, 0)),
+            pl.BlockSpec((1,) + block, lambda step: (base + parts + early(step), 0, 0)),
+            pl.BlockSpec((1,) + block, lambda step: (base + 2 * parts + early(step), 0, 0)),
+            pl.BlockSpec((1, rows, 3 * width), lambda step: (late(step), 0, 0)),
+            pl.BlockSpec((1, rows, width), lambda step: (late(step), 0, 0)),
+            pl.BlockSpec((1, rows, hidden), lambda step: (early(step), 0, 0)),
+            pl.BlockSpec((1, rows, hidden), lambda step: (early(step), 0, 0)),
+        ],
+        out_specs=[
+            whole((rows, D)),
+            pl.BlockSpec((1,) + block, lambda step: (late(step), 0, 0)),
+            pl.BlockSpec((2, 1) + block, lambda step: (0, early(step), 0, 0)),
+            whole((6, D)),
+            pl.BlockSpec((1, 1, 3 * width), lambda step: (late(step), 0, 0)),
+            pl.BlockSpec((1, 1, hidden), lambda step: (early(step), 0, 0)),
+        ],
+        scratch_shapes=[
+            pltpu.VMEM((rows, D), jnp.float32),
+            pltpu.VMEM((rows, D), low),
+            pltpu.VMEM((D, rows), low),
+            pltpu.VMEM((D, rows), low),
+        ],
+        compiler_params=pltpu.CompilerParams(vmem_limit_bytes=56 << 20),
+    )(grad, x, mid, gains, weights, weights, weights, qkv, mixed, act, slope)
+
+
+MESH_SHAPE = (8, 4)
+ROW_HALVES = 2
+SMALL_WIDTH = 1024
+LAYER_BLOCKS = 3
+
+
+def hand_made():
+    return (lax.axis_size("dp"), lax.axis_size("tensor")) == MESH_SHAPE
+
+
+def device_rows_first(values):
+    return values.transpose((0, 3, 4, 5, 1, 2) + tuple(range(6, values.ndim)))
+
+
+def device_rows_last(values):
+    return values.transpose((0, 4, 5, 1, 2, 3) + tuple(range(6, values.ndim)))
+
+
+def gather_all(blocks, small, vectors):
+    parts, depth = lax.axis_size("tensor"), lax.axis_size("dp")
+    count, rows, columns = blocks.shape
+    if hand_made():
+        groups = (
+            (((1, (0,), (), 0), (2, (), (), 1)),)
+            + tuple(
+                tuple((0, (at,), (half,), half) for half in range(ROW_HALVES))
+                for at in range(count)
+            )
+            + (((1, (1,), (), 1),),)
+        )
+        halves = blocks.reshape(count, ROW_HALVES, rows // ROW_HALVES, columns)
+        padded = jnp.pad(vectors, (0, -vectors.size % 1024)).reshape(-1, 128)
+        wide, thin, lists = spread([halves, small, padded], groups, 1)
+        thin = device_rows_first(thin)
+        lists = lists[:, :, 0, 0, 0].reshape(parts, -1)[:, : vectors.size]
+    else:
+        both = ("dp", "tensor")
+        wide = lax.all_gather(blocks, both, axis=0, tiled=False)
+        wide = wide.reshape(depth, parts, count, rows, columns).transpose(2, 1, 0, 3, 4)
+        thin = lax.all_gather(small, both, axis=1, tiled=True)
+        lists = lax.all_gather(vectors, "tensor", axis=0, tiled=False)
+    return (
+        wide.reshape(count * parts, depth * rows, columns),
+        thin.reshape(small.shape[0], -1, small.shape[-1]),
+        lists,
+    )
+
+
+def sum_layer(attn_part, mlp_part):
+    parts, depth = lax.axis_size("tensor"), lax.axis_size("dp")
+    rows, columns = attn_part.shape[1] // depth, attn_part.shape[2]
+    if hand_made():
+        form = (2,) * len(DIMS) + (ROW_HALVES, rows // ROW_HALVES, columns)
+        groups = tuple(
+            tuple((1, (at,), (half,), half) for half in range(ROW_HALVES)) for at in range(2)
+        ) + (tuple((0, (), (half,), half) for half in range(ROW_HALVES)),)
+        attn_sum, mlp_sum = collect(
+            [attn_part.reshape(form), mlp_part.reshape((2,) + form)], groups, 2
+        )
+    else:
+        whole = jnp.concatenate([attn_part[None], mlp_part]).reshape(
+            LAYER_BLOCKS, parts, depth, rows, columns
+        )
+        whole = whole.transpose(2, 1, 0, 3, 4).reshape(-1, LAYER_BLOCKS, rows, columns)
+        total = lax.psum_scatter(
+            whole, ("dp", "tensor"), scatter_dimension=0, tiled=False
+        ).astype(jnp.float32)
+        attn_sum, mlp_sum = total[0], total[1:]
+    return attn_sum.reshape(rows, columns), mlp_sum.reshape(2, rows, columns)
+
+
+def sum_small(small):
+    devices = lax.axis_size("dp") * lax.axis_size("tensor")
+    rows = small.shape[1] // devices
+    if hand_made():
+        form = device_rows_last(small.reshape((2,) + (2,) * len(DIMS) + (rows, SMALL_WIDTH)))
+        groups = (tuple((0, (at,), (), at) for at in range(2)),)
+        return collect([form], groups, 3)[0]
+    blocks = small.reshape(2, devices, rows, -1).transpose(1, 0, 2, 3)
+    return lax.psum_scatter(
+        blocks, ("dp", "tensor"), scatter_dimension=0, tiled=False
+    ).astype(jnp.float32)
 
 
 def finish_step(weight, update, update_sq, weight_sq, entries):
@@ -92,59 +681,42 @@
     shared_vec, shared_sq, head_bias, head_bias_sq,
 ):
     both = ("dp", "tensor")
+    low = jnp.bfloat16
     tensor_width = lax.axis_size("tensor")
     dp_width = lax.axis_size("dp")
     tensor_rank = lax.axis_index("tensor")
     shard_rank = lax.axis_index("dp")
     images = patches.shape[0]
-    row_count = images * SEQ
     own_rows = attn_weight.shape[1]
     attn_width = attn_weight.shape[3]
     mlp_width = mlp_weight.shape[3]
-    heads = D // HEAD_DIM
-    score_scale = HEAD_DIM ** (-0.5)
-    head_shape = (images, SEQ, heads, HEAD_DIM)
-    key_valid = jnp.arange(SEQ) < TOK_IMG
     slot_index = tensor_rank * images + jnp.arange(images)
     image_total = jnp.sum(image_count).astype(jnp.float32)
     image_weight = (
         jnp.where(slot_index < image_count[shard_rank], 1.0, 0.0).astype(jnp.float32) / image_total
     )
 
-    low = jnp.bfloat16
-    small_full = gather_blocks(
-        jnp.concatenate([patch_weight, embed_table], axis=1).astype(low)[None]
-    ).reshape(D, D + EXTRA)
-    patch_full, table_full = small_full[:, :D], small_full[:, D:]
-    layers = []
-    for layer_idx in range(LAYERS):
-        attn_full = gather_blocks(
-            attn_weight[layer_idx].astype(low).reshape(1, own_rows, 4 * attn_width)
-        )
-        mlp_full = gather_blocks(mlp_weight[layer_idx].astype(low))
-        attn_full = (
-            attn_full.reshape(dp_width, tensor_width, own_rows, 4, attn_width)
-            .transpose(3, 0, 2, 1, 4)
-            .reshape(4, D, D)
-        )
-        mlp_full = mlp_full.transpose(2, 0, 3, 1, 4).reshape(2, D, FF)
-        layers.append((attn_full, mlp_full))
-    head_full = gather_blocks(head_weight.astype(low)[None]).reshape(D, CLASSES)
-    split_full, hidden_full = split_vec, hidden_bias
-    vectors = flatten_all([split_vec, hidden_bias])
-    vectors = lax.all_gather(vectors, "tensor", axis=0, tiled=False)
-    split_full = (
-        vectors[:, : split_vec.size]
-        .reshape(tensor_width, LAYERS, 2, attn_width)
-        .transpose(1, 2, 0, 3)
-        .reshape(LAYERS, 2, D)
-    )
-    hidden_full = (
-        vectors[:, split_vec.size :]
-        .reshape(tensor_width, LAYERS, mlp_width)
-        .transpose(1, 0, 2)
-        .reshape(LAYERS, FF)
-    )
+    blocks = jnp.concatenate(
+        [attn_weight.reshape(LAYERS, 1, own_rows, 4 * attn_width), mlp_weight], axis=1
+    ).astype(low)
+    widen = lambda values: jnp.pad(
+        values, ((0, 0), (0, SMALL_WIDTH - values.shape[1]))
+    )
+    small = jnp.stack(
+        [widen(jnp.concatenate([patch_weight, embed_table], axis=1)), widen(head_weight)]
+    ).astype(low)
+    weights, small_full, vectors = gather_all(
+        blocks.reshape(LAYERS * LAYER_BLOCKS, own_rows, mlp_width),
+        small,
+        flatten_all([split_vec, hidden_bias]),
+    )
+    patch_full, table_full = small_full[0, :, :D], small_full[0, :, D : D + EXTRA]
+    head_full = small_full[1, :, :CLASSES]
+    split_rows = vectors[:, : split_vec.size].reshape(tensor_width, LAYERS, 2, attn_width)
+    split_rows = jnp.stack(
+        [split_rows[:, :, 0], jnp.zeros_like(split_rows[:, :, 0]), split_rows[:, :, 1]], axis=2
+    ).reshape(tensor_width, LAYERS, 1, 3 * attn_width)
+    hidden_rows = vectors[:, split_vec.size :].reshape(tensor_width, LAYERS, 1, mlp_width)
 
     table_rows = table_full.astype(jnp.float32).T
     pixel_rows = patches.reshape(images * (TOK_IMG - 1), PATCH)
@@ -156,64 +728,21 @@
         [
             jnp.broadcast_to(table_rows[0], (images, 1, D)),
             embedded,
-            jnp.zeros((images, SEQ - TOK_IMG, D), jnp.float32),
+            jnp.zeros((images, PAD_ROWS - TOK_IMG, D), jnp.float32),
         ],
         axis=1,
-    ).reshape(row_count, D)
-
-    def attend(query_heads, key_heads):
-        scores = (
-            jnp.einsum(
-                "bqhd,bkhd->bhqk", query_heads, key_heads, preferred_element_type=jnp.float32
-            )
-            * score_scale
-        )
-        return jnp.where(key_valid, scores, -1e30)
+    ).reshape(images * PAD_ROWS, D)
 
     saved = []
     for layer_idx in range(LAYERS):
-        attn_full, mlp_full = layers[layer_idx]
         gains = shared_vec[6 * layer_idx : 6 * layer_idx + 6]
-        attn_input = residual
-        normed = layer_norm(residual, gains[0], gains[1]).astype(low)
-        query_rows = (
-            jnp.dot(normed, attn_full[0], preferred_element_type=jnp.float32)
-            + split_full[layer_idx, 0]
-        ).astype(low)
-        key_rows = jnp.dot(normed, attn_full[1], preferred_element_type=jnp.float32).astype(low)
-        value_rows = (
-            jnp.dot(normed, attn_full[2], preferred_element_type=jnp.float32)
-            + split_full[layer_idx, 1]
-        ).astype(low)
-        scores = attend(query_rows.reshape(head_shape), key_rows.reshape(head_shape))
-        log_total = jax.nn.logsumexp(scores, axis=-1, keepdims=True)
-        probs = jnp.exp(scores - log_total)
-        mixed = (
-            jnp.einsum(
-                "bhqk,bkhd->bqhd",
-                probs.astype(low),
-                value_rows.reshape(head_shape),
-                preferred_element_type=jnp.float32,
-            )
-            .astype(low)
-            .reshape(row_count, D)
+        layer_input = residual
+        residual, mid, qkv, mixed, act, slope = forward_layer(
+            layer_idx, images, residual, gains, weights,
+            split_rows[:, layer_idx], hidden_rows[:, layer_idx],
         )
-        residual = residual + times_transposed(mixed, attn_full[3]) + gains[2]
-        mlp_input = residual
-        mlp_normed = layer_norm(residual, gains[3], gains[4]).astype(low)
-        hidden_pre = (
-            jnp.dot(mlp_normed, mlp_full[0], preferred_element_type=jnp.float32)
-            + hidden_full[layer_idx]
-        )
-        hidden_act = jax.nn.gelu(hidden_pre, approximate=False).astype(low)
-        residual = residual + times_transposed(hidden_act, mlp_full[1]) + gains[5]
-        saved.append(
-            (
-                attn_input, normed, query_rows, key_rows, value_rows, log_total,
-                mixed, mlp_input, mlp_normed, hidden_pre, hidden_act,
-            )
-        )
-    cls_rows = residual.reshape(images, SEQ, D)[:, 0]
+        saved.append((layer_input, mid, gains, qkv, mixed, act, slope))
+    cls_rows = residual.reshape(images, PAD_ROWS, D)[:, 0]
     feature, final_back = jax.vjp(
         layer_norm, cls_rows, shared_vec[6 * LAYERS], shared_vec[6 * LAYERS + 1]
     )
@@ -232,115 +761,40 @@
     grad_feature = times_transposed(logits_low, head_full)
     grad_cls, grad_final_gain, grad_final_shift = final_back(grad_feature)
     grad_rows = jnp.concatenate(
-        [grad_cls[:, None], jnp.zeros((images, SEQ - 1, D), jnp.float32)], axis=1
-    ).reshape(row_count, D)
-    head_grad = scatter_blocks(
-        grad_head.astype(low).reshape(dp_width, tensor_width, 1, -1, CLASSES)
-    )[0].astype(jnp.float32)
+        [grad_cls[:, None], jnp.zeros((images, PAD_ROWS - 1, D), jnp.float32)], axis=1
+    ).reshape(images * PAD_ROWS, D)
     shared_list = [None] * LAYERS
     split_list = [None] * LAYERS
     hidden_list = [None] * LAYERS
     attn_list = [None] * LAYERS
     mlp_list = [None] * LAYERS
     for layer_idx in reversed(range(LAYERS)):
-        (
-            attn_input, normed, query_rows, key_rows, value_rows, log_total,
-            mixed, mlp_input, mlp_normed, hidden_pre, hidden_act,
-        ) = saved[layer_idx]
-        attn_full, mlp_full = layers[layer_idx]
-        gains = shared_vec[6 * layer_idx : 6 * layer_idx + 6]
-        grad_down_bias = jnp.sum(grad_rows, axis=0)
-        grad_out = grad_rows.astype(low)
-        grad_act = jnp.dot(grad_out, mlp_full[1], preferred_element_type=jnp.float32)
-        grad_down = outer_sum(grad_out, hidden_act)
-        _, gelu_back = jax.vjp(partial(jax.nn.gelu, approximate=False), hidden_pre)
-        grad_pre = gelu_back(grad_act)[0]
-        hidden_list[layer_idx] = jnp.sum(grad_pre, axis=0)
-        pre_low = grad_pre.astype(low)
-        grad_up = outer_sum(mlp_normed, pre_low)
-        mlp_blocks = (
-            jnp.stack([grad_up.astype(low), grad_down.astype(low)])
-            .reshape(2, dp_width, own_rows, tensor_width, mlp_width)
-            .transpose(1, 3, 0, 2, 4)
+        layer_input, mid, gains, qkv, mixed, act, slope = saved[layer_idx]
+        grad_rows, attn_part, mlp_part, shared_list[layer_idx], split_part, hidden_part = (
+            backward_layer(
+                layer_idx, images, grad_rows, layer_input, mid, gains, weights,
+                qkv, mixed, act, slope,
+            )
         )
-        mlp_list[layer_idx] = scatter_blocks(mlp_blocks).astype(jnp.float32)
-        grad_mlp_in = times_transposed(pre_low, mlp_full[0])
-        _, second_back = jax.vjp(layer_norm, mlp_input, gains[3], gains[4])
-        grad_mid, grad_gain_two, grad_shift_two = second_back(grad_mlp_in)
-        grad_rows = grad_rows + grad_mid
-        grad_out_bias = jnp.sum(grad_rows, axis=0)
-        grad_attn_out = grad_rows.astype(low)
-        grad_mixed = (
-            jnp.dot(grad_attn_out, attn_full[3], preferred_element_type=jnp.float32)
-            .astype(low)
-            .reshape(head_shape)
-        )
-        grad_out_proj = outer_sum(grad_attn_out, mixed)
-        query_heads = query_rows.reshape(head_shape)
-        key_heads = key_rows.reshape(head_shape)
-        value_heads = value_rows.reshape(head_shape)
-        probs = jnp.exp(attend(query_heads, key_heads) - log_total)
-        grad_probs = jnp.einsum(
-            "bqhd,bkhd->bhqk", grad_mixed, value_heads, preferred_element_type=jnp.float32
-        )
-        grad_value = jnp.einsum(
-            "bhqk,bqhd->bkhd", probs.astype(low), grad_mixed, preferred_element_type=jnp.float32
-        ).reshape(row_count, D)
-        inner_sum = jnp.sum(probs * grad_probs, axis=-1, keepdims=True)
-        grad_scores = (probs * (grad_probs - inner_sum) * score_scale).astype(low)
-        grad_query = jnp.einsum(
-            "bhqk,bkhd->bqhd", grad_scores, key_heads, preferred_element_type=jnp.float32
-        ).reshape(row_count, D)
-        grad_key = jnp.einsum(
-            "bhqk,bqhd->bkhd", grad_scores, query_heads, preferred_element_type=jnp.float32
-        ).reshape(row_count, D)
-        split_list[layer_idx] = jnp.stack([jnp.sum(grad_query, axis=0), jnp.sum(grad_value, axis=0)])
-        query_low, key_low, value_low = (
-            grad_query.astype(low), grad_key.astype(low), grad_value.astype(low)
-        )
-        attn_blocks = (
-            jnp.stack(
-                [
-                    outer_sum(normed, query_low).astype(low),
-                    outer_sum(normed, key_low).astype(low),
-                    outer_sum(normed, value_low).astype(low),
-                    grad_out_proj.astype(low),
-                ]
-            )
-            .reshape(4, dp_width, own_rows, tensor_width, attn_width)
-            .transpose(1, 3, 2, 0, 4)
-            .reshape(dp_width, tensor_width, 1, own_rows, 4 * attn_width)
-        )
-        attn_list[layer_idx] = (
-            scatter_blocks(attn_blocks).astype(jnp.float32).reshape(own_rows, 4, attn_width)
-        )
-        grad_attn_in = (
-            times_transposed(query_low, attn_full[0])
-            + times_transposed(key_low, attn_full[1])
-            + times_transposed(value_low, attn_full[2])
-        )
-        _, first_back = jax.vjp(layer_norm, attn_input, gains[0], gains[1])
-        grad_low, grad_gain_one, grad_shift_one = first_back(grad_attn_in)
-        grad_rows = grad_rows + grad_low
-        shared_list[layer_idx] = jnp.stack(
-            [
-                grad_gain_one, grad_shift_one, grad_out_bias,
-                grad_gain_two, grad_shift_two, grad_down_bias,
-            ]
-        )
-    grad_image = grad_rows.reshape(images, SEQ, D)
+        split_part = split_part.reshape(tensor_width, 3, attn_width)
+        split_list[layer_idx] = jnp.stack([split_part[:, 0], split_part[:, 2]], axis=1)
+        hidden_list[layer_idx] = hidden_part.reshape(tensor_width, mlp_width)
+        attn_sum, mlp_list[layer_idx] = sum_layer(attn_part, mlp_part)
+        attn_list[layer_idx] = attn_sum.reshape(own_rows, 4, attn_width)
+    grad_image = grad_rows.reshape(images, PAD_ROWS, D)
     grad_first = jnp.sum(grad_image[:, 0], axis=0)
     grad_position = jnp.sum(grad_image[:, 1:TOK_IMG], axis=0)
     grad_patch_bias = jnp.sum(grad_position, axis=0)
     embed_low = grad_image[:, 1:TOK_IMG].astype(low).reshape(images * (TOK_IMG - 1), D)
     grad_patch = outer_sum(pixel_rows, embed_low)
     grad_table = jnp.concatenate([grad_first[None], grad_position, grad_patch_bias[None]], axis=0).T
-    small_grad = scatter_blocks(
-        jnp.concatenate([grad_patch, grad_table], axis=1)
-        .astype(low)
-        .reshape(dp_width, tensor_width, 1, -1, D + EXTRA)
-    )[0].astype(jnp.float32)
-    patch_grad, table_grad = small_grad[:, :D], small_grad[:, D:]
+    small_sum = sum_small(
+        jnp.stack(
+            [widen(jnp.concatenate([grad_patch, grad_table], axis=1)), widen(grad_head)]
+        ).astype(low)
+    )
+    patch_grad, table_grad = small_sum[0, :, :D], small_sum[0, :, D : D + EXTRA]
+    head_grad = small_sum[1, :, :CLASSES]
     attn_grad = jnp.stack(attn_list)
     mlp_grad = jnp.stack(mlp_list)
     shared_grad = jnp.concatenate(
@@ -353,10 +807,11 @@
     head_sq = head_grad * head_grad
 
     split_sums, hidden_sums, shared_full, head_bias_full, loss_total = summed_over(
-        both, [jnp.stack(split_list), jnp.stack(hidden_list), shared_grad, grad_head_bias, loss_part]
-    )
-    split_total = lax.dynamic_slice_in_dim(split_sums, tensor_rank * attn_width, attn_width, 2)
-    hidden_total = lax.dynamic_slice_in_dim(hidden_sums, tensor_rank * mlp_width, mlp_width, 1)
+        both,
+        [jnp.stack(split_list, 1), jnp.stack(hidden_list, 1), shared_grad, grad_head_bias, loss_part],
+    )
+    split_total = lax.dynamic_index_in_dim(split_sums, tensor_rank, 0, keepdims=False)
+    hidden_total = lax.dynamic_index_in_dim(hidden_sums, tensor_rank, 0, keepdims=False)
     attn_row_full, mlp_row_full = summed_over(
         "tensor", [jnp.sum(attn_sq, axis=3).transpose(0, 2, 1), jnp.sum(mlp_sq, axis=3)]
     )

time: 2180 us -> 955 us (0.44)
  waiting for transfers between devices: 875 us -> 0.02 us
  Pallas kernels: 0 us -> 691 us
  local copies, waits for them, and re-layouts: 668 us -> 51 us
  matrix products: 304 us -> 6.4 us
  other arithmetic: 165 us -> 53.9 us
    pallas_call x0 -> x11, Pallas kernels: none -> 691 us  [the longest x4 287 us: collect(): pl.pallas_call(partial(collect_kernel, groups, len(arrays)), out_shape=[j...]
    reduce_scatter x8 -> x0, waiting for transfers between devices: 687 us -> none  [scatter_blocks(): lax.psum_scatter(flat, ('dp', 'tensor'), scatter_dimension=0, tiled=False)]
    another operation x48 -> x7, local copies, waits for them, and re-layouts: 232 us -> 3.5 us  [the longest x4 3.41 us: shards(): attn_grad = jnp.stack(attn_list)]
    dot_general x36 -> x0, matrix products: 195 us -> none  [the longest x3 47.6 us: shards(): jnp.dot(mlp_normed, mlp_full[0], preferred_element_type=jnp.float32)]
    all_gather x8 -> x0, waiting for transfers between devices: 187 us -> none  [gather_blocks(): full = lax.all_gather(blocks, ('dp', 'tensor'), axis=0, tiled=False)]
    slice x25 -> x7, local copies, waits for them, and re-layouts: 162 us -> 0.95 us  [the longest x1 0.89 us: shards(): gains = shared_vec[6 * layer_idx:6 * layer_idx + 6]]
    reshape x33 -> x7, local copies, waits for them, and re-layouts: 95.2 us -> 1.01 us  [the longest x1 0.52 us: shards(): attn_weight.reshape(LAYERS, 1, own_rows, 4 * attn_width)]
    transpose x6 -> x1, other arithmetic: 80.9 us -> 0.45 us  [device_rows_last(): return values.transpose((0, 4, 5, 1, 2, 3) + tuple(range(6, values.ndim)))]
  transfers between devices with their start and end apart: 17 -> 1, of which waited for: 12 -> 0; matrix products, arithmetic and copies ran while one was open for 39% -> 4% of each run, Pallas kernels for 0% -> 30%
where the time goes in v2:
time: 955 us; the launch traced here: 944 us
  Pallas kernels  691 us (72%)
  blocking collectives  120 us (13%)
  other arithmetic  53.9 us (6%)
  local copies, waits for them, and re-layouts  51 us (5%)
  between operations  21.7 us (2%)
    pallas_call x4, Pallas kernels, collect(): pl.pallas_call(partial(collect_kernel, groups, len(arrays)), out_shape=[j...  287 us
    pallas_call x1, Pallas kernels, spread(): pl.pallas_call(partial(spread_kernel, groups), out_shape=[jax.ShapeDtypeS...  217 us
    pallas_call x3, Pallas kernels, backward_layer(): pl.pallas_call(partial(backward_kernel, images, parts), grid=(2 * parts,)...  124 us
    psum x4, blocking collectives, summed_over(): lax.psum(flatten_all(arrays), axes)  120 us
    pallas_call x3, Pallas kernels, forward_layer(): pl.pallas_call(partial(forward_kernel, images, parts), grid=(2 * parts,),...  63.2 us
  transfers between devices with their start and end apart: 1, of which 0 were waited for; matrix products, arithmetic and copies ran while one was open for 4% of the time, Pallas kernels for 30%

profile of v2, /device:TPU:0, one launch (start us, length us, event | category | flops | bytes accessed | tf_op | source)
XLA Modules:
  0.0 944.3 jit_solution(16004884870305400099)
XLA Ops:
  10.5 1.4 multiply_reduce_fusion.17
  11.9 1.7 multiply_reduce_fusion.15
  13.7 1.6 multiply_reduce_fusion.11
  15.3 2.9 multiply_reduce_fusion.6
  19.7 216.7 %shard_map.442 = (bf16[9,2,2,2,2,2,2,48,768]{8,7,6,5,4,3,2,1,0:T(8,128)(2,1)}, bf16[2,2,2,2,2,2,24,1024]{7,6,5,4,3,2,1,0:T(8,128)(2,1)S(1)}, f32[2,2,2,2,2,32,128]{6,5,4,3,2,1,0:T(8,128)S(1)}) custom-call(bf16[9,2,48,768]{3,2,1,0:T(8,128)(2,1)S(1)} %bitcast.179, bf16[2,24,1024]{2,1,0:T(8,128)(2,1)S(1)} %pad_maximum_fusion.4.refs_1_, ...), custom_call_target="tpu_custom_call" | custom-call | tf_op jit(solution)/shard_map/pallas_call | solution.py:161
  237.3 1.4 slice.307
  240.7 2.0 copy.87
  242.7 2.0 reshape.577
  245.1 2.8 convolution_bitcast_fusion
  247.8 1.5 reshape.578
  249.9 20.6 %shard_map.443 = (f32[416,768]{1,0:T(8,128)S(1)}, f32[416,768]{1,0:T(8,128)S(1)}, bf16[4,416,576]{2,1,0:T(8,128)(2,1)}, bf16[4,416,192]{2,1,0:T(8,128)(2,1)S(1)}...) custom-call(f32[416,768]{1,0:T(8,128)S(1)} %bitcast.177, f32[6,768]{1,0:T(8,128)S(1)} %get-tuple-element.167.gain_ref, ...), custom_call_target="tpu_custom_call" | custom-call | tf_op jit(solution)/shard_map/pallas_call | solution.py:409
  270.6 21.4 %shard_map.444 = (f32[416,768]{1,0:T(8,128)S(1)}, f32[416,768]{1,0:T(8,128)S(1)}, bf16[4,416,576]{2,1,0:T(8,128)(2,1)}, bf16[4,416,192]{2,1,0:T(8,128)(2,1)S(1)}...) custom-call(f32[416,768]{1,0:T(8,128)S(1)} %get-tuple-element.72.x_ref, ...), custom_call_target="tpu_custom_call" | custom-call | tf_op jit(solution)/shard_map/pallas_call | solution.py:409
  292.9 21.2 %shard_map.445 = (f32[416,768]{1,0:T(8,128)S(1)}, f32[416,768]{1,0:T(8,128)S(1)}, bf16[4,416,576]{2,1,0:T(8,128)(2,1)}, bf16[4,416,192]{2,1,0:T(8,128)(2,1)S(1)}...) custom-call(f32[416,768]{1,0:T(8,128)S(1)} %get-tuple-element.73.x_ref, ...), custom_call_target="tpu_custom_call" | custom-call | tf_op jit(solution)/shard_map/pallas_call | solution.py:409
  321.3 41.7 %shard_map.446 = (f32[416,768]{1,0:T(8,128)}, bf16[4,768,768]{2,1,0:T(8,128)(2,1)}, bf16[2,4,768,768]{3,2,1,0:T(8,128)(2,1)}, f32[6,768]{1,0:T(8,128)}, f32[4,1,576]{2,1,0:T(1,128)}, /*index=5*/f32[4,1,768]{2,1,0:T(1,128)}) custom-call(f32[416,768]{1,0:T(8,128)} %bitcast.219, f32[416,768]{1,0:T(8,128)} %copy-done.2, f32[416,768]{1,0:T(8,128)} %copy-done.7, ...), custom_call_target="tpu_custom_call" | custom-call | tf_op jit(solution)/shard_map/pallas_call | solution.py:541
  363.9 41.4 %shard_map.447 = (f32[416,768]{1,0:T(8,128)}, bf16[4,768,768]{2,1,0:T(8,128)(2,1)}, bf16[2,4,768,768]{3,2,1,0:T(8,128)(2,1)}, f32[6,768]{1,0:T(8,128)}, f32[4,1,576]{2,1,0:T(1,128)}, /*index=5*/f32[4,1,768]{2,1,0:T(1,128)}) custom-call(f32[416,768]{1,0:T(8,128)} %get-tuple-element.80.grad_ref, f32[416,768]{1,0:T(8,128)} %copy-done.1, f32[416,768]{1,0:T(8,128)} %copy-done.6, ...), custom_call_target="tpu_custom_call" | custom-call | tf_op jit(solution)/shard_map/pallas_call | solution.py:541
  405.3 41.3 %shard_map.448 = (f32[416,768]{1,0:T(8,128)}, bf16[4,768,768]{2,1,0:T(8,128)(2,1)}, bf16[2,4,768,768]{3,2,1,0:T(8,128)(2,1)}, f32[6,768]{1,0:T(8,128)}, f32[4,1,576]{2,1,0:T(1,128)}, /*index=5*/f32[4,1,768]{2,1,0:T(1,128)}) custom-call(f32[416,768]{1,0:T(8,128)} %get-tuple-element.86.grad_ref, f32[416,768]{1,0:T(8,128)} %bitcast.178, f32[416,768]{1,0:T(8,128)} %copy-done.5, ...), custom_call_target="tpu_custom_call" | custom-call | tf_op jit(solution)/shard_map/pallas_call | solution.py:541
  449.7 1.4 concatenate.51
  454.6 1.8 fusion
  457.7 2.5 pad_maximum_fusion.2
  460.2 1.7 copy.110
  462.7 32.0 %shard_map.449 = f32[2,24,1024]{2,1,0:T(8,128)S(1)} custom-call(bf16[2,2,2,2,2,2,24,1024]{7,6,5,4,3,2,1,0:T(8,128)(2,1)S(1)} %copy_bitcast_fusion.refs_0_), custom_call_target="tpu_custom_call" | custom-call | tf_op jit(solution)/shard_map/pallas_call | solution.py:278
  496.9 85.0 %shard_map.452 = (f32[2,48,768]{2,1,0:T(8,128)S(1)}, f32[2,2,48,768]{3,2,1,0:T(8,128)S(1)}) custom-call(bf16[2,2,2,2,2,2,48,768]{7,6,5,4,3,2,1,0:T(8,128)(2,1)S(1)} %bitcast.191, bf16[2,2,2,2,2,2,2,48,768]{8,7,6,5,4,3,2,1,0:T(8,128)(2,1)} %bitcast.214), custom_call_target="tpu_custom_call" | custom-call | tf_op jit(solution)/shard_map/pallas_call | solution.py:278
  582.9 2.3 copy-done.4
  585.2 84.1 %shard_map.450 = (f32[2,48,768]{2,1,0:T(8,128)S(1)}, f32[2,2,48,768]{3,2,1,0:T(8,128)S(1)}) custom-call(bf16[2,2,2,2,2,2,48,768]{7,6,5,4,3,2,1,0:T(8,128)(2,1)S(1)} %bitcast.193, bf16[2,2,2,2,2,2,2,48,768]{8,7,6,5,4,3,2,1,0:T(8,128)(2,1)} %bitcast.216), custom_call_target="tpu_custom_call" | custom-call | tf_op jit(solution)/shard_map/pallas_call | solution.py:278
  669.7 2.3 copy-done.3
  672.0 85.9 %shard_map.451 = (f32[2,48,768]{2,1,0:T(8,128)S(1)}, f32[2,2,48,768]{3,2,1,0:T(8,128)S(1)}) custom-call(bf16[2,2,2,2,2,2,48,768]{7,6,5,4,3,2,1,0:T(8,128)(2,1)S(1)} %bitcast.192, bf16[2,2,2,2,2,2,2,48,768]{8,7,6,5,4,3,2,1,0:T(8,128)(2,1)} %bitcast.215), custom_call_target="tpu_custom_call" | custom-call | tf_op jit(solution)/shard_map/pallas_call | solution.py:278
  763.2 5.9 psum.37
  771.9 4.0 concatenate.54
  775.9 40.9 %psum.36 = f32[2026]{0:T(1024)S(1)} all-reduce(f32[2026]{0:T(1024)S(1)} %concatenate.54), channel_id=1, replica_groups=mesh['dp'=8,'tensor'=4] {'dp','tensor'}, use_global_device_ids=true, to_apply=%region_34.35 | all-reduce | flops 2026 | bytes 16208 | tf_op jit(solution)/shard_map/psum | solution.py:65
  817.7 36.6 %psum.38 = f32[6912]{0:T(1024)S(1)} all-reduce(f32[6912]{0:T(1024)S(1)} %pad_maximum_fusion.7), channel_id=1, replica_groups=mesh['dp'=8,'tensor'=4] {'dp'}, use_global_device_ids=true, to_apply=%region_40.41 | all-reduce | flops 6912 | bytes 55296 | tf_op jit(solution)/shard_map/psum | solution.py:65
  861.4 1.3 multiply_reduce_fusion.14
  862.7 1.4 multiply_reduce_fusion.10
  864.1 1.3 multiply_reduce_fusion.16
  868.5 2.0 concatenate.57
  870.5 36.8 %psum.39 = f32[39]{0:T(128)S(1)} all-reduce(f32[39]{0:T(128)S(1)} %concatenate.57), channel_id=1, replica_groups=mesh['dp'=8,'tensor'=4] {'dp','tensor'}, use_global_device_ids=true, to_apply=%region_50.51 | all-reduce | flops 39 | bytes 312 | tf_op jit(solution)/shard_map/psum | solution.py:65
  909.7 1.9 multiply_reduce_fusion.26
  913.2 1.6 multiply_reduce_fusion.12
  918.1 1.3 max.154
  919.4 1.3 max.156
  920.7 1.3 max.140
  922.0 3.0 divide_subtract_fusion.1
  925.4 1.7 divide_subtract_fusion
  927.1 1.3 divide_subtract_fusion.5
  928.5 1.4 divide_subtract_fusion.4
  929.9 1.4 divide_subtract_fusion.2
  932.0 1.4 divide_subtract_fusion.6
  933.4 1.4 divide_subtract_fusion.7
  936.0 1.3 divide_subtract_fusion.8
  (358 shorter events, 51.6 us)
Async XLA Ops:
  7.2 858.2 %all-reduce.8.cloned.1.call-start = ((), (), s32[]{:S(2)}) async-start(), calls=%async_computation | async-start | bytes 245760 | tf_op jit(solution)/shard_map/psum | solution.py:65
  9.0 240.9 %copy-start.11 = (f32[6,768]{1,0:T(8,128)}, f32[6,768]{1,0:T(8,128)S(1)}, u32[]{:S(2)}) copy-start(f32[6,768]{1,0:T(8,128)S(1)} %get-tuple-element.167.gain_ref) | copy-start | bytes 55300
  9.0 261.6 %copy-start.12 = (f32[6,768]{1,0:T(8,128)}, f32[6,768]{1,0:T(8,128)S(1)}, u32[]{:S(2)}) copy-start(f32[6,768]{1,0:T(8,128)S(1)} %get-tuple-element.166.gain_ref) | copy-start | bytes 55300
  9.0 283.9 %copy-start.13 = (f32[6,768]{1,0:T(8,128)}, f32[6,768]{1,0:T(8,128)S(1)}, u32[]{:S(2)}) copy-start(f32[6,768]{1,0:T(8,128)S(1)} %get-tuple-element.165.gain_ref) | copy-start | bytes 55300
  249.9 20.7 %copy-start = (f32[2,208,768]{2,1,0:T(8,128)}, f32[2,208,768]{2,1,0:T(8,128)S(1)}, u32[]{:S(2)}) copy-start(f32[2,208,768]{2,1,0:T(8,128)S(1)} %maximum_maximum_fusion) | copy-start | bytes 3833860
  270.6 21.4 %copy-start.1 = (f32[416,768]{1,0:T(8,128)}, f32[416,768]{1,0:T(8,128)S(1)}, u32[]{:S(2)}) copy-start(f32[416,768]{1,0:T(8,128)S(1)} %get-tuple-element.72.x_ref) | copy-start | bytes 3833860
  270.6 21.4 %copy-start.5 = (f32[416,768]{1,0:T(8,128)}, f32[416,768]{1,0:T(8,128)S(1)}, u32[]{:S(2)}) copy-start(f32[416,768]{1,0:T(8,128)S(1)} %get-tuple-element.87.mid_ref) | copy-start | bytes 3833860
  270.6 21.4 %copy-start.8 = (bf16[4,416,192]{2,1,0:T(8,128)(2,1)}, bf16[4,416,192]{2,1,0:T(8,128)(2,1)S(1)}, u32[]{:S(2)}) copy-start(bf16[4,416,192]{2,1,0:T(8,128)(2,1)S(1)} %get-tuple-element.89.mixed_ref) | copy-start | bytes 1916932
  292.9 21.2 %copy-start.2 = (f32[416,768]{1,0:T(8,128)}, f32[416,768]{1,0:T(8,128)S(1)}, u32[]{:S(2)}) copy-start(f32[416,768]{1,0:T(8,128)S(1)} %get-tuple-element.73.x_ref) | copy-start | bytes 3833860
  292.9 21.2 %copy-start.6 = (f32[416,768]{1,0:T(8,128)}, f32[416,768]{1,0:T(8,128)S(1)}, u32[]{:S(2)}) copy-start(f32[416,768]{1,0:T(8,128)S(1)} %get-tuple-element.81.mid_ref) | copy-start | bytes 3833860
  292.9 23.5 %copy-start.17 = (bf16[2,2,2,2,2,2,24,1024]{7,6,5,4,3,2,1,0:T(8,128)(2,1)S(1)}, bf16[2,2,2,2,2,2,24,1024]{7,6,5,4,3,2,1,0:T(8,128)(2,1)}, u32[]{:S(2)}) copy-start(bf16[2,2,2,2,2,2,24,1024]{7,6,5,4,3,2,1,0:T(8,128)(2,1)} %copy-done.16) | copy-start | bytes 9437188
  292.9 23.5 %copy-start.48 = (f32[1000]{0:T(1024)S(1)}, f32[1000]{0:T(1024)}, u32[]{:S(2)}) copy-start(f32[1000]{0:T(1024)} %param.51) | copy-start | bytes 12004
  405.2 42.3 %copy-start.56 = (f32[4,1,576]{2,1,0:T(1,128)S(1)}, f32[4,1,576]{2,1,0:T(1,128)}, u32[]{:S(2)}) copy-start(f32[4,1,576]{2,1,0:T(1,128)} %get-tuple-element.93) | copy-start | bytes 27652
  405.2 42.7 %copy-start.41 = (f32[6,768]{1,0:T(8,128)S(1)}, f32[6,768]{1,0:T(8,128)}, u32[]{:S(2)}) copy-start(f32[6,768]{1,0:T(8,128)} %get-tuple-element.100) | copy-start | bytes 55300
  405.3 42.7 %copy-start.42 = (f32[6,768]{1,0:T(8,128)S(1)}, f32[6,768]{1,0:T(8,128)}, u32[]{:S(2)}) copy-start(f32[6,768]{1,0:T(8,128)} %get-tuple-element.99) | copy-start | bytes 55300
  405.3 43.6 %copy-start.54 = (f32[4,1,768]{2,1,0:T(1,128)S(1)}, f32[4,1,768]{2,1,0:T(1,128)}, u32[]{:S(2)}) copy-start(f32[4,1,768]{2,1,0:T(1,128)} %get-tuple-element.97) | copy-start | bytes 36868
  405.3 43.6 %copy-start.55 = (f32[4,1,768]{2,1,0:T(1,128)S(1)}, f32[4,1,768]{2,1,0:T(1,128)}, u32[]{:S(2)}) copy-start(f32[4,1,768]{2,1,0:T(1,128)} %get-tuple-element.96) | copy-start | bytes 36868
  405.3 46.4 %copy-start.27 = (f32[3,768]{1,0:T(4,128)S(1)}, f32[3,768]{1,0:T(4,128)}, u32[]{:S(2)}) copy-start(f32[3,768]{1,0:T(4,128)} %param.47) | copy-start | bytes 27652
  405.3 47.0 %copy-start.20 = (f32[20,768]{1,0:T(8,128)S(1)}, f32[20,768]{1,0:T(8,128)}, u32[]{:S(2)}) copy-start(f32[20,768]{1,0:T(8,128)} %param.49) | copy-start | bytes 184324
  405.3 47.7 %copy-start.31 = (f32[3,2,192]{2,1,0:T(2,128)S(1)}, f32[3,2,192]{2,1,0:T(2,128)}, u32[]{:S(2)}) copy-start(f32[3,2,192]{2,1,0:T(2,128)} %param.45) | copy-start | bytes 13828
  462.3 34.6 %slice-start = ((s8[4718592]{0:T(1024)(128)(4,1)}), s8[4194304]{0:T(1024)(128)(4,1)S(1)}, s32[]{:S(2)}) async-start(s8[4718592]{0:T(1024)(128)(4,1)} %bitcast.189), calls=%async_computation.1 | async-start | bytes 8388608
  462.3 34.6 %slice-start.1 = ((s8[4718592]{0:T(1024)(128)(4,1)}), s8[524288]{0:T(1024)(128)(4,1)S(1)}, s32[]{:S(2)}) async-start(s8[4718592]{0:T(1024)(128)(4,1)} %bitcast.189), calls=%async_computation.2 | async-start | bytes 1048576
  760.0 10.0 %copy-start.83 = (f32[24]{0:T(128)S(1)}, f32[24]{0:T(128)}, u32[]{:S(2)}) copy-start(f32[24]{0:T(128)} %get-tuple-element.128) | copy-start | bytes 292
  760.1 10.0 %copy-start.91 = (f32[24]{0:T(128)S(1)}, f32[24]{0:T(128)}, u32[]{:S(2)}) copy-start(f32[24]{0:T(128)} %param.37) | copy-start | bytes 292
  760.1 10.6 %copy-start.84 = (f32[24]{0:T(128)S(1)}, f32[24]{0:T(128)}, u32[]{:S(2)}) copy-start(f32[24]{0:T(128)} %get-tuple-element.124) | copy-start | bytes 292
  760.1 10.6 %copy-start.85 = (f32[24]{0:T(128)S(1)}, f32[24]{0:T(128)}, u32[]{:S(2)}) copy-start(f32[24]{0:T(128)} %get-tuple-element.126) | copy-start | bytes 292
  760.1 11.8 %copy-start.50 = (f32[768]{0:T(1024)S(1)}, f32[768]{0:T(1024)}, u32[]{:S(2)}) copy-start(f32[768]{0:T(1024)} %get-tuple-element.129) | copy-start | bytes 9220
  760.1 11.8 %copy-start.51 = (f32[1000]{0:T(1024)S(1)}, f32[1000]{0:T(1024)}, u32[]{:S(2)}) copy-start(f32[1000]{0:T(1024)} %get-tuple-element.125) | copy-start | bytes 12004
  760.1 11.8 %copy-start.78 = (f32[198]{0:T(256)S(1)}, f32[198]{0:T(256)}, u32[]{:S(2)}) copy-start(f32[198]{0:T(256)} %get-tuple-element.127) | copy-start | bytes 2380
  761.3 93.8 %copy-start.90 = (f32[3]{0:T(128)S(1)}, f32[3]{0:T(128)}, u32[]{:S(2)}) copy-start(f32[3]{0:T(128)} %multiply_reduce_fusion.18) | copy-start | bytes 40
  761.3 93.8 %copy-start.87 = (f32[20]{0:T(128)S(1)}, f32[20]{0:T(128)}, u32[]{:S(2)}) copy-start(f32[20]{0:T(128)} %multiply_reduce_fusion.13) | copy-start | bytes 244
  761.3 94.4 %copy-start.64 = (f32[3,2]{1,0:T(4,128)S(1)}, f32[3,2]{1,0:T(4,128)}, u32[]{:S(2)}) copy-start(f32[3,2]{1,0:T(4,128)} %multiply_reduce_fusion.21) | copy-start | bytes 76
  761.3 94.5 %copy-start.86 = (f32[198]{0:T(256)S(1)}, f32[198]{0:T(256)}, u32[]{:S(2)}) copy-start(f32[198]{0:T(256)} %param.41) | copy-start | bytes 2380
  761.3 98.0 %copy-start.75 = (f32[768]{0:T(1024)S(1)}, f32[768]{0:T(1024)}, u32[]{:S(2)}) copy-start(f32[768]{0:T(1024)} %param.38) | copy-start | bytes 9220
  761.3 98.0 %copy-start.76 = (f32[1000]{0:T(1024)S(1)}, f32[1000]{0:T(1024)}, u32[]{:S(2)}) copy-start(f32[1000]{0:T(1024)} %param.44) | copy-start | bytes 12004
  761.3 98.2 %copy-start.46 = (f32[3,2,768]{2,1,0:T(2,128)S(1)}, f32[3,2,768]{2,1,0:T(2,128)}, u32[]{:S(2)}) copy-start(f32[3,2,768]{2,1,0:T(2,128)} %param.35) | copy-start | bytes 55300
  763.0 97.4 %copy-start.52 = (f32[3,4,192]{2,1,0:T(4,128)S(1)}, f32[3,4,192]{2,1,0:T(4,128)}, u32[]{:S(2)}) copy-start(f32[3,4,192]{2,1,0:T(4,128)} %param.32) | copy-start | bytes 27652
  769.7 91.5 %copy-start.40 = (f32[3,4,96]{2,1,0:T(4,128)}, f32[3,4,96]{2,1,0:T(4,128)S(1)}, u32[]{:S(2)}) copy-start(f32[3,4,96]{2,1,0:T(4,128)S(1)} %get-tuple-element.191) | copy-start | bytes 13828
  769.9 90.4 %copy-start.38 = (f32[3,2,96]{2,1,0:T(2,128)}, f32[3,2,96]{2,1,0:T(2,128)S(1)}, u32[]{:S(2)}) copy-start(f32[3,2,96]{2,1,0:T(2,128)S(1)} %get-tuple-element.193) | copy-start | bytes 6916
  770.6 90.7 %copy-start.69 = (f32[24]{0:T(128)}, f32[24]{0:T(128)S(1)}, u32[]{:S(2)}) copy-start(f32[24]{0:T(128)S(1)} %get-tuple-element.150) | copy-start | bytes 292
  771.9 90.8 %copy-start.71 = (f32[24]{0:T(128)}, f32[24]{0:T(128)S(1)}, u32[]{:S(2)}) copy-start(f32[24]{0:T(128)S(1)} %get-tuple-element.146) | copy-start | bytes 292
  771.9 92.1 %copy-start.73 = (f32[24]{0:T(128)}, f32[24]{0:T(128)S(1)}, u32[]{:S(2)}) copy-start(f32[24]{0:T(128)S(1)} %get-tuple-element.210) | copy-start | bytes 292
  859.6 65.5 %copy-start.25 = (f32[3,2,768]{2,1,0:T(2,128)}, f32[3,2,768]{2,1,0:T(2,128)S(1)}, u32[]{:S(2)}) copy-start(f32[3,2,768]{2,1,0:T(2,128)S(1)} %add_multiply_fusion.1) | copy-start | bytes 55300
  859.6 50.1 %copy-start.77 = (f32[1000]{0:T(1024)S(1)}, f32[1000]{0:T(1024)}, u32[]{:S(2)}) copy-start(f32[1000]{0:T(1024)} %param.52) | copy-start | bytes 12004
  860.5 64.6 %copy-start.26 = (f32[3,4,192]{2,1,0:T(4,128)}, f32[3,4,192]{2,1,0:T(4,128)S(1)}, u32[]{:S(2)}) copy-start(f32[3,4,192]{2,1,0:T(4,128)S(1)} %add_multiply_fusion.2) | copy-start | bytes 27652
  867.8 44.5 %copy-start.29 = (f32[4,3,768]{2,1,0:T(4,128)}, f32[4,3,768]{2,1,0:T(4,128)S(1)}, u32[]{:S(2)}) copy-start(f32[4,3,768]{2,1,0:T(4,128)S(1)} %reshape.620) | copy-start | bytes 110596
  925.4 10.6 %copy-start.47 = (f32[1000]{0:T(1024)S(1)}, f32[1000]{0:T(1024)}, u32[]{:S(2)}) copy-start(f32[1000]{0:T(1024)} %get-tuple-element.138) | copy-start | bytes 12004
  925.4 10.6 %copy-start.49 = (f32[1000]{0:T(1024)S(1)}, f32[1000]{0:T(1024)}, u32[]{:S(2)}) copy-start(f32[1000]{0:T(1024)} %param.51) | copy-start | bytes 12004
  (48 other events, 227.7 us)
Sparse Core Ops, SparseCore 0:
  451.2 126.8 all-reduce.7

commit v3 on v2

--- a/solution.py
+++ b/solution.py
@@ -68,8 +68,8 @@
 
 MESH = pl.DeviceIdType.MESH
 DIMS = ("y", "c", "zb", "za", "x")
-OUT_ORDERS = (("zb", "za", "x", "y", "c"), ("zb", "za", "y", "x", "c"))
-IN_ORDERS = (("c", "y", "x", "za", "zb"), ("c", "x", "y", "za", "zb"))
+OUT_ORDERS = (("zb", "x", "za", "y", "c"), ("zb", "y", "za", "x", "c"))
+IN_ORDERS = tuple(order[::-1] for order in OUT_ORDERS)
 
 
 def place_of_device():
@@ -662,6 +662,82 @@
     return lax.psum_scatter(
         blocks, ("dp", "tensor"), scatter_dimension=0, tiled=False
     ).astype(jnp.float32)
+
+
+def exchange_kernel(routes, *refs):
+    count = len(routes)
+    sources, totals = refs[:count], refs[count : 2 * count]
+    landed = refs[2 * count : 3 * count]
+    send_sem, recv_sem = refs[3 * count :]
+    place = place_of_device()
+    for source, total in zip(sources, totals):
+        total[...] = source[...]
+    meet_partners(place)
+    for stage in range(max(len(route) for route in routes)):
+        copies = []
+        for index, route in enumerate(routes):
+            if stage < len(route):
+                copies.append(
+                    (
+                        index,
+                        pltpu.make_async_remote_copy(
+                            src_ref=totals[index],
+                            dst_ref=landed[index].at[stage],
+                            send_sem=send_sem.at[index, stage],
+                            recv_sem=recv_sem.at[index, stage],
+                            device_id=partner_of(place, route[stage]),
+                            device_id_type=MESH,
+                        ),
+                    )
+                )
+        for _, copy in copies:
+            copy.start()
+        for index, copy in copies:
+            copy.wait()
+            totals[index][...] += landed[index][stage]
+
+
+def exchange(arrays, routes, collective_id):
+    depth = max(len(route) for route in routes)
+    return pl.pallas_call(
+        partial(exchange_kernel, routes),
+        out_shape=[jax.ShapeDtypeStruct(member.shape, member.dtype) for member in arrays],
+        in_specs=[pl.BlockSpec(memory_space=pltpu.VMEM)] * len(arrays),
+        out_specs=[pl.BlockSpec(memory_space=pltpu.VMEM)] * len(arrays),
+        scratch_shapes=[
+            pltpu.VMEM((len(route),) + member.shape, member.dtype)
+            for member, route in zip(arrays, routes)
+        ]
+        + [
+            pltpu.SemaphoreType.DMA((len(arrays), depth)),
+            pltpu.SemaphoreType.DMA((len(arrays), depth)),
+        ],
+        compiler_params=pltpu.CompilerParams(
+            collective_id=collective_id, has_side_effects=True, vmem_limit_bytes=16 << 20
+        ),
+    )(*arrays)
+
+
+ROUTES = {
+    "both": ("c", "y", "x", "za", "zb"),
+    "tensor": ("c", "y"),
+    "dp": ("x", "za", "zb"),
+}
+
+
+def sums_over(requests, collective_id):
+    if not hand_made():
+        names = {"both": ("dp", "tensor"), "tensor": "tensor", "dp": "dp"}
+        return [summed_over(names[axes], arrays) for axes, arrays in requests]
+    packed = []
+    for _, arrays in requests:
+        flat = flatten_all(arrays)
+        packed.append(jnp.pad(flat, (0, -flat.size % 1024)).reshape(-1, 128))
+    totals = exchange(packed, tuple(ROUTES[axes] for axes, _ in requests), collective_id)
+    return [
+        split_all(total.reshape(-1), [member.shape for member in arrays])
+        for total, (_, arrays) in zip(totals, requests)
+    ]
 
 
 def finish_step(weight, update, update_sq, weight_sq, entries):
@@ -812,47 +888,56 @@
     )
     split_total = lax.dynamic_index_in_dim(split_sums, tensor_rank, 0, keepdims=False)
     hidden_total = lax.dynamic_index_in_dim(hidden_sums, tensor_rank, 0, keepdims=False)
-    attn_row_full, mlp_row_full = summed_over(
-        "tensor", [jnp.sum(attn_sq, axis=3).transpose(0, 2, 1), jnp.sum(mlp_sq, axis=3)]
-    )
-    attn_col_full, mlp_col_full = summed_over("dp", [jnp.sum(attn_sq, axis=1), jnp.sum(mlp_sq, axis=2)])
+    patch_row_new = decay_rate * patch_rows + (1.0 - decay_rate) * (
+        jnp.sum(patch_sq, axis=1) / D + tiny_sq
+    )
+    table_row_new = decay_rate * embed_rows + (1.0 - decay_rate) * (
+        jnp.sum(table_sq, axis=1) / EXTRA + tiny_sq
+    )
+    head_row_new = decay_rate * head_rows + (1.0 - decay_rate) * (
+        jnp.sum(head_sq, axis=1) / CLASSES + tiny_sq
+    )
+    own_share = 1.0 / tensor_width
+    (
+        (
+            patch_col_full, table_col_full, head_col_full, whole_row_sum,
+            attn_old_sum, mlp_old_sum, attn_total, mlp_total, weight_sq_parts,
+        ),
+        (attn_row_full, mlp_row_full),
+        (attn_col_full, mlp_col_full),
+    ) = sums_over(
+        [
+            (
+                "both",
+                [
+                    jnp.sum(patch_sq, axis=0),
+                    jnp.sum(table_sq, axis=0),
+                    jnp.sum(head_sq, axis=0),
+                    jnp.stack(
+                        [jnp.sum(patch_row_new), jnp.sum(table_row_new), jnp.sum(head_row_new)]
+                    ),
+                    jnp.sum(attn_rows, axis=-1) * own_share,
+                    jnp.sum(mlp_rows, axis=-1) * own_share,
+                    jnp.sum(attn_sq, axis=(1, 3)),
+                    jnp.sum(mlp_sq, axis=(2, 3)),
+                    flatten_all(
+                        [
+                            jnp.sum(attn_weight * attn_weight, axis=(1, 3)),
+                            jnp.sum(mlp_weight * mlp_weight, axis=(2, 3)),
+                            jnp.sum(patch_weight * patch_weight),
+                            jnp.sum(embed_table * embed_table),
+                            jnp.sum(head_weight * head_weight),
+                        ]
+                    ),
+                ],
+            ),
+            ("tensor", [jnp.sum(attn_sq, axis=3).transpose(0, 2, 1), jnp.sum(mlp_sq, axis=3)]),
+            ("dp", [jnp.sum(attn_sq, axis=1), jnp.sum(mlp_sq, axis=2)]),
+        ],
+        4,
+    )
     attn_row_new = decay_rate * attn_rows + (1.0 - decay_rate) * (attn_row_full / D + tiny_sq)
     mlp_row_new = decay_rate * mlp_rows + (1.0 - decay_rate) * (mlp_row_full / FF + tiny_sq)
-    patch_row_new = decay_rate * patch_rows + (1.0 - decay_rate) * (
-        jnp.sum(patch_sq, axis=1) / D + tiny_sq
-    )
-    table_row_new = decay_rate * embed_rows + (1.0 - decay_rate) * (
-        jnp.sum(table_sq, axis=1) / EXTRA + tiny_sq
-    )
-    head_row_new = decay_rate * head_rows + (1.0 - decay_rate) * (
-        jnp.sum(head_sq, axis=1) / CLASSES + tiny_sq
-    )
-    own_share = 1.0 / tensor_width
-    (
-        patch_col_full, table_col_full, head_col_full, whole_row_sum,
-        attn_old_sum, mlp_old_sum, attn_total, mlp_total, weight_sq_parts,
-    ) = summed_over(
-        both,
-        [
-            jnp.sum(patch_sq, axis=0),
-            jnp.sum(table_sq, axis=0),
-            jnp.sum(head_sq, axis=0),
-            jnp.stack([jnp.sum(patch_row_new), jnp.sum(table_row_new), jnp.sum(head_row_new)]),
-            jnp.sum(attn_rows, axis=-1) * own_share,
-            jnp.sum(mlp_rows, axis=-1) * own_share,
-            jnp.sum(attn_sq, axis=(1, 3)),
-            jnp.sum(mlp_sq, axis=(2, 3)),
-            flatten_all(
-                [
-                    jnp.sum(attn_weight * attn_weight, axis=(1, 3)),
-                    jnp.sum(mlp_weight * mlp_weight, axis=(2, 3)),
-                    jnp.sum(patch_weight * patch_weight),
-                    jnp.sum(embed_table * embed_table),
-                    jnp.sum(head_weight * head_weight),
-                ]
-            ),
-        ],
-    )
     weight_sq = split_all(weight_sq_parts, [(LAYERS, 4), (LAYERS, 2), (), (), ()])
     attn_row_mean = (
         decay_rate * attn_old_sum + (1.0 - decay_rate) * (attn_total / D + D * tiny_sq)
@@ -902,10 +987,9 @@
     )
     head_bias_update = head_bias_full * lax.rsqrt(head_bias_sq_new)
     dp_share = 1.0 / dp_width
-    attn_u2, mlp_u2, patch_u2, table_u2, head_u2, split_u2, hidden_u2, split_w2, hidden_w2 = (
-        summed_over(
-            both,
-            [
+    ((attn_u2, mlp_u2, patch_u2, table_u2, head_u2, split_u2, hidden_u2, split_w2, hidden_w2),) = (
+        sums_over(
+            [("both", [
                 jnp.sum(attn_update * attn_update, axis=(1, 3)),
                 jnp.sum(mlp_update * mlp_update, axis=(2, 3)),
                 jnp.sum(patch_update * patch_update),
@@ -915,7 +999,8 @@
                 jnp.sum(hidden_update * hidden_update, axis=-1) * dp_share,
                 jnp.sum(split_vec * split_vec, axis=-1) * dp_share,
                 jnp.sum(hidden_bias * hidden_bias, axis=-1) * dp_share,
-            ],
+            ])],
+            5,
         )
     )
     vector_sq = [split_w2, hidden_w2]

time: 955 us -> 831 us (0.87)
  blocking collectives: 120 us -> 0 us
  Pallas kernels: 691 us -> 681 us
    psum x4 -> x0, blocking collectives: 120 us -> none  [summed_over(): lax.psum(flatten_all(arrays), axes)]
    pallas_call x0 -> x2, Pallas kernels: none -> 31 us  [exchange(): pl.pallas_call(partial(exchange_kernel, routes), out_shape=[jax.ShapeDtyp...]
    pallas_call x1, Pallas kernels: 217 us -> 186 us  [spread(): pl.pallas_call(partial(spread_kernel, groups), out_shape=[jax.ShapeDtypeS...]
    pallas_call x4, Pallas kernels: 287 us -> 277 us  [collect(): pl.pallas_call(partial(collect_kernel, groups, len(arrays)), out_shape=[j...]
  transfers between devices with their start and end apart: 1 -> 1, of which waited for: 0 -> 0; matrix products, arithmetic and copies ran while one was open for 4% -> 5% of each run, Pallas kernels for 30% -> 36%
where the time goes in v3:
time: 831 us; the launch traced here: 821 us
  Pallas kernels  681 us (82%)
  other arithmetic  56.6 us (7%)
  local copies, waits for them, and re-layouts  54.7 us (7%)
  between operations  22.1 us (3%)
    pallas_call x4, Pallas kernels, collect(): pl.pallas_call(partial(collect_kernel, groups, len(arrays)), out_shape=[j...  277 us
    pallas_call x1, Pallas kernels, spread(): pl.pallas_call(partial(spread_kernel, groups), out_shape=[jax.ShapeDtypeS...  186 us
    pallas_call x3, Pallas kernels, backward_layer(): pl.pallas_call(partial(backward_kernel, images, parts), grid=(2 * parts,)...  124 us
    pallas_call x3, Pallas kernels, forward_layer(): pl.pallas_call(partial(forward_kernel, images, parts), grid=(2 * parts,),...  63.2 us
    pallas_call x2, Pallas kernels, exchange(): pl.pallas_call(partial(exchange_kernel, routes), out_shape=[jax.ShapeDtyp...  31 us
  transfers between devices with their start and end apart: 1, of which 0 were waited for; matrix products, arithmetic and copies ran while one was open for 5% of the time, Pallas kernels for 36%

profile of v3, /device:TPU:0, one launch (start us, length us, event | category | flops | bytes accessed | tf_op | source)
XLA Modules:
  0.0 821.0 jit_solution(11060152889341092473)
XLA Ops:
  10.5 1.4 multiply_reduce_fusion.17
  11.9 1.7 multiply_reduce_fusion.15
  13.6 1.6 multiply_reduce_fusion.11
  15.2 2.9 multiply_reduce_fusion.6
  19.6 186.0 %shard_map.442 = (bf16[9,2,2,2,2,2,2,48,768]{8,7,6,5,4,3,2,1,0:T(8,128)(2,1)}, bf16[2,2,2,2,2,2,24,1024]{7,6,5,4,3,2,1,0:T(8,128)(2,1)S(1)}, f32[2,2,2,2,2,32,128]{6,5,4,3,2,1,0:T(8,128)S(1)}) custom-call(bf16[9,2,48,768]{3,2,1,0:T(8,128)(2,1)S(1)} %bitcast.194, bf16[2,24,1024]{2,1,0:T(8,128)(2,1)S(1)} %pad_maximum_fusion.4.refs_1_, ...), custom_call_target="tpu_custom_call" | custom-call | tf_op jit(solution)/shard_map/pallas_call | solution.py:161
  206.5 1.4 slice.304
  210.0 2.0 copy.87
  211.9 2.0 reshape.561
  214.3 2.7 convolution_bitcast_fusion
  217.1 1.5 reshape.562
  219.2 20.6 %shard_map.443 = (f32[416,768]{1,0:T(8,128)S(1)}, f32[416,768]{1,0:T(8,128)S(1)}, bf16[4,416,576]{2,1,0:T(8,128)(2,1)}, bf16[4,416,192]{2,1,0:T(8,128)(2,1)S(1)}...) custom-call(f32[416,768]{1,0:T(8,128)S(1)} %bitcast.192, f32[6,768]{1,0:T(8,128)S(1)} %get-tuple-element.175.gain_ref, ...), custom_call_target="tpu_custom_call" | custom-call | tf_op jit(solution)/shard_map/pallas_call | solution.py:409
  239.8 21.4 %shard_map.444 = (f32[416,768]{1,0:T(8,128)S(1)}, f32[416,768]{1,0:T(8,128)S(1)}, bf16[4,416,576]{2,1,0:T(8,128)(2,1)}, bf16[4,416,192]{2,1,0:T(8,128)(2,1)S(1)}...) custom-call(f32[416,768]{1,0:T(8,128)S(1)} %get-tuple-element.75.x_ref, ...), custom_call_target="tpu_custom_call" | custom-call | tf_op jit(solution)/shard_map/pallas_call | solution.py:409
  262.2 21.1 %shard_map.445 = (f32[416,768]{1,0:T(8,128)S(1)}, f32[416,768]{1,0:T(8,128)S(1)}, bf16[4,416,576]{2,1,0:T(8,128)(2,1)}, bf16[4,416,192]{2,1,0:T(8,128)(2,1)S(1)}...) custom-call(f32[416,768]{1,0:T(8,128)S(1)} %get-tuple-element.76.x_ref, ...), custom_call_target="tpu_custom_call" | custom-call | tf_op jit(solution)/shard_map/pallas_call | solution.py:409
  288.2 1.3 multiply_reduce_fusion.28
  289.5 1.1 concatenate.49.clone
  290.6 41.6 %shard_map.446 = (f32[416,768]{1,0:T(8,128)}, bf16[4,768,768]{2,1,0:T(8,128)(2,1)}, bf16[2,4,768,768]{3,2,1,0:T(8,128)(2,1)}, f32[6,768]{1,0:T(8,128)}, f32[4,1,576]{2,1,0:T(1,128)}, /*index=5*/f32[4,1,768]{2,1,0:T(1,128)}) custom-call(f32[416,768]{1,0:T(8,128)} %bitcast.242, f32[416,768]{1,0:T(8,128)} %copy-done.2, f32[416,768]{1,0:T(8,128)} %copy-done.8, ...), custom_call_target="tpu_custom_call" | custom-call | tf_op jit(solution)/shard_map/pallas_call | solution.py:541
  333.0 41.4 %shard_map.447 = (f32[416,768]{1,0:T(8,128)}, bf16[4,768,768]{2,1,0:T(8,128)(2,1)}, bf16[2,4,768,768]{3,2,1,0:T(8,128)(2,1)}, f32[6,768]{1,0:T(8,128)}, f32[4,1,576]{2,1,0:T(1,128)}, /*index=5*/f32[4,1,768]{2,1,0:T(1,128)}) custom-call(f32[416,768]{1,0:T(8,128)} %get-tuple-element.83.grad_ref, f32[416,768]{1,0:T(8,128)} %copy-done.1, f32[416,768]{1,0:T(8,128)} %copy-done.7, ...), custom_call_target="tpu_custom_call" | custom-call | tf_op jit(solution)/shard_map/pallas_call | solution.py:541
  374.4 41.3 %shard_map.448 = (f32[416,768]{1,0:T(8,128)}, bf16[4,768,768]{2,1,0:T(8,128)(2,1)}, bf16[2,4,768,768]{3,2,1,0:T(8,128)(2,1)}, f32[6,768]{1,0:T(8,128)}, f32[4,1,576]{2,1,0:T(1,128)}, /*index=5*/f32[4,1,768]{2,1,0:T(1,128)}) custom-call(f32[416,768]{1,0:T(8,128)} %get-tuple-element.89.grad_ref, f32[416,768]{1,0:T(8,128)} %bitcast.193, f32[416,768]{1,0:T(8,128)} %copy-done.6, ...), custom_call_target="tpu_custom_call" | custom-call | tf_op jit(solution)/shard_map/pallas_call | solution.py:541
  418.8 1.4 concatenate.51
  423.7 1.8 fusion
  426.7 2.5 pad_maximum_fusion.2
  429.2 1.7 copy.110
  431.7 37.8 %shard_map.449 = f32[2,24,1024]{2,1,0:T(8,128)S(1)} custom-call(bf16[2,2,2,2,2,2,24,1024]{7,6,5,4,3,2,1,0:T(8,128)(2,1)S(1)} %copy_bitcast_fusion.refs_0_), custom_call_target="tpu_custom_call" | custom-call | tf_op jit(solution)/shard_map/pallas_call | solution.py:278
  474.3 2.3 copy-done.3
  476.6 80.8 %shard_map.452 = (f32[2,48,768]{2,1,0:T(8,128)S(1)}, f32[2,2,48,768]{3,2,1,0:T(8,128)S(1)}) custom-call(bf16[2,2,2,2,2,2,48,768]{7,6,5,4,3,2,1,0:T(8,128)(2,1)S(1)} %bitcast.204, bf16[2,2,2,2,2,2,2,48,768]{8,7,6,5,4,3,2,1,0:T(8,128)(2,1)} %bitcast.237), custom_call_target="tpu_custom_call" | custom-call | tf_op jit(solution)/shard_map/pallas_call | solution.py:278
  558.5 2.3 copy-done.5
  560.8 78.9 %shard_map.450 = (f32[2,48,768]{2,1,0:T(8,128)S(1)}, f32[2,2,48,768]{3,2,1,0:T(8,128)S(1)}) custom-call(bf16[2,2,2,2,2,2,48,768]{7,6,5,4,3,2,1,0:T(8,128)(2,1)S(1)} %bitcast.206, bf16[2,2,2,2,2,2,2,48,768]{8,7,6,5,4,3,2,1,0:T(8,128)(2,1)} %bitcast.239), custom_call_target="tpu_custom_call" | custom-call | tf_op jit(solution)/shard_map/pallas_call | solution.py:278
  640.1 2.3 copy-done.4
  642.4 79.0 %shard_map.451 = (f32[2,48,768]{2,1,0:T(8,128)S(1)}, f32[2,2,48,768]{3,2,1,0:T(8,128)S(1)}) custom-call(bf16[2,2,2,2,2,2,48,768]{7,6,5,4,3,2,1,0:T(8,128)(2,1)S(1)} %bitcast.205, bf16[2,2,2,2,2,2,2,48,768]{8,7,6,5,4,3,2,1,0:T(8,128)(2,1)} %bitcast.238), custom_call_target="tpu_custom_call" | custom-call | tf_op jit(solution)/shard_map/pallas_call | solution.py:278
  725.1 1.2 constant_dynamic-update-slice_fusion.1
  729.5 4.0 concatenate.54
  733.6 16.9 %shard_map.453 = (f32[16,128]{1,0:T(8,128)S(1)}, f32[16,128]{1,0:T(8,128)S(1)}, f32[56,128]{1,0:T(8,128)S(1)}) custom-call(f32[16,128]{1,0:T(8,128)S(1)} %pad_bitcast_fusion.1.refs_0_, f32[16,128]{1,0:T(8,128)S(1)} %fusion.21.refs_1_, f32[56,128]{1,0:T(8,128)S(1)} %fusion.12.refs_2_), custom_call_target="tpu_custom_call" | custom-call | tf_op jit(solution)/shard_map/pallas_call | solution.py:702
  759.1 1.4 multiply_reduce_fusion.10
  760.4 1.3 multiply_reduce_fusion.14
  761.8 1.3 multiply_reduce_fusion.16
  766.2 2.0 concatenate.57
  768.2 14.2 %shard_map.454 = f32[8,128]{1,0:T(8,128)S(1)} custom-call(f32[8,128]{1,0:T(8,128)S(1)} %pad_bitcast_fusion.2.refs_0_), custom_call_target="tpu_custom_call" | custom-call | tf_op jit(solution)/shard_map/pallas_call | solution.py:702
  786.0 1.9 multiply_reduce_fusion.26
  789.5 1.6 multiply_reduce_fusion.12
  796.0 2.1 divide_subtract_fusion.5
  798.1 2.3 divide_subtract_fusion.4
  800.4 2.3 divide_subtract_fusion.2
  802.6 3.1 divide_subtract_fusion.1
  805.9 1.7 divide_subtract_fusion
  808.3 1.4 divide_subtract_fusion.6
  809.7 1.4 divide_subtract_fusion.7
  811.1 1.3 slice.324
  812.4 1.3 divide_subtract_fusion.8
  (347 shorter events, 52.4 us)
Async XLA Ops:
  7.2 755.9 %all-reduce.12.cloned.1.call-start = ((), (), s32[]{:S(2)}) async-start(), calls=%async_computation | async-start | bytes 245760 | tf_op jit(solution)/shard_map/psum | solution.py:65
  9.0 210.2 %copy-start.12 = (f32[6,768]{1,0:T(8,128)}, f32[6,768]{1,0:T(8,128)S(1)}, u32[]{:S(2)}) copy-start(f32[6,768]{1,0:T(8,128)S(1)} %get-tuple-element.175.gain_ref) | copy-start | bytes 55300
  9.0 230.8 %copy-start.13 = (f32[6,768]{1,0:T(8,128)}, f32[6,768]{1,0:T(8,128)S(1)}, u32[]{:S(2)}) copy-start(f32[6,768]{1,0:T(8,128)S(1)} %get-tuple-element.174.gain_ref) | copy-start | bytes 55300
  9.0 253.2 %copy-start.14 = (f32[6,768]{1,0:T(8,128)}, f32[6,768]{1,0:T(8,128)S(1)}, u32[]{:S(2)}) copy-start(f32[6,768]{1,0:T(8,128)S(1)} %get-tuple-element.173.gain_ref) | copy-start | bytes 55300
  206.0 8.3 %copy-start.17 = (bf16[2,2,2,2,2,2,24,1024]{7,6,5,4,3,2,1,0:T(8,128)(2,1)}, bf16[2,2,2,2,2,2,24,1024]{7,6,5,4,3,2,1,0:T(8,128)(2,1)S(1)}, u32[]{:S(2)}) copy-start(bf16[2,2,2,2,2,2,24,1024]{7,6,5,4,3,2,1,0:T(8,128)(2,1)S(1)} %copy.86) | copy-start | bytes 9437188
  219.1 20.7 %copy-start = (f32[2,208,768]{2,1,0:T(8,128)}, f32[2,208,768]{2,1,0:T(8,128)S(1)}, u32[]{:S(2)}) copy-start(f32[2,208,768]{2,1,0:T(8,128)S(1)} %maximum_maximum_fusion) | copy-start | bytes 3833860
  239.8 21.4 %copy-start.1 = (f32[416,768]{1,0:T(8,128)}, f32[416,768]{1,0:T(8,128)S(1)}, u32[]{:S(2)}) copy-start(f32[416,768]{1,0:T(8,128)S(1)} %get-tuple-element.75.x_ref) | copy-start | bytes 3833860
  239.8 21.4 %copy-start.6 = (f32[416,768]{1,0:T(8,128)}, f32[416,768]{1,0:T(8,128)S(1)}, u32[]{:S(2)}) copy-start(f32[416,768]{1,0:T(8,128)S(1)} %get-tuple-element.90.mid_ref) | copy-start | bytes 3833860
  239.8 21.4 %copy-start.9 = (bf16[4,416,192]{2,1,0:T(8,128)(2,1)}, bf16[4,416,192]{2,1,0:T(8,128)(2,1)S(1)}, u32[]{:S(2)}) copy-start(bf16[4,416,192]{2,1,0:T(8,128)(2,1)S(1)} %get-tuple-element.92.mixed_ref) | copy-start | bytes 1916932
  262.2 21.2 %copy-start.2 = (f32[416,768]{1,0:T(8,128)}, f32[416,768]{1,0:T(8,128)S(1)}, u32[]{:S(2)}) copy-start(f32[416,768]{1,0:T(8,128)S(1)} %get-tuple-element.76.x_ref) | copy-start | bytes 3833860
  262.2 21.2 %copy-start.7 = (f32[416,768]{1,0:T(8,128)}, f32[416,768]{1,0:T(8,128)S(1)}, u32[]{:S(2)}) copy-start(f32[416,768]{1,0:T(8,128)S(1)} %get-tuple-element.84.mid_ref) | copy-start | bytes 3833860
  262.2 23.5 %copy-start.18 = (bf16[2,2,2,2,2,2,24,1024]{7,6,5,4,3,2,1,0:T(8,128)(2,1)S(1)}, bf16[2,2,2,2,2,2,24,1024]{7,6,5,4,3,2,1,0:T(8,128)(2,1)}, u32[]{:S(2)}) copy-start(bf16[2,2,2,2,2,2,24,1024]{7,6,5,4,3,2,1,0:T(8,128)(2,1)} %copy-done.17) | copy-start | bytes 9437188
  262.2 23.5 %copy-start.45 = (f32[1000]{0:T(1024)S(1)}, f32[1000]{0:T(1024)}, u32[]{:S(2)}) copy-start(f32[1000]{0:T(1024)} %param.51) | copy-start | bytes 12004
  374.4 42.3 %copy-start.55 = (f32[4,1,576]{2,1,0:T(1,128)S(1)}, f32[4,1,576]{2,1,0:T(1,128)}, u32[]{:S(2)}) copy-start(f32[4,1,576]{2,1,0:T(1,128)} %get-tuple-element.96) | copy-start | bytes 27652
  374.4 42.7 %copy-start.37 = (f32[6,768]{1,0:T(8,128)S(1)}, f32[6,768]{1,0:T(8,128)}, u32[]{:S(2)}) copy-start(f32[6,768]{1,0:T(8,128)} %get-tuple-element.103) | copy-start | bytes 55300
  374.4 42.7 %copy-start.38 = (f32[6,768]{1,0:T(8,128)S(1)}, f32[6,768]{1,0:T(8,128)}, u32[]{:S(2)}) copy-start(f32[6,768]{1,0:T(8,128)} %get-tuple-element.102) | copy-start | bytes 55300
  374.4 43.6 %copy-start.53 = (f32[4,1,768]{2,1,0:T(1,128)S(1)}, f32[4,1,768]{2,1,0:T(1,128)}, u32[]{:S(2)}) copy-start(f32[4,1,768]{2,1,0:T(1,128)} %get-tuple-element.100) | copy-start | bytes 36868
  374.4 43.6 %copy-start.54 = (f32[4,1,768]{2,1,0:T(1,128)S(1)}, f32[4,1,768]{2,1,0:T(1,128)}, u32[]{:S(2)}) copy-start(f32[4,1,768]{2,1,0:T(1,128)} %get-tuple-element.99) | copy-start | bytes 36868
  374.4 46.4 %copy-start.26 = (f32[3,768]{1,0:T(4,128)S(1)}, f32[3,768]{1,0:T(4,128)}, u32[]{:S(2)}) copy-start(f32[3,768]{1,0:T(4,128)} %param.47) | copy-start | bytes 27652
  374.4 47.0 %copy-start.21 = (f32[20,768]{1,0:T(8,128)S(1)}, f32[20,768]{1,0:T(8,128)}, u32[]{:S(2)}) copy-start(f32[20,768]{1,0:T(8,128)} %param.49) | copy-start | bytes 184324
  374.4 47.7 %copy-start.29 = (f32[3,2,192]{2,1,0:T(2,128)S(1)}, f32[3,2,192]{2,1,0:T(2,128)}, u32[]{:S(2)}) copy-start(f32[3,2,192]{2,1,0:T(2,128)} %param.45) | copy-start | bytes 13828
  415.8 7.7 copy-start.20
  431.7 40.0 %copy-start.40 = (f32[3,4,96]{2,1,0:T(4,128)S(1)}, f32[3,4,96]{2,1,0:T(4,128)}, u32[]{:S(2)}) copy-start(f32[3,4,96]{2,1,0:T(4,128)} %param.31) | copy-start | bytes 13828
  431.7 40.7 %copy-start.51 = (f32[3,2,96]{2,1,0:T(2,128)S(1)}, f32[3,2,96]{2,1,0:T(2,128)}, u32[]{:S(2)}) copy-start(f32[3,2,96]{2,1,0:T(2,128)} %param.34) | copy-start | bytes 6916
  431.7 41.4 %copy-start.60 = (f32[3,4]{1,0:T(4,128)S(1)}, f32[3,4]{1,0:T(4,128)}, u32[]{:S(2)}) copy-start(f32[3,4]{1,0:T(4,128)} %get-tuple-element.165) | copy-start | bytes 148
  431.7 42.0 %copy-start.57 = (f32[3,2]{1,0:T(4,128)S(1)}, f32[3,2]{1,0:T(4,128)}, u32[]{:S(2)}) copy-start(f32[3,2]{1,0:T(4,128)} %get-tuple-element.161) | copy-start | bytes 76
  725.0 27.1 %copy-start.84 = (f32[3]{0:T(128)S(1)}, f32[3]{0:T(128)}, u32[]{:S(2)}) copy-start(f32[3]{0:T(128)} %multiply_reduce_fusion.18) | copy-start | bytes 40
  725.0 27.1 %copy-start.82 = (f32[20]{0:T(128)S(1)}, f32[20]{0:T(128)}, u32[]{:S(2)}) copy-start(f32[20]{0:T(128)} %multiply_reduce_fusion.13) | copy-start | bytes 244
  725.0 27.6 %copy-start.59 = (f32[3,2]{1,0:T(4,128)S(1)}, f32[3,2]{1,0:T(4,128)}, u32[]{:S(2)}) copy-start(f32[3,2]{1,0:T(4,128)} %multiply_reduce_fusion.21) | copy-start | bytes 76
  725.0 27.7 %copy-start.80 = (f32[198]{0:T(256)S(1)}, f32[198]{0:T(256)}, u32[]{:S(2)}) copy-start(f32[198]{0:T(256)} %param.41) | copy-start | bytes 2380
  725.0 31.8 %copy-start.65 = (f32[1000]{0:T(1024)S(1)}, f32[1000]{0:T(1024)}, u32[]{:S(2)}) copy-start(f32[1000]{0:T(1024)} %param.44) | copy-start | bytes 12004
  725.0 31.9 %copy-start.66 = (f32[768]{0:T(1024)S(1)}, f32[768]{0:T(1024)}, u32[]{:S(2)}) copy-start(f32[768]{0:T(1024)} %param.38) | copy-start | bytes 9220
  725.0 32.0 %copy-start.52 = (f32[3,2,96]{2,1,0:T(2,128)S(1)}, f32[3,2,96]{2,1,0:T(2,128)}, u32[]{:S(2)}) copy-start(f32[3,2,96]{2,1,0:T(2,128)} %param.34) | copy-start | bytes 6916
  726.2 30.9 %copy-start.41 = (f32[3,4,96]{2,1,0:T(4,128)S(1)}, f32[3,4,96]{2,1,0:T(4,128)}, u32[]{:S(2)}) copy-start(f32[3,4,96]{2,1,0:T(4,128)} %param.31) | copy-start | bytes 13828
  726.2 31.0 %copy-start.43 = (f32[3,2,768]{2,1,0:T(2,128)S(1)}, f32[3,2,768]{2,1,0:T(2,128)}, u32[]{:S(2)}) copy-start(f32[3,2,768]{2,1,0:T(2,128)} %param.35) | copy-start | bytes 55300
  727.9 30.2 %copy-start.49 = (f32[3,4,192]{2,1,0:T(4,128)S(1)}, f32[3,4,192]{2,1,0:T(4,128)}, u32[]{:S(2)}) copy-start(f32[3,4,192]{2,1,0:T(4,128)} %param.32) | copy-start | bytes 27652
  728.8 31.6 %copy-start.62 = (f32[24]{0:T(128)}, f32[24]{0:T(128)S(1)}, u32[]{:S(2)}) copy-start(f32[24]{0:T(128)S(1)} %get-tuple-element.156) | copy-start | bytes 292
  729.4 29.6 %copy-start.63 = (f32[24]{0:T(128)}, f32[24]{0:T(128)S(1)}, u32[]{:S(2)}) copy-start(f32[24]{0:T(128)S(1)} %get-tuple-element.152) | copy-start | bytes 292
  729.4 32.3 %copy-start.64 = (f32[24]{0:T(128)}, f32[24]{0:T(128)S(1)}, u32[]{:S(2)}) copy-start(f32[24]{0:T(128)S(1)} %get-tuple-element.211) | copy-start | bytes 292
  752.7 9.1 %copy-start.56 = (f32[198]{0:T(256)}, f32[198]{0:T(256)S(1)}, u32[]{:S(2)}) copy-start(f32[198]{0:T(256)S(1)} %fusion.46) | copy-start | bytes 2380
  756.9 43.4 %copy-start.33 = (f32[1000]{0:T(1024)}, f32[1000]{0:T(1024)S(1)}, u32[]{:S(2)}) copy-start(f32[1000]{0:T(1024)S(1)} %fusion.27) | copy-start | bytes 12004
  756.9 41.2 %copy-start.34 = (f32[768]{0:T(1024)}, f32[768]{0:T(1024)S(1)}, u32[]{:S(2)}) copy-start(f32[768]{0:T(1024)S(1)} %fusion.29) | copy-start | bytes 9220
  757.1 48.7 %copy-start.35 = (f32[3,2,96]{2,1,0:T(2,128)}, f32[3,2,96]{2,1,0:T(2,128)S(1)}, u32[]{:S(2)}) copy-start(f32[3,2,96]{2,1,0:T(2,128)S(1)} %add_multiply_fusion.5) | copy-start | bytes 6916
  757.3 48.4 %copy-start.24 = (f32[3,2,768]{2,1,0:T(2,128)}, f32[3,2,768]{2,1,0:T(2,128)S(1)}, u32[]{:S(2)}) copy-start(f32[3,2,768]{2,1,0:T(2,128)S(1)} %add_multiply_fusion.1) | copy-start | bytes 55300
  757.3 8.1 copy-start.50
  757.9 28.1 %copy-start.67 = (f32[1000]{0:T(1024)S(1)}, f32[1000]{0:T(1024)}, u32[]{:S(2)}) copy-start(f32[1000]{0:T(1024)} %param.52) | copy-start | bytes 12004
  758.2 44.5 %copy-start.25 = (f32[3,4,192]{2,1,0:T(4,128)}, f32[3,4,192]{2,1,0:T(4,128)S(1)}, u32[]{:S(2)}) copy-start(f32[3,4,192]{2,1,0:T(4,128)S(1)} %add_multiply_fusion.2) | copy-start | bytes 27652
  765.5 23.1 %copy-start.28 = (f32[4,3,768]{2,1,0:T(4,128)}, f32[4,3,768]{2,1,0:T(4,128)S(1)}, u32[]{:S(2)}) copy-start(f32[4,3,768]{2,1,0:T(4,128)S(1)} %reshape.609) | copy-start | bytes 110596
  (42 other events, 135.4 us)
Sparse Core Ops, SparseCore 0:
  420.3 136.5 all-reduce.11

commit v4 on v3

--- a/solution.py
+++ b/solution.py
@@ -298,7 +298,7 @@
             pltpu.SemaphoreType.DMA((count,)),
         ],
         compiler_params=pltpu.CompilerParams(
-            collective_id=collective_id, has_side_effects=True, vmem_limit_bytes=48 << 20
+            collective_id=collective_id, has_side_effects=True, vmem_limit_bytes=67043328
         ),
     )(*arrays)
 
@@ -628,18 +628,27 @@
     )
 
 
-def sum_layer(attn_part, mlp_part):
+def sum_layers(pairs):
     parts, depth = lax.axis_size("tensor"), lax.axis_size("dp")
-    rows, columns = attn_part.shape[1] // depth, attn_part.shape[2]
+    rows, columns = pairs[0][0].shape[1] // depth, pairs[0][0].shape[2]
+    sums = []
     if hand_made():
         form = (2,) * len(DIMS) + (ROW_HALVES, rows // ROW_HALVES, columns)
-        groups = tuple(
-            tuple((1, (at,), (half,), half) for half in range(ROW_HALVES)) for at in range(2)
-        ) + (tuple((0, (), (half,), half) for half in range(ROW_HALVES)),)
-        attn_sum, mlp_sum = collect(
-            [attn_part.reshape(form), mlp_part.reshape((2,) + form)], groups, 2
-        )
-    else:
+        arrays, groups = [], []
+        for attn_part, mlp_part in pairs:
+            position = len(arrays)
+            arrays += [attn_part.reshape(form), mlp_part.reshape((2,) + form)]
+            for at in range(2):
+                groups.append(
+                    tuple((position + 1, (at,), (half,), half) for half in range(ROW_HALVES))
+                )
+            groups.append(tuple((position, (), (half,), half) for half in range(ROW_HALVES)))
+        totals = collect(arrays, tuple(groups), 2)
+        for index in range(len(pairs)):
+            attn_sum, mlp_sum = totals[2 * index : 2 * index + 2]
+            sums.append((attn_sum.reshape(rows, columns), mlp_sum.reshape(2, rows, columns)))
+        return sums
+    for attn_part, mlp_part in pairs:
         whole = jnp.concatenate([attn_part[None], mlp_part]).reshape(
             LAYER_BLOCKS, parts, depth, rows, columns
         )
@@ -647,8 +656,8 @@
         total = lax.psum_scatter(
             whole, ("dp", "tensor"), scatter_dimension=0, tiled=False
         ).astype(jnp.float32)
-        attn_sum, mlp_sum = total[0], total[1:]
-    return attn_sum.reshape(rows, columns), mlp_sum.reshape(2, rows, columns)
+        sums.append((total[0], total[1:]))
+    return sums
 
 
 def sum_small(small):
@@ -844,6 +853,7 @@
     hidden_list = [None] * LAYERS
     attn_list = [None] * LAYERS
     mlp_list = [None] * LAYERS
+    layer_parts = []
     for layer_idx in reversed(range(LAYERS)):
         layer_input, mid, gains, qkv, mixed, act, slope = saved[layer_idx]
         grad_rows, attn_part, mlp_part, shared_list[layer_idx], split_part, hidden_part = (
@@ -855,8 +865,10 @@
         split_part = split_part.reshape(tensor_width, 3, attn_width)
         split_list[layer_idx] = jnp.stack([split_part[:, 0], split_part[:, 2]], axis=1)
         hidden_list[layer_idx] = hidden_part.reshape(tensor_width, mlp_width)
-        attn_sum, mlp_list[layer_idx] = sum_layer(attn_part, mlp_part)
+        layer_parts.append((attn_part, mlp_part))
+    for layer_idx, (attn_sum, mlp_sum) in zip(reversed(range(LAYERS)), sum_layers(layer_parts)):
         attn_list[layer_idx] = attn_sum.reshape(own_rows, 4, attn_width)
+        mlp_list[layer_idx] = mlp_sum
     grad_image = grad_rows.reshape(images, PAD_ROWS, D)
     grad_first = jnp.sum(grad_image[:, 0], axis=0)
     grad_position = jnp.sum(grad_image[:, 1:TOK_IMG], axis=0)

time: 831 us -> 753 us (0.906)
  Pallas kernels: 681 us -> 622 us
  local copies, waits for them, and re-layouts: 54.7 us -> 36.7 us
    pallas_call x4 -> x2, Pallas kernels: 277 us -> 219 us  [collect(): pl.pallas_call(partial(collect_kernel, groups, len(arrays)), out_shape=[j...]
    unnamed x185 -> x213, local copies, waits for them, and re-layouts: 16.3 us -> 7.8 us
  transfers between devices with their start and end apart: 1 -> 1, of which waited for: 0 -> 0; matrix products, arithmetic and copies ran while one was open for 5% -> 5% of each run, Pallas kernels for 36% -> 32%
where the time goes in v4:
time: 753 us; the launch traced here: 744 us
  Pallas kernels  622 us (83%)
  other arithmetic  53 us (7%)
  local copies, waits for them, and re-layouts  36.7 us (5%)
  between operations  22.2 us (3%)
  matrix products  9.4 us (1%)
    pallas_call x2, Pallas kernels, collect(): pl.pallas_call(partial(collect_kernel, groups, len(arrays)), out_shape=[j...  219 us
    pallas_call x1, Pallas kernels, spread(): pl.pallas_call(partial(spread_kernel, groups), out_shape=[jax.ShapeDtypeS...  186 us
    pallas_call x3, Pallas kernels, backward_layer(): pl.pallas_call(partial(backward_kernel, images, parts), grid=(2 * parts,)...  124 us
    pallas_call x3, Pallas kernels, forward_layer(): pl.pallas_call(partial(forward_kernel, images, parts), grid=(2 * parts,),...  63.1 us
    pallas_call x2, Pallas kernels, exchange(): pl.pallas_call(partial(exchange_kernel, routes), out_shape=[jax.ShapeDtyp...  30.4 us
  transfers between devices with their start and end apart: 1, of which 0 were waited for; matrix products, arithmetic and copies ran while one was open for 5% of the time, Pallas kernels for 32%

profile of v4, /device:TPU:0, one launch (start us, length us, event | category | flops | bytes accessed | tf_op | source)
XLA Modules:
  0.0 743.7 jit_solution(11348715519757573337)
XLA Ops:
  7.2 2.9 multiply_reduce_fusion.1
  10.2 1.1 multiply_reduce_fusion.6
  14.0 186.0 %shard_map.442 = (bf16[9,2,2,2,2,2,2,48,768]{8,7,6,5,4,3,2,1,0:T(8,128)(2,1)}, bf16[2,2,2,2,2,2,24,1024]{7,6,5,4,3,2,1,0:T(8,128)(2,1)S(1)}, f32[2,2,2,2,2,32,128]{6,5,4,3,2,1,0:T(8,128)S(1)}) custom-call(bf16[9,2,48,768]{3,2,1,0:T(8,128)(2,1)S(1)} %bitcast.194, bf16[2,24,1024]{2,1,0:T(8,128)(2,1)S(1)} %pad_maximum_fusion.4.refs_1_, ...), custom_call_target="tpu_custom_call" | custom-call | tf_op jit(solution)/shard_map/pallas_call | solution.py:161
  202.4 2.9 convolution_bitcast_fusion
  205.4 1.4 reshape.562
  207.9 20.6 %shard_map.443 = (f32[416,768]{1,0:T(8,128)S(1)}, f32[416,768]{1,0:T(8,128)S(1)}, bf16[4,416,576]{2,1,0:T(8,128)(2,1)}, bf16[4,416,192]{2,1,0:T(8,128)(2,1)S(1)}...) custom-call(f32[416,768]{1,0:T(8,128)S(1)} %bitcast.192, f32[6,768]{1,0:T(8,128)S(1)} %get-tuple-element.175.gain_ref, ...), custom_call_target="tpu_custom_call" | custom-call | tf_op jit(solution)/shard_map/pallas_call | solution.py:409
  228.6 21.4 %shard_map.444 = (f32[416,768]{1,0:T(8,128)S(1)}, f32[416,768]{1,0:T(8,128)S(1)}, bf16[4,416,576]{2,1,0:T(8,128)(2,1)}, bf16[4,416,192]{2,1,0:T(8,128)(2,1)S(1)}...) custom-call(f32[416,768]{1,0:T(8,128)S(1)} %get-tuple-element.75.x_ref, ...), custom_call_target="tpu_custom_call" | custom-call | tf_op jit(solution)/shard_map/pallas_call | solution.py:409
  250.9 21.1 %shard_map.445 = (f32[416,768]{1,0:T(8,128)S(1)}, f32[416,768]{1,0:T(8,128)S(1)}, bf16[4,416,576]{2,1,0:T(8,128)(2,1)}, bf16[4,416,192]{2,1,0:T(8,128)(2,1)S(1)}...) custom-call(f32[416,768]{1,0:T(8,128)S(1)} %get-tuple-element.76.x_ref, ...), custom_call_target="tpu_custom_call" | custom-call | tf_op jit(solution)/shard_map/pallas_call | solution.py:409
  272.1 1.1 copy-done.5
  276.3 1.9 fusion.76
  279.2 2.1 multiply_reduce_fusion.23
  281.6 1.1 concatenate.49.clone
  282.7 41.6 %shard_map.446 = (f32[416,768]{1,0:T(8,128)}, bf16[4,768,768]{2,1,0:T(8,128)(2,1)}, bf16[2,4,768,768]{3,2,1,0:T(8,128)(2,1)}, f32[6,768]{1,0:T(8,128)}, f32[4,1,576]{2,1,0:T(1,128)}, /*index=5*/f32[4,1,768]{2,1,0:T(1,128)}) custom-call(f32[416,768]{1,0:T(8,128)} %bitcast.239, f32[416,768]{1,0:T(8,128)} %copy-done.2, f32[416,768]{1,0:T(8,128)} %copy-done.5, ...), custom_call_target="tpu_custom_call" | custom-call | tf_op jit(solution)/shard_map/pallas_call | solution.py:541
  325.1 41.4 %shard_map.447 = (f32[416,768]{1,0:T(8,128)}, bf16[4,768,768]{2,1,0:T(8,128)(2,1)}, bf16[2,4,768,768]{3,2,1,0:T(8,128)(2,1)}, f32[6,768]{1,0:T(8,128)}, f32[4,1,576]{2,1,0:T(1,128)}, /*index=5*/f32[4,1,768]{2,1,0:T(1,128)}) custom-call(f32[416,768]{1,0:T(8,128)} %get-tuple-element.83.grad_ref, f32[416,768]{1,0:T(8,128)} %copy-done.1, f32[416,768]{1,0:T(8,128)} %copy-done.4, ...), custom_call_target="tpu_custom_call" | custom-call | tf_op jit(solution)/shard_map/pallas_call | solution.py:541
  366.6 41.3 %shard_map.448 = (f32[416,768]{1,0:T(8,128)}, bf16[4,768,768]{2,1,0:T(8,128)(2,1)}, bf16[2,4,768,768]{3,2,1,0:T(8,128)(2,1)}, f32[6,768]{1,0:T(8,128)}, f32[4,1,576]{2,1,0:T(1,128)}, /*index=5*/f32[4,1,768]{2,1,0:T(1,128)}) custom-call(f32[416,768]{1,0:T(8,128)} %get-tuple-element.89.grad_ref, f32[416,768]{1,0:T(8,128)} %bitcast.193, f32[416,768]{1,0:T(8,128)} %copy-done.3, ...), custom_call_target="tpu_custom_call" | custom-call | tf_op jit(solution)/shard_map/pallas_call | solution.py:541
  411.0 1.3 multiply_reduce_fusion.28
  412.2 1.4 concatenate.51
  414.7 1.8 fusion
  417.6 2.5 pad_maximum_fusion.2
  420.1 1.7 copy.110
  422.2 2.1 copy_bitcast_fusion.refs_0_
  424.3 38.6 %shard_map.449 = f32[2,24,1024]{2,1,0:T(8,128)} custom-call(bf16[2,2,2,2,2,2,24,1024]{7,6,5,4,3,2,1,0:T(8,128)(2,1)} %copy_bitcast_fusion.refs_0_), custom_call_target="tpu_custom_call" | custom-call | tf_op jit(solution)/shard_map/pallas_call | solution.py:278
  463.0 1.6 fusion.8
  464.6 1.4 fusion.13
  466.0 1.6 fusion.6
  467.6 179.9 %shard_map.450 = (f32[2,48,768]{2,1,0:T(8,128)}, f32[2,2,48,768]{3,2,1,0:T(8,128)}, f32[2,48,768]{2,1,0:T(8,128)}, f32[2,2,48,768]{3,2,1,0:T(8,128)}, f32[2,48,768]{2,1,0:T(8,128)}, /*index=5*/f32[2,2,48,768]{3,2,1,0:T(8,128)}) custom-call(bf16[2,2,2,2,2,2,48,768]{7,6,5,4,3,2,1,0:T(8,128)(2,1)} %bitcast.240, ...), custom_call_target="tpu_custom_call" | custom-call | tf_op jit(solution)/shard_map/pallas_call | solution.py:278
  647.6 1.3 stack_reshape_reshape.9
  649.2 1.0 stack_reshape_reshape.11
  650.7 1.1 constant_dynamic-update-slice_fusion
  654.7 4.0 concatenate.54
  659.1 16.4 %shard_map.451 = (f32[16,128]{1,0:T(8,128)S(1)}, f32[16,128]{1,0:T(8,128)S(1)}, f32[56,128]{1,0:T(8,128)S(1)}) custom-call(f32[16,128]{1,0:T(8,128)S(1)} %pad_bitcast_fusion.1.refs_0_, f32[16,128]{1,0:T(8,128)S(1)} %fusion.21.refs_1_, f32[56,128]{1,0:T(8,128)S(1)} %fusion.12.refs_2_), custom_call_target="tpu_custom_call" | custom-call | tf_op jit(solution)/shard_map/pallas_call | solution.py:711
  685.7 1.3 multiply_reduce_fusion.14
  687.0 1.4 multiply_reduce_fusion.10
  688.4 1.3 multiply_reduce_fusion.16
  692.8 2.0 concatenate.57
  694.9 14.0 %shard_map.452 = f32[8,128]{1,0:T(8,128)S(1)} custom-call(f32[8,128]{1,0:T(8,128)S(1)} %pad_bitcast_fusion.2.refs_0_), custom_call_target="tpu_custom_call" | custom-call | tf_op jit(solution)/shard_map/pallas_call | solution.py:711
  711.9 1.4 fusion.35
  716.9 1.0 multiply_reduce_fusion.12
  718.5 1.9 multiply_reduce_fusion.26
  721.2 3.1 divide_subtract_fusion.1
  724.5 1.7 divide_subtract_fusion
  726.2 1.4 divide_subtract_fusion.4
  727.6 1.3 divide_subtract_fusion.5
  728.9 1.4 divide_subtract_fusion.2
  730.3 1.4 divide_subtract_fusion.7
  731.7 1.4 divide_subtract_fusion.6
  733.8 1.3 slice.324
  735.1 1.3 divide_subtract_fusion.8
  (373 shorter events, 37.3 us)
Async XLA Ops:
  7.2 682.5 %all-reduce.12.cloned.1.call-start = ((), (), s32[]{:S(2)}) async-start(), calls=%async_computation | async-start | bytes 245760 | tf_op jit(solution)/shard_map/psum | solution.py:65
  202.2 26.4 %copy-start.10 = (f32[6,768]{1,0:T(8,128)}, f32[6,768]{1,0:T(8,128)S(1)}, u32[]{:S(2)}) copy-start(f32[6,768]{1,0:T(8,128)S(1)} %get-tuple-element.174.gain_ref) | copy-start | bytes 55300
  202.2 48.7 %copy-start.11 = (f32[6,768]{1,0:T(8,128)}, f32[6,768]{1,0:T(8,128)S(1)}, u32[]{:S(2)}) copy-start(f32[6,768]{1,0:T(8,128)S(1)} %get-tuple-element.173.gain_ref) | copy-start | bytes 55300
  207.9 20.6 %copy-start = (f32[2,208,768]{2,1,0:T(8,128)}, f32[2,208,768]{2,1,0:T(8,128)S(1)}, u32[]{:S(2)}) copy-start(f32[2,208,768]{2,1,0:T(8,128)S(1)} %maximum_maximum_fusion) | copy-start | bytes 3833860
  228.6 21.4 %copy-start.1 = (f32[416,768]{1,0:T(8,128)}, f32[416,768]{1,0:T(8,128)S(1)}, u32[]{:S(2)}) copy-start(f32[416,768]{1,0:T(8,128)S(1)} %get-tuple-element.75.x_ref) | copy-start | bytes 3833860
  228.6 21.4 %copy-start.3 = (f32[416,768]{1,0:T(8,128)}, f32[416,768]{1,0:T(8,128)S(1)}, u32[]{:S(2)}) copy-start(f32[416,768]{1,0:T(8,128)S(1)} %get-tuple-element.90.mid_ref) | copy-start | bytes 3833860
  228.6 21.4 %copy-start.6 = (bf16[4,416,192]{2,1,0:T(8,128)(2,1)}, bf16[4,416,192]{2,1,0:T(8,128)(2,1)S(1)}, u32[]{:S(2)}) copy-start(bf16[4,416,192]{2,1,0:T(8,128)(2,1)S(1)} %get-tuple-element.92.mixed_ref) | copy-start | bytes 1916932
  250.9 21.2 %copy-start.2 = (f32[416,768]{1,0:T(8,128)}, f32[416,768]{1,0:T(8,128)S(1)}, u32[]{:S(2)}) copy-start(f32[416,768]{1,0:T(8,128)S(1)} %get-tuple-element.76.x_ref) | copy-start | bytes 3833860
  250.9 21.2 %copy-start.4 = (f32[416,768]{1,0:T(8,128)}, f32[416,768]{1,0:T(8,128)S(1)}, u32[]{:S(2)}) copy-start(f32[416,768]{1,0:T(8,128)S(1)} %get-tuple-element.84.mid_ref) | copy-start | bytes 3833860
  250.9 23.5 %copy-start.102 = (s32[8]{0:T(128)S(1)}, s32[8]{0:T(128)}, u32[]{:S(2)}) copy-start(s32[8]{0:T(128)} %param.29) | copy-start | bytes 100
  250.9 25.4 %copy-start.61 = (f32[1000]{0:T(1024)S(1)}, f32[1000]{0:T(1024)}, u32[]{:S(2)}) copy-start(f32[1000]{0:T(1024)} %param.51) | copy-start | bytes 12004
  366.5 42.3 %copy-start.71 = (f32[4,1,576]{2,1,0:T(1,128)S(1)}, f32[4,1,576]{2,1,0:T(1,128)}, u32[]{:S(2)}) copy-start(f32[4,1,576]{2,1,0:T(1,128)} %get-tuple-element.96) | copy-start | bytes 27652
  366.5 42.7 %copy-start.69 = (f32[4,1,768]{2,1,0:T(1,128)S(1)}, f32[4,1,768]{2,1,0:T(1,128)}, u32[]{:S(2)}) copy-start(f32[4,1,768]{2,1,0:T(1,128)} %get-tuple-element.100) | copy-start | bytes 36868
  366.5 42.6 %copy-start.70 = (f32[4,1,768]{2,1,0:T(1,128)S(1)}, f32[4,1,768]{2,1,0:T(1,128)}, u32[]{:S(2)}) copy-start(f32[4,1,768]{2,1,0:T(1,128)} %get-tuple-element.99) | copy-start | bytes 36868
  366.5 43.4 %copy-start.51 = (f32[6,768]{1,0:T(8,128)S(1)}, f32[6,768]{1,0:T(8,128)}, u32[]{:S(2)}) copy-start(f32[6,768]{1,0:T(8,128)} %get-tuple-element.103) | copy-start | bytes 55300
  366.6 43.4 %copy-start.52 = (f32[6,768]{1,0:T(8,128)S(1)}, f32[6,768]{1,0:T(8,128)}, u32[]{:S(2)}) copy-start(f32[6,768]{1,0:T(8,128)} %get-tuple-element.102) | copy-start | bytes 55300
  407.9 6.4 copy-start.19
  652.0 23.7 %copy-start.41 = (f32[3,2,192]{2,1,0:T(2,128)S(1)}, f32[3,2,192]{2,1,0:T(2,128)}, u32[]{:S(2)}) copy-start(f32[3,2,192]{2,1,0:T(2,128)} %param.45) | copy-start | bytes 13828
  652.0 23.8 %copy-start.35 = (f32[3,768]{1,0:T(4,128)S(1)}, f32[3,768]{1,0:T(4,128)}, u32[]{:S(2)}) copy-start(f32[3,768]{1,0:T(4,128)} %param.47) | copy-start | bytes 27652
  652.0 24.5 %copy-start.21 = (f32[20,768]{1,0:T(8,128)S(1)}, f32[20,768]{1,0:T(8,128)}, u32[]{:S(2)}) copy-start(f32[20,768]{1,0:T(8,128)} %param.49) | copy-start | bytes 184324
  652.0 24.6 %copy-start.62 = (f32[1000]{0:T(1024)S(1)}, f32[1000]{0:T(1024)}, u32[]{:S(2)}) copy-start(f32[1000]{0:T(1024)} %param.51) | copy-start | bytes 12004
  652.7 25.0 %copy-start.66 = (f32[3,4,192]{2,1,0:T(4,128)S(1)}, f32[3,4,192]{2,1,0:T(4,128)}, u32[]{:S(2)}) copy-start(f32[3,4,192]{2,1,0:T(4,128)} %param.32) | copy-start | bytes 27652
  653.2 25.6 %copy-start.59 = (f32[3,2,768]{2,1,0:T(2,128)S(1)}, f32[3,2,768]{2,1,0:T(2,128)}, u32[]{:S(2)}) copy-start(f32[3,2,768]{2,1,0:T(2,128)} %param.35) | copy-start | bytes 55300
  654.1 31.6 %copy-start.81 = (f32[24]{0:T(128)}, f32[24]{0:T(128)S(1)}, u32[]{:S(2)}) copy-start(f32[24]{0:T(128)S(1)} %get-tuple-element.156) | copy-start | bytes 292
  654.7 32.3 %copy-start.83 = (f32[24]{0:T(128)}, f32[24]{0:T(128)S(1)}, u32[]{:S(2)}) copy-start(f32[24]{0:T(128)S(1)} %get-tuple-element.152) | copy-start | bytes 292
  654.7 33.7 %copy-start.85 = (f32[24]{0:T(128)}, f32[24]{0:T(128)S(1)}, u32[]{:S(2)}) copy-start(f32[24]{0:T(128)S(1)} %get-tuple-element.211) | copy-start | bytes 292
  677.7 43.4 %copy-start.33 = (f32[3,4,192]{2,1,0:T(4,128)}, f32[3,4,192]{2,1,0:T(4,128)S(1)}, u32[]{:S(2)}) copy-start(f32[3,4,192]{2,1,0:T(4,128)S(1)} %add_multiply_fusion.2) | copy-start | bytes 27652
  677.7 8.0 %copy-start.18 = (f32[2,24,1024]{2,1,0:T(8,128)S(1)}, f32[2,24,1024]{2,1,0:T(8,128)}, u32[]{:S(2)}) copy-start(f32[2,24,1024]{2,1,0:T(8,128)} %shard_map.449) | copy-start | bytes 589828
  677.7 12.8 %copy-start.80 = (f32[3,2,192]{2,1,0:T(2,128)S(1)}, f32[3,2,192]{2,1,0:T(2,128)}, u32[]{:S(2)}) copy-start(f32[3,2,192]{2,1,0:T(2,128)} %param.46) | copy-start | bytes 13828
  678.5 13.5 %copy-start.67 = (f32[3,768]{1,0:T(4,128)S(1)}, f32[3,768]{1,0:T(4,128)}, u32[]{:S(2)}) copy-start(f32[3,768]{1,0:T(4,128)} %param.48) | copy-start | bytes 27652
  678.7 12.6 %copy-start.57 = (f32[3,2]{1,0:T(4,128)}, f32[3,2]{1,0:T(4,128)S(1)}, u32[]{:S(2)}) copy-start(f32[3,2]{1,0:T(4,128)S(1)} %div.309) | copy-start | bytes 76
  678.8 10.9 %copy-start.48 = (f32[3,2,96]{2,1,0:T(2,128)}, f32[3,2,96]{2,1,0:T(2,128)S(1)}, u32[]{:S(2)}) copy-start(f32[3,2,96]{2,1,0:T(2,128)S(1)} %add_multiply_fusion.5) | copy-start | bytes 6916
  679.5 41.6 %copy-start.56 = (f32[3,4]{1,0:T(4,128)S(1)}, f32[3,4]{1,0:T(4,128)}, u32[]{:S(2)}) copy-start(f32[3,4]{1,0:T(4,128)} %copy-done.55) | copy-start | bytes 148
  680.8 45.4 %copy-start.45 = (f32[768]{0:T(1024)}, f32[768]{0:T(1024)S(1)}, u32[]{:S(2)}) copy-start(f32[768]{0:T(1024)S(1)} %fusion.29) | copy-start | bytes 9220
  680.9 8.8 %copy-start.72 = (f32[198]{0:T(256)}, f32[198]{0:T(256)S(1)}, u32[]{:S(2)}) copy-start(f32[198]{0:T(256)S(1)} %fusion.46) | copy-start | bytes 2380
  681.0 8.7 %copy-start.46 = (f32[1000]{0:T(1024)}, f32[1000]{0:T(1024)S(1)}, u32[]{:S(2)}) copy-start(f32[1000]{0:T(1024)S(1)} %fusion.27) | copy-start | bytes 12004
  717.9 15.2 %copy-start.28 = (f32[20,768]{1,0:T(8,128)}, f32[20,768]{1,0:T(8,128)S(1)}, u32[]{:S(2)}) copy-start(f32[20,768]{1,0:T(8,128)S(1)} %get-tuple-element.146) | copy-start | bytes 184324
  724.4 5.9 copy-start.42
  724.4 5.9 copy-start.53
  724.4 5.9 copy-start.77
  724.4 7.3 copy-start.36
  724.4 7.3 copy-start.44
  724.4 7.2 copy-start.91
  724.5 7.2 copy-start.92
  724.5 8.6 %copy-start.97 = (f32[20]{0:T(128)S(1)}, f32[20]{0:T(128)}, u32[]{:S(2)}) copy-start(f32[20]{0:T(128)} %sqrt_maximum_fusion) | copy-start | bytes 244
  724.5 8.6 %copy-start.98 = (f32[20]{0:T(128)S(1)}, f32[20]{0:T(128)}, u32[]{:S(2)}) copy-start(f32[20]{0:T(128)} %multiply_maximum_fusion) | copy-start | bytes 244
  724.5 10.6 %copy-start.60 = (f32[1000]{0:T(1024)S(1)}, f32[1000]{0:T(1024)}, u32[]{:S(2)}) copy-start(f32[1000]{0:T(1024)} %get-tuple-element.144) | copy-start | bytes 12004
  724.5 10.6 %copy-start.63 = (f32[1000]{0:T(1024)S(1)}, f32[1000]{0:T(1024)}, u32[]{:S(2)}) copy-start(f32[1000]{0:T(1024)} %param.51) | copy-start | bytes 12004
  (56 other events, 145.1 us)
Sparse Core Ops, SparseCore 0:
  413.7 131.4 all-reduce.11
